TPU v7x, 256 devices: a whole 4x4x8 slice. The times are simulated.
256 devices in a mesh: section: 16 (over y, z_hi, core), rep: 4 (over z_lo), sub: 4 (over x).
Axes of the slice: x: 4, y: 4, z: 8 (z_hi: 2, z_lo: 4; z = z_hi * 4 + z_lo), core: 2. Of those that a mesh axis runs over, the one named last changes fastest.
Arguments:
- token_ids: int32 [8, 512], P(None, ('rep', 'sub')), may hold values from 0 to 255
- target_ids: int32 [8, 512], P(None, ('rep', 'sub')), may hold values from 0 to 255
- embedding: bfloat16 [256, 2048], P(('rep', 'sub')), may hold values from -3 to 3
- section_weight: bfloat16 [16, 2048, 2048], P('section', ('rep', 'sub')), may hold values from -0.125 to 0.125
- section_gain: float32 [16, 2048], P('section'), may hold values from 0.1 to 1.9
- final_gain: float32 [2048], replicated, may hold values from 0.5 to 1.5
Outputs:
- weight_grad: float32 [16, 2048, 2048], P('section', ('rep', 'sub'))
- gain_grad: float32 [16, 2048], P('section')
- embed_grad: float32 [256, 2048], P(('section', 'rep', 'sub'))
- final_grad: float32 [2048], replicated
All inputs are finite; a program needn't handle non-finite values.
Results may differ from a plain program's by a relative error of at most 0.024.
Values may be sent and summed in bfloat16 or wider, within the bound.
No kernel may reach another device: no remote copies, remote signals or barrier semaphores. Data moves between devices by JAX's collectives and lax.ppermute only.
A program may use at most 64 MiB of HBM per device.

v0:
```python
import functools

import jax
import jax.numpy as jnp
from jax import lax
from jax.experimental import pallas as pl
from jax.experimental.pallas import tpu as pltpu
from jax.sharding import Mesh, PartitionSpec as P


epsilon = 1e-06
gelu_coef = 0.7978845608028654
cube_coef = 0.044715
BF = jnp.bfloat16
F32 = jnp.float32
CONTRACT_LAST = (((1,), (1,)), ((), ()))
SLOTS = 4
CHUNKS = 4
COLS = 2


def gelu(pre_act):
    return (
        0.5
        * pre_act
        * (1.0 + jnp.tanh(gelu_coef * (pre_act + cube_coef * pre_act * pre_act * pre_act)))
    )


def gelu_slope(pre_act):
    inside = gelu_coef * (pre_act + cube_coef * pre_act * pre_act * pre_act)
    tangent = jnp.tanh(inside)
    return 0.5 * (1.0 + tangent) + 0.5 * pre_act * (1.0 - tangent * tangent) * gelu_coef * (
        1.0 + 3.0 * cube_coef * pre_act * pre_act
    )


def unit_of(residual):
    values = residual.astype(F32)
    scale_inv = lax.rsqrt(jnp.mean(values * values, axis=-1, keepdims=True) + epsilon)
    return values * scale_inv, scale_inv


def start_chunk(pos, pieces, layer, part, buf, sem, by_rows):
    half = layer // 2
    count = len(pieces) // 2

    def run(refs):
        top, column, left, right, far = refs
        nx, cut = top.shape[1], top.shape[2]
        zs = column.shape[0] // 2
        low = column.shape[1]
        ix = pos[1]
        size = column.shape[2] // CHUNKS

        def copy(ref, base, x):
            if by_rows:
                source = ref.at[base + part]
                target = buf.at[x, pl.ds(cut, low), :]
            else:
                source = ref.at[pl.ds(base, zs), :, pl.ds(part * size, size)]
                target = buf.at[:, x, pl.ds(cut, low), :]
            pltpu.make_async_copy(source, target, sem).start()

        if by_rows:
            source, target = top.at[half * zs + part], buf.at[:, pl.ds(0, cut), :]
        else:
            source = top.at[pl.ds(half * zs, zs), :, :, pl.ds(part * size, size)]
            target = buf.at[:, :, pl.ds(0, cut), :]
        pltpu.make_async_copy(source, target, sem).start()
        copy(column, half * zs, ix)
        copy(left, half * zs, lax.rem(ix + nx - 1, nx))
        copy(right, half * zs, lax.rem(ix + 1, nx))

        copy(far, half * zs, lax.rem(ix + 2, nx))

    @pl.when(pos[0] == layer % 2)
    def _():
        run(pieces[:count])

    @pl.when(pos[0] != layer % 2)
    def _():
        run(pieces[count:])


def wait_chunk(buf, sem):
    pltpu.make_async_copy(buf, buf, sem).wait()


def forward_kernel(pos, x_ref, gain_ref, *refs):
    count = len(refs) - 6
    pieces = refs[:count]
    xs_ref, ns_ref, as_ref, out_ref, wbuf, sems = refs[count:]
    layers = gain_ref.shape[0]
    nx, block, size = wbuf.shape[2:]
    for part in range(CHUNKS):
        start_chunk(pos, pieces, 0, part, wbuf.at[part], sems.at[part], False)
    out_ref[...] = x_ref[...]

    def layer_step(layer, carry):
        residual = out_ref[...]
        xs_ref[layer] = residual
        unit, _ = unit_of(residual)
        rounded = (unit * gain_ref[pl.ds(layer, 1), :]).astype(BF)
        for b in range(rounded.shape[1] // block):
            ns_ref[b % nx, layer, :, b // nx * block : (b // nx + 1) * block] = rounded[:, b * block : (b + 1) * block]
        for part in range(CHUNKS):
            cols = slice(part * size, (part + 1) * size)
            wait_chunk(wbuf.at[part], sems.at[part])
            pre_act = jnp.dot(rounded, wbuf[part].reshape(-1, size), preferred_element_type=F32)
            as_ref[layer, :, cols] = pre_act
            out_ref[:, cols] = (residual[:, cols].astype(F32) + gelu(pre_act)).astype(BF)

            @pl.when(layer + 1 < layers)
            def _():
                start_chunk(pos, pieces, layer + 1, part, wbuf.at[part], sems.at[part], False)

        return carry

    lax.fori_loop(0, layers, layer_step, 0)


def backward_kernel(pos, grad_ref, gain_ref, xs_ref, as_ref, *refs, first):
    count = len(refs) - 6
    pieces = refs[:count]
    da_ref, gp_ref, out_ref, wbuf, dn_ref, sems = refs[count:]
    layers = xs_ref.shape[0]
    features = wbuf.shape[3]
    size = features // CHUNKS
    for part in range(CHUNKS):
        start_chunk(pos, pieces, first + layers - 1, part, wbuf.at[part], sems.at[part], True)
    out_ref[...] = grad_ref[...]

    def layer_step(step, carry):
        local = layers - 1 - step
        layer = first + local
        grad = out_ref[...].astype(F32)
        grad_pre = (grad * gelu_slope(as_ref[local])).astype(BF)
        da_ref[local] = grad_pre
        for part in range(CHUNKS):
            cols = slice(part * size, (part + 1) * size)
            wait_chunk(wbuf.at[part], sems.at[part])
            dn_ref[:, cols] = lax.dot_general(
                grad_pre, wbuf[part].reshape(size, features), CONTRACT_LAST, preferred_element_type=F32
            )

            @pl.when(step + 1 < layers)
            def _():
                start_chunk(pos, pieces, layer - 1, part, wbuf.at[part], sems.at[part], True)

        unit, scale_inv = unit_of(xs_ref[local])
        grad_norm = dn_ref[...]
        gp_ref[pl.ds(local, 1), :] = jnp.sum(grad_norm * unit, axis=0, keepdims=True)
        grad_unit = grad_norm * gain_ref[pl.ds(layer, 1), :]
        grad_in = scale_inv * (grad_unit - unit * jnp.mean(grad_unit * unit, axis=-1, keepdims=True))
        out_ref[...] = (grad + grad_in).astype(BF)
        return carry

    lax.fori_loop(0, layers, layer_step, 0)


def product_kernel(n_ref, *refs):
    halves = n_ref.shape[0]
    das, tail_ref, out_ref = refs[: 2 * halves], refs[2 * halves], refs[2 * halves + 1]
    per_half = out_ref.shape[0] // halves
    shard = out_ref.shape[1] - tail_ref.shape[1]
    wide = out_ref.shape[2]
    for h in range(halves):
        rows = jnp.concatenate([das[2 * h][...].reshape(-1, wide), das[2 * h + 1][...].reshape(-1, wide)])
        for b in range(per_half):
            out_ref[h * per_half + b, :shard, :] = jnp.dot(
                n_ref[h, b * shard : (b + 1) * shard, :], rows, preferred_element_type=F32
            ).astype(BF)
    out_ref[:, shard:, :] = tail_ref[...]


def head_kernel(x_ref, table_ref, target_ref, gain_ref, q_ref, f_ref, fp_ref, out_ref):
    features = x_ref.shape[1]
    logit_scale = float(features) ** (-0.5)
    unit, scale_inv = unit_of(x_ref[...])
    gain = gain_ref[...]
    rows = (unit * gain).astype(BF)
    f_ref[...] = rows
    logits = lax.dot_general(rows, table_ref[...], CONTRACT_LAST, preferred_element_type=F32) * logit_scale
    exp_logit = jnp.exp(logits)
    probability = exp_logit / jnp.sum(exp_logit, axis=-1, keepdims=True)
    vocab = lax.broadcasted_iota(jnp.int32, logits.shape, 1)
    onehot = (target_ref[...] == vocab).astype(F32)
    grad_logit = ((probability - onehot) * logit_scale).astype(BF)
    q_ref[...] = grad_logit
    grad_norm = jnp.dot(grad_logit, table_ref[...], preferred_element_type=F32)
    fp_ref[...] = jnp.sum(grad_norm * unit, axis=0, keepdims=True)
    grad_unit = grad_norm * gain
    grad_in = scale_inv * (grad_unit - unit * jnp.mean(grad_unit * unit, axis=-1, keepdims=True))
    out_ref[...] = grad_in.astype(BF)


VM = pl.BlockSpec(memory_space=pltpu.VMEM)
SM = pl.BlockSpec(memory_space=pltpu.SMEM)
HB = pl.BlockSpec(memory_space=pl.ANY)


def shape(dims, kind):
    return jax.ShapeDtypeStruct(dims, kind)


def forward_stage(core, x, gains, stores, nx):
    layers, (rows, features) = gains.shape[0], x.shape
    nz, blocks_x, _, _ = stores[0].shape
    rows_in = features // (nz // 2 * blocks_x)
    return pl.pallas_call(
        forward_kernel,
        in_specs=[SM, VM, VM] + [HB] * len(stores),
        out_specs=[VM] * 4,
        out_shape=[
            shape((layers, rows, features), BF),
            shape((nx, layers, rows, features // nx), BF),
            shape((layers, rows, features), F32),
            shape((rows, features), BF),
        ],
        scratch_shapes=[
            pltpu.VMEM((SLOTS, nz // 2, blocks_x, rows_in, features // CHUNKS), BF),
            pltpu.SemaphoreType.DMA((SLOTS,)),
        ],
        name="forward_stage",
    )(core, x, gains, *stores)


def backward_stage(core, grad, gains, xs, pres, stores, first, layers):
    rows, features = grad.shape
    nz, blocks_x, _, _ = stores[0].shape
    rows_in = features // (nz // 2 * blocks_x)

    def part_of():
        return pl.BlockSpec((layers, rows, features), lambda i: (first // layers, 0, 0), memory_space=pltpu.VMEM)

    return pl.pallas_call(
        functools.partial(backward_kernel, first=first),
        grid=(1,),
        in_specs=[SM, VM, VM, part_of(), part_of()] + [HB] * len(stores),
        out_specs=[VM] * 3,
        out_shape=[
            shape((layers, rows, features), BF),
            shape((layers, features), F32),
            shape((rows, features), BF),
        ],
        scratch_shapes=[
            pltpu.VMEM((SLOTS, blocks_x, rows_in, features), BF),
            pltpu.VMEM((rows, features), F32),
            pltpu.SemaphoreType.DMA((SLOTS,)),
        ],
        name="backward_stage",
    )(core, grad, gains, xs, pres, *stores)


def product_stage(n_rows, das, tails, chunk):
    halves, _, _ = n_rows.shape
    blocks, extra, features = tails.shape
    wide = features // COLS
    shard = n_rows.shape[1] * halves // blocks
    return pl.pallas_call(
        product_kernel,
        grid=(1,),
        in_specs=[VM]
        + [pl.BlockSpec(das[0].shape[:2] + (wide,), lambda i: (0, 0, chunk), memory_space=pltpu.VMEM)] * (2 * halves)
        + [pl.BlockSpec((blocks, extra, wide), lambda i: (0, 0, chunk), memory_space=pltpu.VMEM)],
        out_specs=VM,
        out_shape=shape((blocks, shard + extra, wide), BF),
        name="product_stage",
    )(n_rows, *das, tails)


def head_stage(x, table, targets, gain):
    rows, features = x.shape
    return pl.pallas_call(
        head_kernel,
        in_specs=[VM] * 4,
        out_specs=[VM] * 4,
        out_shape=[
            shape((rows, table.shape[0]), BF),
            shape((rows, features), BF),
            shape((1, features), F32),
            shape((rows, features), BF),
        ],
        name="head_stage",
    )(x, table, targets, gain)


def turn(value, axis, steps):
    count = lax.axis_size(axis)
    return lax.ppermute(value, axis, [(i, (i + steps) % count) for i in range(count)])


def shift(value, axis, steps):
    count = lax.axis_size(axis)
    return lax.ppermute(value, axis, [(i, i + steps) for i in range(count) if 0 <= i + steps < count])


def pick(value, index, axis):
    return lax.dynamic_index_in_dim(value, index, axis, keepdims=False)


def in_order(own, partner, place):
    return jnp.where(place == 0, jnp.stack([own, partner]), jnp.stack([partner, own]))


def ring_spread(value, axes, ups):
    count = lax.axis_size(axes)
    out = [(0, value)]
    moving = value
    for step in range(1, ups + 1):
        moving = turn(moving, axes, 1)
        out.append((step, moving))
    moving = value
    for step in range(1, count - ups):
        moving = turn(moving, axes, -1)
        out.append((-step, moving))
    return out


def gather_weights(own_rows, small):
    nzh, nzl, nx = (lax.axis_size(a) for a in ("zh", "zl", "x"))
    iz, ix = lax.axis_index(("zh", "zl")), lax.axis_index("x")
    nz = nzh * nzl
    rows, features = own_rows.shape
    cut = rows * 3 // 8
    a = own_rows[:cut]
    a_left, a_right = turn(a, "x", 1), turn(a, "x", -1)
    a_half = cut // 3
    a_far = jnp.concatenate([turn(a_left[:a_half], "x", 1), turn(a_right[a_half:], "x", -1)])
    line = jnp.zeros((nx, cut, features), BF)
    for steps, piece in ((0, a), (1, a_left), (-1, a_right), (2, a_far)):
        line = lax.dynamic_update_slice(line, piece[None], ((ix - steps) % nx, 0, 0))
    column = jnp.zeros((nz, rows - cut, features), BF)
    for steps, piece in ring_spread(own_rows[cut:], ("zh", "zl"), nz // 2 - 1):
        column = lax.dynamic_update_slice(column, piece[None], ((iz - steps) % nz, 0, 0))
    line, column, small = lax.optimization_barrier((line, column, small))
    top = jnp.zeros((nz, nx, cut, features), BF)
    for steps, piece in ring_spread(line, ("zh", "zl"), nz // 2):
        top = lax.dynamic_update_slice(top, piece[None], ((iz - steps) % nz, 0, 0, 0))
    left, right = turn(column, "x", 1), turn(column, "x", -1)
    far = jnp.concatenate([turn(left[: nz // 2], "x", 1), turn(right[nz // 2 :], "x", -1)])
    own = [top, column, left, right, far]
    return own + [turn(piece, "c", 1) for piece in own], small


def body(token_ids, target_ids, embedding, section_weight, section_gain, final_gain):
    ny, nzh, nc, nzl, nx = (lax.axis_size(a) for a in ("y", "zh", "c", "zl", "x"))
    iy, izh, ic, izl, ix = (lax.axis_index(a) for a in ("y", "zh", "c", "zl", "x"))
    features = embedding.shape[1]
    part_rows = embedding.shape[0]
    vocab_rows = part_rows * nzl * nx
    layers = nzh * nc
    shard = section_weight.shape[1]
    tokens = token_ids.size // layers
    core = jnp.stack([ic, ix])

    gain_pair = in_order(section_gain[0], turn(section_gain[0], "c", 1), ic)
    gains = in_order(gain_pair, turn(gain_pair, "zh", 1), izh).reshape(layers, features)

    ring = embedding[None]
    for axis, count in (("x", nx), ("zl", nzl)):
        reach = 1
        while reach < count:
            ring = jnp.concatenate([ring, turn(ring, axis, reach)])
            reach *= 2
    stores, (gains, ring) = gather_weights(section_weight[0], (gains, ring))
    from_zl = (izl - jnp.arange(nzl)) % nzl
    from_x = (ix - jnp.arange(nx)) % nx
    owner = from_zl[:, None] * nx + from_x[None, :]
    row_ids = (owner[:, :, None] * part_rows + jnp.arange(part_rows)).reshape(-1)
    vocab_iota = jnp.arange(vocab_rows, dtype=jnp.int32)
    select = (vocab_iota[:, None] == row_ids[None, :]).astype(BF)
    table = jnp.dot(select, ring.reshape(vocab_rows, features), preferred_element_type=F32).astype(BF)

    share = izh * nc + ic
    token_own = pick(token_ids.reshape(layers, tokens), share, 0)
    target_own = pick(target_ids.reshape(layers, tokens), share, 0)
    onehot_in = (token_own[:, None] == vocab_iota[None, :]).astype(BF)
    x = jnp.dot(onehot_in, table, preferred_element_type=F32).astype(BF)

    saved = (
        jnp.zeros((layers, tokens, features), BF),
        jnp.zeros((nx, layers, tokens, features // nx), BF),
        jnp.zeros((layers, tokens, features), F32),
        x,
    )
    for stage in range(ny):
        x_in = x if stage == 0 else shift(saved[3], "y", 1)
        saved = lax.cond(
            iy == stage,
            lambda x_in, saved: tuple(forward_stage(core, x_in, gains, stores, nx)),
            lambda x_in, saved: saved,
            x_in,
            saved,
        )
    xs, ns, pres, x_top = saved

    q, f, final_part, grad = lax.cond(
        iy == ny - 1,
        lambda x_top: tuple(head_stage(x_top, table, target_own[:, None], final_gain[None, :])),
        lambda x_top: (
            jnp.zeros((tokens, vocab_rows), BF),
            jnp.zeros((tokens, features), BF),
            jnp.zeros((1, features), F32),
            jnp.zeros((tokens, features), BF),
        ),
        x_top,
    )

    pair = layers // nzh

    def backward(stage, grad_in, kept, first, count):
        return lax.cond(
            iy == stage,
            lambda grad_in, kept: tuple(backward_stage(core, grad_in, gains, xs, pres, stores, first, count)),
            lambda grad_in, kept: kept,
            grad_in,
            kept,
        )

    back = (jnp.zeros((layers, tokens, features), BF), jnp.zeros((layers, features), F32), grad)
    left = jnp.where(iy == 0, onehot_in, q)
    for stage in range(ny - 1, 0, -1):
        grad_in = grad if stage == ny - 1 else shift(back[-1], "y", -1)
        back = backward(stage, grad_in, back, 0, layers)
        if stage == ny - 1:
            back, ns, left = lax.optimization_barrier((back, ns, left))

    n4 = ns.reshape(nx, nzh, nc, tokens, features // nx)
    n_swap = turn(pick(n4, 1 - ic, 2), "c", 1)
    n2 = jnp.stack([pick(n4, ic, 2), n_swap], axis=2)
    left2 = jnp.concatenate([left, turn(left, "c", 1)])

    def columns(to_x):
        return pick(n2, to_x, 0)

    n_parts = [columns(ix)] + [turn(columns((ix + k) % nx), "x", k) for k in (1, -1, 2)]
    n_rows = jnp.transpose(jnp.stack(n_parts, axis=2), (0, 4, 1, 2, 3)).reshape(nzh, nzl * shard, nc * nx * tokens)
    l_rows = pick(left2.reshape(nc * tokens, ny, nzh, nc, nzl, nx), ic, 3)
    l_rows = jnp.transpose(l_rows, (4, 2, 3, 1, 0)).reshape(-1, nc * tokens)

    grad_in = shift(back[-1], "y", -1)
    grad_in, n_rows, l_rows = lax.optimization_barrier((grad_in, n_rows, l_rows))
    last, grad_low = [None] * nzh, grad_in
    for h in range(nzh - 1, -1, -1):
        kept = tuple(b[h * pair : (h + 1) * pair] for b in back[:-1]) + (grad_low,)
        last[h] = backward(0, grad_low, kept, h * pair, pair)
        grad_low = last[h][-1]

    def exchanged(da):
        near = (da, turn(da, "x", 1), turn(da, "x", -1))
        far = jnp.concatenate([turn(near[1][:1], "x", 1), turn(near[2][1:], "x", -1)])
        pieces = jnp.stack(near + (far,))
        return pick(pieces, ic, 1), turn(pick(pieces, 1 - ic, 1), "c", 1)

    das = [None] * nzh
    for h in range(nzh - 1, -1, -1):
        das[h] = exchanged(last[h][0])

    right = jnp.where(iy == 0, grad_low, f)
    gp4 = jnp.stack([last[h][1] for h in range(nzh)])
    misc_rows = 16

    def misc(which):
        return jnp.concatenate(
            [pick(gp4, which, 1), final_part, jnp.zeros((misc_rows - nzh - 1, features), F32)]
        ).astype(BF)

    swapped = turn(jnp.concatenate([right, misc(1 - ic)]), "c", 1)
    right2 = jnp.concatenate([right, swapped[:tokens]])
    rows_all = jnp.dot(l_rows, right2, preferred_element_type=F32).astype(BF).reshape(nx, -1, features)
    misc2 = (misc(ic).astype(F32) + swapped[tokens:].astype(F32)).astype(BF)

    def rows_for(to_x):
        return jnp.concatenate([pick(rows_all, to_x, 0), misc2])

    rows_sum = rows_for(ix).astype(F32)
    for k in (1, -1, 2):
        rows_sum = rows_sum + turn(rows_for((ix + k) % nx), "x", k).astype(F32)
    rows_sum = rows_sum.astype(BF)
    rows_z = rows_sum[: nzh * nzl * ny].reshape(nzh, nzl, ny, features)
    misc_sum = rows_sum[nzh * nzl * ny :]
    gain_rows = jnp.broadcast_to(misc_sum[:nzh].reshape(nzh, 1, 1, features), (nzh, nzl, 1, features))
    final_rows = jnp.broadcast_to(misc_sum[nzh], (nzh, nzl, 1, features))
    extra = 16
    empty = jnp.zeros((nzh, nzl, extra - ny - 2, features), BF)
    tails = jnp.concatenate([rows_z, gain_rows, final_rows, empty], axis=2).reshape(nzh * nzl, extra, features)

    z_axes = ("zh", "zl")
    nz = nzh * nzl
    iz = izh * nzl + izl

    def scattered(blocks, up_steps):
        def block(offset):
            return pick(blocks, (iz + offset) % nz, 0)

        total = block(0).astype(F32)
        for sign, count in ((1, up_steps), (-1, nz - 1 - up_steps)):
            moving = block(sign * count)
            for offset in range(count - 1, 0, -1):
                arrived = turn(moving, z_axes, sign)
                moving = (arrived.astype(F32) + block(sign * offset).astype(F32)).astype(BF)
            total = total + turn(moving, z_axes, sign).astype(F32)
        return total

    chunks = []
    for k in range(COLS):
        flat = [v for pieces in das for v in pieces]
        chunks.append(scattered(product_stage(n_rows, flat, tails, k), nz // 2 - k % 2))
    total = jnp.concatenate(chunks, axis=1)

    weight_grad = total[:shard]
    gain_grad = total[shard + ny : shard + ny + 1]
    rows_y = total[shard : shard + ny]
    final_plane = total[shard + ny + 1 : shard + ny + 2]

    def to_plane(which):
        return jnp.concatenate([pick(rows_y, which, 0)[None], final_plane])

    y_sum = to_plane(iy)
    for k in range(1, ny):
        y_sum = y_sum + turn(to_plane((iy + k) % ny), "y", k)
    return (weight_grad[None], gain_grad, y_sum[:1], y_sum[1])


def solution(mesh):
    names = ("y", "zh", "c", "zl", "x")
    inner = Mesh(mesh.devices.reshape(4, 2, 2, 4, 4), names)
    section = ("y", "zh", "c")
    group = ("zl", "x")
    in_specs = (
        P(None, group),
        P(None, group),
        P(group, None),
        P(section, group, None),
        P(section, None),
        P(),
    )
    out_specs = (
        P(section, group, None),
        P(section, None),
        P(section + group, None),
        P(),
    )
    return jax.shard_map(body, mesh=inner, in_specs=in_specs, out_specs=out_specs, check_vma=False)
```

profile of v0, /device:TPU:102, one launch (start us, length us, event | category | flops | bytes accessed | tf_op | source)
XLA Modules:
  0.0 541.4 jit_solution(1026935765361004188)
XLA Ops:
  44.9 6.9 %collective-permute-done.5 = bf16[80,2048]{1,0:T(8,128)(2,1)S(1)} collective-permute-done((bf16[80,2048]{1,0:T(8,128)(2,1)}, bf16[80,2048]{1,0:T(8,128)(2,1)S(1)}, u32[]{:S(2)}, u32[]{:S(2)}) %collective-permute-start.5) | collective-permute-done | bytes 327712 | tf_op jit(solution)/shard_map/ppermute | solution.py:291
  51.9 11.1 %collective-permute-start.9 = (bf16[80,2048]{1,0:T(8,128)(2,1)S(1)}, bf16[80,2048]{1,0:T(8,128)(2,1)S(1)}, u32[]{:S(2)}, u32[]{:S(2)}) collective-permute-start(bf16[80,2048]{1,0:T(8,128)(2,1)S(1)} %collective-permute-done.8), channel_id=1, source_target_pairs={{0,44},{4,0},{8,4},{12,8},{32,12},{36,32},{40,36},{44,40},{1,45},{... | collective-permute-start | bytes 983048 | tf_op jit(solution)/shard_map/ppermute | solution.py:291
  63.1 6.5 %collective-permute-done.9 = bf16[80,2048]{1,0:T(8,128)(2,1)S(1)} collective-permute-done((bf16[80,2048]{1,0:T(8,128)(2,1)S(1)}, bf16[80,2048]{1,0:T(8,128)(2,1)S(1)}, u32[]{:S(2)}, u32[]{:S(2)}) %collective-permute-start.9) | collective-permute-done | bytes 327712 | tf_op jit(solution)/shard_map/ppermute | solution.py:291
  69.6 7.9 %collective-permute-start.10 = (bf16[80,2048]{1,0:T(8,128)(2,1)S(1)}, bf16[80,2048]{1,0:T(8,128)(2,1)S(1)}, u32[]{:S(2)}, u32[]{:S(2)}) collective-permute-start(bf16[80,2048]{1,0:T(8,128)(2,1)S(1)} %collective-permute-done.9), channel_id=1, source_target_pairs={{0,44},{4,0},{8,4},{12,8},{32,12},{36,32},{40,36},{44,40},{1,45},{... | collective-permute-start | bytes 983048 | tf_op jit(solution)/shard_map/ppermute | solution.py:291
  83.6 6.0 %collective-permute-start.17 = (bf16[4,48,2048]{2,1,0:T(8,128)(2,1)S(1)}, bf16[4,48,2048]{2,1,0:T(8,128)(2,1)}, u32[]{:S(2)}, u32[]{:S(2)}) collective-permute-start(bf16[4,48,2048]{2,1,0:T(8,128)(2,1)S(1)} %fusion.25), channel_id=1, source_target_pairs={{0,4},{4,8},{8,12},{12,32},{32,36},{36,40},{40,44},{44,0},{1,5},{5... | collective-permute-start | bytes 2359304 | tf_op jit(solution)/shard_map/ppermute | solution.py:291
  89.6 15.9 %collective-permute-done.17 = bf16[4,48,2048]{2,1,0:T(8,128)(2,1)} collective-permute-done((bf16[4,48,2048]{2,1,0:T(8,128)(2,1)S(1)}, bf16[4,48,2048]{2,1,0:T(8,128)(2,1)}, u32[]{:S(2)}, u32[]{:S(2)}) %collective-permute-start.17) | collective-permute-done | bytes 786464 | tf_op jit(solution)/shard_map/ppermute | solution.py:291
  112.5 16.1 %collective-permute-done.18 = bf16[4,48,2048]{2,1,0:T(8,128)(2,1)} collective-permute-done((bf16[4,48,2048]{2,1,0:T(8,128)(2,1)}, bf16[4,48,2048]{2,1,0:T(8,128)(2,1)}, u32[]{:S(2)}, u32[]{:S(2)}) %collective-permute-start.18) | collective-permute-done | bytes 786464 | tf_op jit(solution)/shard_map/ppermute | solution.py:291
  138.9 10.6 %collective-permute-done.19 = bf16[4,48,2048]{2,1,0:T(8,128)(2,1)S(1)} collective-permute-done((bf16[4,48,2048]{2,1,0:T(8,128)(2,1)}, bf16[4,48,2048]{2,1,0:T(8,128)(2,1)S(1)}, u32[]{:S(2)}, u32[]{:S(2)}) %collective-permute-start.19) | collective-permute-done | bytes 786464 | tf_op jit(solution)/shard_map/ppermute | solution.py:291
  156.2 6.4 %collective-permute-done.20 = bf16[4,48,2048]{2,1,0:T(8,128)(2,1)S(1)} collective-permute-done((bf16[4,48,2048]{2,1,0:T(8,128)(2,1)S(1)}, bf16[4,48,2048]{2,1,0:T(8,128)(2,1)S(1)}, u32[]{:S(2)}, u32[]{:S(2)}) %collective-permute-start.20) | collective-permute-done | bytes 786464 | tf_op jit(solution)/shard_map/ppermute | solution.py:291
  173.2 27.1 %collective-permute-done.26 = bf16[4,80,2048]{2,1,0:T(8,128)(2,1)S(1)} collective-permute-done((bf16[4,80,2048]{2,1,0:T(8,128)(2,1)S(1)}, bf16[4,80,2048]{2,1,0:T(8,128)(2,1)S(1)}, u32[]{:S(2)}, u32[]{:S(2)}) %collective-permute-start.26) | collective-permute-done | bytes 1310752 | tf_op jit(solution)/shard_map/ppermute | solution.py:291
  209.5 14.9 %conditional.10 = ((bf16[4,64,2048]{2,1,0:T(8,128)(2,1)}, bf16[4,4,64,512]{3,2,1,0:T(8,128)(2,1)}, f32[4,64,2048]{2,1,0:T(8,128)}, bf16[64,2048]{1,0:T(8,128)(2,1)S(1)})) conditional(s32[]{:T(128)} %convert_element_type.207, bf16[64,2048]{1,0:T(8,128)(2,1)S(1)} %convolution_convert_fusion.2, (s32[2]{0:T(128)S(1)}, bf16[64,2048]{1,0:T(8,128)(2,1)S(1)}, ...), branch_computations={%region_0.1_spmd, %region_1.2_spmd} | conditional | bytes 4194352 | solution.py:390
  210.2 14.2 %forward_stage.4 = (bf16[4,64,2048]{2,1,0:T(8,128)(2,1)}, bf16[4,4,64,512]{3,2,1,0:T(8,128)(2,1)}, f32[4,64,2048]{2,1,0:T(8,128)}, bf16[64,2048]{1,0:T(8,128)(2,1)S(1)}) custom-call(s32[2]{0:T(128)S(1)} %get-tuple-element.425.pos, bf16[64,2048]{1,0:T(8,128)(2,1)} %copy.141.x_ref, f32[4,2048]{1,0:T(4,128)S(1)} %get-tuple-element.427.gain_ref, ...), custom_call_target="tpu_custom_call" | custom-call | tf_op jit(solution)/shard_map/cond/branch_1_fun/forward_stage/pallas_call | solution.py:211
  225.8 6.3 %collective-permute-done.33 = bf16[64,2048]{1,0:T(8,128)(2,1)S(1)} collective-permute-done((bf16[64,2048]{1,0:T(8,128)(2,1)S(1)}, bf16[64,2048]{1,0:T(8,128)(2,1)S(1)}, u32[]{:S(2)}, u32[]{:S(2)}) %collective-permute-start.33) | collective-permute-done | bytes 262176 | tf_op jit(solution)/shard_map/ppermute | solution.py:296
  232.1 18.2 %collective-permute-start.34 = (bf16[64,2048]{1,0:T(8,128)(2,1)S(1)}, bf16[64,2048]{1,0:T(8,128)(2,1)S(1)}, u32[]{:S(2)}, u32[]{:S(2)}) collective-permute-start(bf16[64,2048]{1,0:T(8,128)(2,1)S(1)} %get-tuple-element.621), channel_id=1, source_target_pairs={{0,64},{64,128},{128,192},{1,65},{65,129},{129,193},{2,66},{66,130... | collective-permute-start | bytes 786440 | tf_op jit(solution)/shard_map/ppermute | solution.py:296
  266.5 9.9 %conditional.15 = ((bf16[4,64,2048]{2,1,0:T(8,128)(2,1)}, f32[4,2048]{1,0:T(4,128)}, bf16[64,2048]{1,0:T(8,128)(2,1)})) conditional(s32[]{:T(128)} %convert_element_type.206, bf16[64,2048]{1,0:T(8,128)(2,1)S(1)} %get-tuple-element.624, (s32[2]{0:T(128)S(1)}, bf16[64,2048]{1,0:T(8,128)(2,1)S(1)}, f32[4,2048]{1,0:T(4,128)S(1)}, ...), branch_computations={%region_10.11_spmd, %region_11.12_spmd} | conditional | bytes 1605670 | solution.py:414
  279.9 22.4 %collective-permute-done.36 = bf16[64,2048]{1,0:T(8,128)(2,1)S(1)} collective-permute-done((bf16[64,2048]{1,0:T(8,128)(2,1)}, bf16[64,2048]{1,0:T(8,128)(2,1)S(1)}, u32[]{:S(2)}, u32[]{:S(2)}) %collective-permute-start.36) | collective-permute-done | bytes 262176 | tf_op jit(solution)/shard_map/ppermute | solution.py:296
  315.8 6.3 %collective-permute-done.41 = bf16[2,2,64,512]{3,2,1,0:T(8,128)(2,1)} collective-permute-done((bf16[2,2,64,512]{3,2,1,0:T(8,128)(2,1)}, bf16[2,2,64,512]{3,2,1,0:T(8,128)(2,1)}, u32[]{:S(2)}, u32[]{:S(2)}) %collective-permute-start.41) | collective-permute-done | bytes 262176 | tf_op jit(solution)/shard_map/ppermute | solution.py:291
  324.3 63.1 %collective-permute-done.38 = bf16[64,2048]{1,0:T(8,128)(2,1)S(1)} collective-permute-done((bf16[64,2048]{1,0:T(8,128)(2,1)}, bf16[64,2048]{1,0:T(8,128)(2,1)S(1)}, u32[]{:S(2)}, u32[]{:S(2)}) %collective-permute-start.38) | collective-permute-done | bytes 262176 | tf_op jit(solution)/shard_map/ppermute | solution.py:296
  387.4 13.3 %conditional.18 = (bf16[2,64,2048]{2,1,0:T(8,128)(2,1)}, bf16[64,2048]{1,0:T(8,128)(2,1)S(1)}, bf16[1,2,64,2048]{3,2,1,0:T(8,128)(2,1)S(1)}, f32[1,2,2048]{2,1,0:T(2,128)S(1)}) conditional(s32[]{:T(128)} %convert_element_type.207, (bf16[4,64,2048]{2,1,0:T(8,128)(2,1)S(1)}, f32[4,2048]{1,0:T(4,128)S(1)}, ...), branch_computations={%region_16.17_spmd, %region_17.18_spmd} | conditional | bytes 2129952 | solution.py:414
  388.1 11.1 %backward_stage.12 = (bf16[2,64,2048]{2,1,0:T(8,128)(2,1)}, f32[2,2048]{1,0:T(2,128)S(1)}, bf16[64,2048]{1,0:T(8,128)(2,1)S(1)}) custom-call(s32[2]{0:T(128)S(1)} %get-tuple-element.533.pos, bf16[64,2048]{1,0:T(8,128)(2,1)} %copy.142.grad_ref, f32[4,2048]{1,0:T(4,128)S(1)} %get-tuple-element.535.gain_ref, bf16[4,64,2048]{2,1,0:T(8,128)(2,1)} %get-tuple-element.536.xs_ref, ...), custom_call_target="tpu_custom_call" | custom-call | tf_op jit(solution)/shard_map/cond/branch_1_fun/backward_stage/pallas_call | solution.py:237
  400.7 12.9 %conditional.19 = (bf16[2,64,2048]{2,1,0:T(8,128)(2,1)}, bf16[64,2048]{1,0:T(8,128)(2,1)S(1)}, bf16[1,2,64,2048]{3,2,1,0:T(8,128)(2,1)S(1)}, f32[1,2,2048]{2,1,0:T(2,128)S(1)}) conditional(s32[]{:T(128)} %convert_element_type.207, (bf16[4,64,2048]{2,1,0:T(8,128)(2,1)}, f32[4,2048]{1,0:T(4,128)S(1)}, bf16[64,2048]{1,0:T(8,128)(2,1)S(1)}) %tuple.209, ...), branch_computations={%region_18.19_spmd, %region_19.20_spmd} | conditional | bytes 2129952 | solution.py:414
  401.4 11.1 %backward_stage.13 = (bf16[2,64,2048]{2,1,0:T(8,128)(2,1)}, f32[2,2048]{1,0:T(2,128)S(1)}, bf16[64,2048]{1,0:T(8,128)(2,1)S(1)}) custom-call(s32[2]{0:T(128)S(1)} %get-tuple-element.554.pos, bf16[64,2048]{1,0:T(8,128)(2,1)} %copy.143.grad_ref, f32[4,2048]{1,0:T(4,128)S(1)} %get-tuple-element.556.gain_ref, bf16[4,64,2048]{2,1,0:T(8,128)(2,1)} %get-tuple-element.557.xs_ref, ...), custom_call_target="tpu_custom_call" | custom-call | tf_op jit(solution)/shard_map/cond/branch_1_fun/backward_stage/pallas_call | solution.py:237
  419.8 9.9 %collective-permute-done.49 = bf16[2,64,2048]{2,1,0:T(8,128)(2,1)S(1)} collective-permute-done((bf16[2,64,2048]{2,1,0:T(8,128)(2,1)}, bf16[2,64,2048]{2,1,0:T(8,128)(2,1)S(1)}, u32[]{:S(2)}, u32[]{:S(2)}) %collective-permute-start.49) | collective-permute-done | bytes 524320 | tf_op jit(solution)/shard_map/ppermute | solution.py:291
  451.2 8.9 %collective-permute-done.46 = bf16[1,64,2048]{2,1,0:T(8,128)(2,1)S(1)} collective-permute-done((bf16[1,64,2048]{2,1,0:T(8,128)(2,1)S(1)}, bf16[1,64,2048]{2,1,0:T(8,128)(2,1)S(1)}, u32[]{:S(2)}, u32[]{:S(2)}) %collective-permute-start.46) | collective-permute-done | bytes 262176 | tf_op jit(solution)/shard_map/ppermute | solution.py:291
  (302 shorter events, 246.5 us)
Async XLA Ops:
  2.5 38.2 %collective-permute-start.4 = (bf16[80,2048]{1,0:T(8,128)(2,1)}, bf16[80,2048]{1,0:T(8,128)(2,1)}, u32[]{:S(2)}, u32[]{:S(2)}) collective-permute-start(bf16[80,2048]{1,0:T(8,128)(2,1)} %get-tuple-element.694), channel_id=1, source_target_pairs={{0,4},{4,8},{8,12},{12,32},{32,36},{36,40},{40,44},{44,0},{1,5},{5... | collective-permute-start | bytes 983048 | tf_op jit(solution)/shard_map/ppermute | solution.py:291
  5.6 36.5 %collective-permute-start.7 = (bf16[80,2048]{1,0:T(8,128)(2,1)}, bf16[80,2048]{1,0:T(8,128)(2,1)}, u32[]{:S(2)}, u32[]{:S(2)}) collective-permute-start(bf16[80,2048]{1,0:T(8,128)(2,1)} %get-tuple-element.694), channel_id=1, source_target_pairs={{0,44},{4,0},{8,4},{12,8},{32,12},{36,32},{40,36},{44,40},{1,45},{... | collective-permute-start | bytes 983048 | tf_op jit(solution)/shard_map/ppermute | solution.py:291
  7.3 28.2 %collective-permute-start = (bf16[48,2048]{1,0:T(8,128)(2,1)}, bf16[48,2048]{1,0:T(8,128)(2,1)}, u32[]{:S(2)}, u32[]{:S(2)}) collective-permute-start(bf16[48,2048]{1,0:T(8,128)(2,1)} %get-tuple-element.696), channel_id=1, source_target_pairs={{0,1},{1,2},{2,3},{3,0},{4,5},{5,6},{6,7},{7,4},{8,9},{9,10},{10,1... | collective-permute-start | bytes 589832 | tf_op jit(solution)/shard_map/ppermute | solution.py:291
  7.8 25.8 %collective-permute-start.1 = (bf16[48,2048]{1,0:T(8,128)(2,1)}, bf16[48,2048]{1,0:T(8,128)(2,1)}, u32[]{:S(2)}, u32[]{:S(2)}) collective-permute-start(bf16[48,2048]{1,0:T(8,128)(2,1)} %get-tuple-element.696), channel_id=1, source_target_pairs={{0,3},{1,0},{2,1},{3,2},{4,7},{5,4},{6,5},{7,6},{8,11},{9,8},{10,9... | collective-permute-start | bytes 589832 | tf_op jit(solution)/shard_map/ppermute | solution.py:291
  44.8 33.9 %collective-permute-start.16 = (bf16[8,16,2048]{2,1,0:T(8,128)(2,1)S(1)}, bf16[8,16,2048]{2,1,0:T(8,128)(2,1)S(1)}, u32[]{:S(2)}, u32[]{:S(2)}) collective-permute-start(bf16[8,16,2048]{2,1,0:T(8,128)(2,1)S(1)} %pad_maximum_fusion.2), channel_id=1, source_target_pairs={{0,8},{4,12},{8,0},{12,4},{1,9},{5,13},{9,1},{13,5},{2,10},{6,14},... | collective-permute-start | bytes 1572872 | tf_op jit(solution)/shard_map/ppermute | solution.py:291
  51.8 25.7 %collective-permute-start.6 = (bf16[80,2048]{1,0:T(8,128)(2,1)S(1)}, bf16[80,2048]{1,0:T(8,128)(2,1)S(1)}, u32[]{:S(2)}, u32[]{:S(2)}) collective-permute-start(bf16[80,2048]{1,0:T(8,128)(2,1)S(1)} %collective-permute-done.5), channel_id=1, source_target_pairs={{0,4},{4,8},{8,12},{12,32},{32,36},{36,40},{40,44},{44,0},{1,5},{5... | collective-permute-start | bytes 983048 | tf_op jit(solution)/shard_map/ppermute | solution.py:291
  105.4 23.2 %collective-permute-start.18 = (bf16[4,48,2048]{2,1,0:T(8,128)(2,1)}, bf16[4,48,2048]{2,1,0:T(8,128)(2,1)}, u32[]{:S(2)}, u32[]{:S(2)}) collective-permute-start(bf16[4,48,2048]{2,1,0:T(8,128)(2,1)} %collective-permute-done.17), channel_id=1, source_target_pairs={{0,4},{4,8},{8,12},{12,32},{32,36},{36,40},{40,44},{44,0},{1,5},{5... | collective-permute-start | bytes 2359304 | tf_op jit(solution)/shard_map/ppermute | solution.py:291
  110.5 57.1 %collective-permute-start.24 = (bf16[8,80,2048]{2,1,0:T(8,128)(2,1)S(1)}, bf16[8,80,2048]{2,1,0:T(8,128)(2,1)}, u32[]{:S(2)}, u32[]{:S(2)}) collective-permute-start(bf16[8,80,2048]{2,1,0:T(8,128)(2,1)S(1)} %bitcast_dynamic-update-slice_fusion.8), channel_id=1, source_target_pairs={{0,1},{1,2},{2,3},{3,0},{4,5},{5,6},{6,7},{7,4},{8,9},{9,10},{10,1... | collective-permute-start | bytes 7864328 | tf_op jit(solution)/shard_map/ppermute | solution.py:291
  110.5 58.6 %collective-permute-start.25 = (bf16[8,80,2048]{2,1,0:T(8,128)(2,1)S(1)}, bf16[8,80,2048]{2,1,0:T(8,128)(2,1)}, u32[]{:S(2)}, u32[]{:S(2)}) collective-permute-start(bf16[8,80,2048]{2,1,0:T(8,128)(2,1)S(1)} %bitcast_dynamic-update-slice_fusion.8), channel_id=1, source_target_pairs={{0,3},{1,0},{2,1},{3,2},{4,7},{5,4},{6,5},{7,6},{8,11},{9,8},{10,9... | collective-permute-start | bytes 7864328 | tf_op jit(solution)/shard_map/ppermute | solution.py:291
  112.5 26.4 %collective-permute-start.22 = (bf16[4,48,2048]{2,1,0:T(8,128)(2,1)}, bf16[4,48,2048]{2,1,0:T(8,128)(2,1)S(1)}, u32[]{:S(2)}, u32[]{:S(2)}) collective-permute-start(bf16[4,48,2048]{2,1,0:T(8,128)(2,1)} %collective-permute-done.21), channel_id=1, source_target_pairs={{0,44},{4,0},{8,4},{12,8},{32,12},{36,32},{40,36},{44,40},{1,45},{... | collective-permute-start | bytes 2359304 | tf_op jit(solution)/shard_map/ppermute | solution.py:291
  138.9 27.7 %collective-permute-start.23 = (bf16[4,48,2048]{2,1,0:T(8,128)(2,1)S(1)}, bf16[4,48,2048]{2,1,0:T(8,128)(2,1)S(1)}, u32[]{:S(2)}, u32[]{:S(2)}) collective-permute-start(bf16[4,48,2048]{2,1,0:T(8,128)(2,1)S(1)} %collective-permute-done.22), channel_id=1, source_target_pairs={{0,44},{4,0},{8,4},{12,8},{32,12},{36,32},{40,36},{44,40},{1,45},{... | collective-permute-start | bytes 2359304 | tf_op jit(solution)/shard_map/ppermute | solution.py:291
  167.5 42.0 %collective-permute-start.28 = (bf16[8,4,48,2048]{3,2,1,0:T(8,128)(2,1)}, bf16[8,4,48,2048]{3,2,1,0:T(8,128)(2,1)}, u32[]{:S(2)}, u32[]{:S(2)}) collective-permute-start(bf16[8,4,48,2048]{3,2,1,0:T(8,128)(2,1)} %bitcast_dynamic-update-slice_fusion), channel_id=1, source_target_pairs={{0,16},{16,0},{1,17},{17,1},{2,18},{18,2},{3,19},{19,3},{4,20},{20... | collective-permute-start | bytes 18874376 | tf_op jit(solution)/shard_map/ppermute | solution.py:291
  169.0 31.3 %collective-permute-start.26 = (bf16[4,80,2048]{2,1,0:T(8,128)(2,1)S(1)}, bf16[4,80,2048]{2,1,0:T(8,128)(2,1)S(1)}, u32[]{:S(2)}, u32[]{:S(2)}) collective-permute-start(bf16[4,80,2048]{2,1,0:T(8,128)(2,1)S(1)} %slice.133), channel_id=1, source_target_pairs={{0,1},{1,2},{2,3},{3,0},{4,5},{5,6},{6,7},{7,4},{8,9},{9,10},{10,1... | collective-permute-start | bytes 3932168 | tf_op jit(solution)/shard_map/ppermute | solution.py:291
  170.6 32.5 %collective-permute-start.27 = (bf16[4,80,2048]{2,1,0:T(8,128)(2,1)S(1)}, bf16[4,80,2048]{2,1,0:T(8,128)(2,1)S(1)}, u32[]{:S(2)}, u32[]{:S(2)}) collective-permute-start(bf16[4,80,2048]{2,1,0:T(8,128)(2,1)S(1)} %slice.134), channel_id=1, source_target_pairs={{0,3},{1,0},{2,1},{3,2},{4,7},{5,4},{6,5},{7,6},{8,11},{9,8},{10,9... | collective-permute-start | bytes 3932168 | tf_op jit(solution)/shard_map/ppermute | solution.py:291
  172.7 34.1 %collective-permute-start.29 = (bf16[8,80,2048]{2,1,0:T(8,128)(2,1)S(1)}, bf16[8,80,2048]{2,1,0:T(8,128)(2,1)}, u32[]{:S(2)}, u32[]{:S(2)}) collective-permute-start(bf16[8,80,2048]{2,1,0:T(8,128)(2,1)S(1)} %bitcast_dynamic-update-slice_fusion.8), channel_id=1, source_target_pairs={{0,16},{16,0},{1,17},{17,1},{2,18},{18,2},{3,19},{19,3},{4,20},{20... | collective-permute-start | bytes 7864328 | tf_op jit(solution)/shard_map/ppermute | solution.py:291
  172.7 34.1 %collective-permute-start.30 = (bf16[8,80,2048]{2,1,0:T(8,128)(2,1)}, bf16[8,80,2048]{2,1,0:T(8,128)(2,1)}, u32[]{:S(2)}, u32[]{:S(2)}) collective-permute-start(bf16[8,80,2048]{2,1,0:T(8,128)(2,1)} %collective-permute-done.24), channel_id=1, source_target_pairs={{0,16},{16,0},{1,17},{17,1},{2,18},{18,2},{3,19},{19,3},{4,20},{20... | collective-permute-start | bytes 7864328 | tf_op jit(solution)/shard_map/ppermute | solution.py:291
  232.1 23.8 %collective-permute-start.34 = (bf16[64,2048]{1,0:T(8,128)(2,1)S(1)}, bf16[64,2048]{1,0:T(8,128)(2,1)S(1)}, u32[]{:S(2)}, u32[]{:S(2)}) collective-permute-start(bf16[64,2048]{1,0:T(8,128)(2,1)S(1)} %get-tuple-element.621), channel_id=1, source_target_pairs={{0,64},{64,128},{128,192},{1,65},{65,129},{129,193},{2,66},{66,130... | collective-permute-start | bytes 786440 | tf_op jit(solution)/shard_map/ppermute | solution.py:296
  278.6 25.0 %collective-permute-start.39 = (bf16[4,2,64,512]{3,2,1,0:T(8,128)(2,1)}, bf16[4,2,64,512]{3,2,1,0:T(8,128)(2,1)}, u32[]{:S(2)}, u32[]{:S(2)}) collective-permute-start(bf16[4,2,64,512]{3,2,1,0:T(8,128)(2,1)} %get-tuple-element.688), channel_id=1, source_target_pairs={{0,16},{16,0},{1,17},{17,1},{2,18},{18,2},{3,19},{19,3},{4,20},{20... | collective-permute-start | bytes 1572872 | tf_op jit(solution)/shard_map/ppermute | solution.py:291
  278.6 23.6 %collective-permute-start.36 = (bf16[64,2048]{1,0:T(8,128)(2,1)}, bf16[64,2048]{1,0:T(8,128)(2,1)S(1)}, u32[]{:S(2)}, u32[]{:S(2)}) collective-permute-start(bf16[64,2048]{1,0:T(8,128)(2,1)} %get-tuple-element.634), channel_id=1, source_target_pairs={{64,0},{128,64},{192,128},{65,1},{129,65},{193,129},{66,2},{130,66... | collective-permute-start | bytes 786440 | tf_op jit(solution)/shard_map/ppermute | solution.py:296
  313.3 74.0 %collective-permute-start.38 = (bf16[64,2048]{1,0:T(8,128)(2,1)}, bf16[64,2048]{1,0:T(8,128)(2,1)S(1)}, u32[]{:S(2)}, u32[]{:S(2)}) collective-permute-start(bf16[64,2048]{1,0:T(8,128)(2,1)} %get-tuple-element.638), channel_id=1, source_target_pairs={{64,0},{128,64},{192,128},{65,1},{129,65},{193,129},{66,2},{130,66... | collective-permute-start | bytes 786440 | tf_op jit(solution)/shard_map/ppermute | solution.py:296
  416.7 24.2 %collective-permute-start.44 = (bf16[2,64,2048]{2,1,0:T(8,128)(2,1)}, bf16[2,64,2048]{2,1,0:T(8,128)(2,1)S(1)}, u32[]{:S(2)}, u32[]{:S(2)}) collective-permute-start(bf16[2,64,2048]{2,1,0:T(8,128)(2,1)} %get-tuple-element.647), channel_id=1, source_target_pairs={{0,1},{1,2},{2,3},{3,0},{4,5},{5,6},{6,7},{7,4},{8,9},{9,10},{10,1... | collective-permute-start | bytes 1572872 | tf_op jit(solution)/shard_map/ppermute | solution.py:291
  419.3 24.2 %collective-permute-start.45 = (bf16[2,64,2048]{2,1,0:T(8,128)(2,1)}, bf16[2,64,2048]{2,1,0:T(8,128)(2,1)S(1)}, u32[]{:S(2)}, u32[]{:S(2)}) collective-permute-start(bf16[2,64,2048]{2,1,0:T(8,128)(2,1)} %get-tuple-element.647), channel_id=1, source_target_pairs={{0,3},{1,0},{2,1},{3,2},{4,7},{5,4},{6,5},{7,6},{8,11},{9,8},{10,9... | collective-permute-start | bytes 1572872 | tf_op jit(solution)/shard_map/ppermute | solution.py:291
  434.1 31.6 %collective-permute-start.55 = (bf16[48,2048]{1,0:T(8,128)(2,1)}, bf16[48,2048]{1,0:T(8,128)(2,1)}, u32[]{:S(2)}, u32[]{:S(2)}) collective-permute-start(bf16[48,2048]{1,0:T(8,128)(2,1)} %get-tuple-element.698), channel_id=1, source_target_pairs={{0,1},{1,2},{2,3},{3,0},{4,5},{5,6},{6,7},{7,4},{8,9},{9,10},{10,1... | collective-permute-start | bytes 589832 | tf_op jit(solution)/shard_map/ppermute | solution.py:291
  440.9 24.8 %collective-permute-start.56 = (bf16[48,2048]{1,0:T(8,128)(2,1)}, bf16[48,2048]{1,0:T(8,128)(2,1)}, u32[]{:S(2)}, u32[]{:S(2)}) collective-permute-start(bf16[48,2048]{1,0:T(8,128)(2,1)} %get-tuple-element.699), channel_id=1, source_target_pairs={{0,3},{1,0},{2,1},{3,2},{4,7},{5,4},{6,5},{7,6},{8,11},{9,8},{10,9... | collective-permute-start | bytes 589832 | tf_op jit(solution)/shard_map/ppermute | solution.py:291
  (70 other events, 871.9 us)
where the time goes:
time: 551 us; the launch traced here: 541 us
  waiting for transfers between devices  276 us (50%)
  starting transfers between devices  132 us (24%)
  local copies, waits for them, and re-layouts  54.4 us (10%)
  Pallas kernels  45.7 us (8%)
  other arithmetic  20.9 us (4%)
  loops' own time  7.92 us (1%)
    ppermute x69, waiting for transfers between devices, turn(): lax.ppermute(value, axis, [(i, (i + steps) % count) for i in range(count)])  170 us
    ppermute x6, waiting for transfers between devices, shift(): lax.ppermute(value, axis, [(i, i + steps) for i in range(count) if 0 <= i...  106 us
    ppermute x69, starting transfers between devices, turn(): lax.ppermute(value, axis, [(i, (i + steps) % count) for i in range(count)])  104 us
    ppermute x6, starting transfers between devices, shift(): lax.ppermute(value, axis, [(i, i + steps) for i in range(count) if 0 <= i...  27.9 us
    pallas_call x2, Pallas kernels, backward_stage(): pl.pallas_call(functools.partial(backward_kernel, first=first), grid=(1,)...  22.3 us
    pallas_call x1, Pallas kernels, forward_stage(): pl.pallas_call(forward_kernel, in_specs=[SM, VM, VM] + [HB] * len(stores)...  14.2 us
    dynamic_update_slice x8, local copies, waits for them, and re-layouts, gather_weights(): lax.dynamic_update_slice(top, piece[None], ((iz - steps) % nz, 0, 0, 0))  11.1 us
  transfers between devices with their start and end apart: 75, of which 43 were waited for; matrix products, arithmetic and copies ran while one was open for 11% of the time, Pallas kernels for 1%

commit v1 on v0

--- a/solution.py
+++ b/solution.py
@@ -14,25 +14,18 @@
 BF = jnp.bfloat16
 F32 = jnp.float32
 CONTRACT_LAST = (((1,), (1,)), ((), ()))
-SLOTS = 4
 CHUNKS = 4
+SLOTS = 2 * CHUNKS
 COLS = 2
-
-
-def gelu(pre_act):
-    return (
-        0.5
-        * pre_act
-        * (1.0 + jnp.tanh(gelu_coef * (pre_act + cube_coef * pre_act * pre_act * pre_act)))
-    )
-
-
-def gelu_slope(pre_act):
-    inside = gelu_coef * (pre_act + cube_coef * pre_act * pre_act * pre_act)
-    tangent = jnp.tanh(inside)
-    return 0.5 * (1.0 + tangent) + 0.5 * pre_act * (1.0 - tangent * tangent) * gelu_coef * (
+LANES = 128
+
+
+def gelu_and_slope(pre_act):
+    tangent = jnp.tanh(gelu_coef * (pre_act + cube_coef * pre_act * pre_act * pre_act))
+    slope = 0.5 * (1.0 + tangent) + 0.5 * pre_act * (1.0 - tangent * tangent) * gelu_coef * (
         1.0 + 3.0 * cube_coef * pre_act * pre_act
     )
+    return 0.5 * pre_act * (1.0 + tangent), slope
 
 
 def unit_of(residual):
@@ -41,38 +34,25 @@
     return values * scale_inv, scale_inv
 
 
-def start_chunk(pos, pieces, layer, part, buf, sem, by_rows):
+def start_layer(pos, pieces, layer, bank, wbuf, sems, by_rows):
     half = layer // 2
     count = len(pieces) // 2
 
     def run(refs):
-        top, column, left, right, far = refs
-        nx, cut = top.shape[1], top.shape[2]
-        zs = column.shape[0] // 2
-        low = column.shape[1]
-        ix = pos[1]
-        size = column.shape[2] // CHUNKS
-
-        def copy(ref, base, x):
-            if by_rows:
-                source = ref.at[base + part]
-                target = buf.at[x, pl.ds(cut, low), :]
-            else:
-                source = ref.at[pl.ds(base, zs), :, pl.ds(part * size, size)]
-                target = buf.at[:, x, pl.ds(cut, low), :]
-            pltpu.make_async_copy(source, target, sem).start()
-
-        if by_rows:
-            source, target = top.at[half * zs + part], buf.at[:, pl.ds(0, cut), :]
-        else:
-            source = top.at[pl.ds(half * zs, zs), :, :, pl.ds(part * size, size)]
-            target = buf.at[:, :, pl.ds(0, cut), :]
-        pltpu.make_async_copy(source, target, sem).start()
-        copy(column, half * zs, ix)
-        copy(left, half * zs, lax.rem(ix + nx - 1, nx))
-        copy(right, half * zs, lax.rem(ix + 1, nx))
-
-        copy(far, half * zs, lax.rem(ix + 2, nx))
+        for part in range(CHUNKS):
+            slot = bank * CHUNKS + part
+            top = 0
+            for ref in refs:
+                nz, _, rows, features = ref.shape
+                zs, size = nz // 2, features // CHUNKS
+                if by_rows:
+                    source = ref.at[half * zs + part]
+                    target = wbuf.at[slot, :, pl.ds(top, rows), :]
+                else:
+                    source = ref.at[pl.ds(half * zs, zs), :, :, pl.ds(part * size, size)]
+                    target = wbuf.at[slot, :, :, pl.ds(top, rows), :]
+                top += rows
+                pltpu.make_async_copy(source, target, sems.at[slot]).start()
 
     @pl.when(pos[0] == layer % 2)
     def _():
@@ -88,72 +68,79 @@
 
 
 def forward_kernel(pos, x_ref, gain_ref, *refs):
-    count = len(refs) - 6
+    count = len(refs) - 7
     pieces = refs[:count]
-    xs_ref, ns_ref, as_ref, out_ref, wbuf, sems = refs[count:]
+    xs_ref, ns_ref, slope_ref, scale_ref, out_ref, wbuf, sems = refs[count:]
     layers = gain_ref.shape[0]
     nx, block, size = wbuf.shape[2:]
-    for part in range(CHUNKS):
-        start_chunk(pos, pieces, 0, part, wbuf.at[part], sems.at[part], False)
+    start_layer(pos, pieces, 0, 0, wbuf, sems, False)
     out_ref[...] = x_ref[...]
 
     def layer_step(layer, carry):
+        bank = lax.rem(layer, 2)
+
+        @pl.when(layer + 1 < layers)
+        def _():
+            start_layer(pos, pieces, layer + 1, 1 - bank, wbuf, sems, False)
+
         residual = out_ref[...]
         xs_ref[layer] = residual
-        unit, _ = unit_of(residual)
+        unit, scale_inv = unit_of(residual)
+        scale_ref[layer] = jnp.broadcast_to(scale_inv, scale_ref.shape[1:])
         rounded = (unit * gain_ref[pl.ds(layer, 1), :]).astype(BF)
         for b in range(rounded.shape[1] // block):
             ns_ref[b % nx, layer, :, b // nx * block : (b // nx + 1) * block] = rounded[:, b * block : (b + 1) * block]
         for part in range(CHUNKS):
             cols = slice(part * size, (part + 1) * size)
-            wait_chunk(wbuf.at[part], sems.at[part])
-            pre_act = jnp.dot(rounded, wbuf[part].reshape(-1, size), preferred_element_type=F32)
-            as_ref[layer, :, cols] = pre_act
-            out_ref[:, cols] = (residual[:, cols].astype(F32) + gelu(pre_act)).astype(BF)
-
-            @pl.when(layer + 1 < layers)
-            def _():
-                start_chunk(pos, pieces, layer + 1, part, wbuf.at[part], sems.at[part], False)
-
+            slot = bank * CHUNKS + part
+            wait_chunk(wbuf.at[slot], sems.at[slot])
+            pre_act = jnp.dot(rounded, wbuf[slot].reshape(-1, size), preferred_element_type=F32)
+            value, slope = gelu_and_slope(pre_act)
+            slope_ref[layer, :, cols] = slope
+            out_ref[:, cols] = (residual[:, cols].astype(F32) + value).astype(BF)
         return carry
 
     lax.fori_loop(0, layers, layer_step, 0)
 
 
-def backward_kernel(pos, grad_ref, gain_ref, xs_ref, as_ref, *refs, first):
+def backward_kernel(pos, grad_ref, gain_ref, xs_ref, slope_ref, scale_ref, *refs, first):
     count = len(refs) - 6
     pieces = refs[:count]
     da_ref, gp_ref, out_ref, wbuf, dn_ref, sems = refs[count:]
     layers = xs_ref.shape[0]
     features = wbuf.shape[3]
     size = features // CHUNKS
-    for part in range(CHUNKS):
-        start_chunk(pos, pieces, first + layers - 1, part, wbuf.at[part], sems.at[part], True)
+    start_layer(pos, pieces, first + layers - 1, 0, wbuf, sems, True)
     out_ref[...] = grad_ref[...]
 
     def layer_step(step, carry):
         local = layers - 1 - step
         layer = first + local
-        grad = out_ref[...].astype(F32)
-        grad_pre = (grad * gelu_slope(as_ref[local])).astype(BF)
+        bank = lax.rem(step, 2)
+
+        @pl.when(step + 1 < layers)
+        def _():
+            start_layer(pos, pieces, layer - 1, 1 - bank, wbuf, sems, True)
+
+        grad_pre = (out_ref[...].astype(F32) * slope_ref[local]).astype(BF)
         da_ref[local] = grad_pre
+        scale_inv = scale_ref[local][:, :1]
+        products = jnp.zeros((grad_pre.shape[0], size), F32)
         for part in range(CHUNKS):
             cols = slice(part * size, (part + 1) * size)
-            wait_chunk(wbuf.at[part], sems.at[part])
-            dn_ref[:, cols] = lax.dot_general(
-                grad_pre, wbuf[part].reshape(size, features), CONTRACT_LAST, preferred_element_type=F32
+            slot = bank * CHUNKS + part
+            wait_chunk(wbuf.at[slot], sems.at[slot])
+            grad_norm = lax.dot_general(
+                grad_pre, wbuf[slot].reshape(size, features), CONTRACT_LAST, preferred_element_type=F32
             )
-
-            @pl.when(step + 1 < layers)
-            def _():
-                start_chunk(pos, pieces, layer - 1, part, wbuf.at[part], sems.at[part], True)
-
-        unit, scale_inv = unit_of(xs_ref[local])
-        grad_norm = dn_ref[...]
-        gp_ref[pl.ds(local, 1), :] = jnp.sum(grad_norm * unit, axis=0, keepdims=True)
-        grad_unit = grad_norm * gain_ref[pl.ds(layer, 1), :]
-        grad_in = scale_inv * (grad_unit - unit * jnp.mean(grad_unit * unit, axis=-1, keepdims=True))
-        out_ref[...] = (grad + grad_in).astype(BF)
+            grad_times = grad_norm * (xs_ref[local, :, cols].astype(F32) * scale_inv)
+            gp_ref[pl.ds(local, 1), cols] = jnp.sum(grad_times, axis=0, keepdims=True)
+            gain = gain_ref[pl.ds(layer, 1), cols]
+            products = products + grad_times * gain
+            dn_ref[:, cols] = grad_norm * gain
+        mean = jnp.sum(products, axis=-1, keepdims=True) / features
+        unit = xs_ref[local].astype(F32) * scale_inv
+        out_ref[...] = (out_ref[...].astype(F32) + scale_inv * (dn_ref[...] - unit * mean)).astype(BF)
         return carry
 
     lax.fori_loop(0, layers, layer_step, 0)
@@ -211,11 +198,12 @@
     return pl.pallas_call(
         forward_kernel,
         in_specs=[SM, VM, VM] + [HB] * len(stores),
-        out_specs=[VM] * 4,
+        out_specs=[VM] * 5,
         out_shape=[
             shape((layers, rows, features), BF),
             shape((nx, layers, rows, features // nx), BF),
             shape((layers, rows, features), F32),
+            shape((layers, rows, LANES), F32),
             shape((rows, features), BF),
         ],
         scratch_shapes=[
@@ -226,18 +214,18 @@
     )(core, x, gains, *stores)
 
 
-def backward_stage(core, grad, gains, xs, pres, stores, first, layers):
+def backward_stage(core, grad, gains, xs, slopes, scales, stores, first, layers):
     rows, features = grad.shape
     nz, blocks_x, _, _ = stores[0].shape
     rows_in = features // (nz // 2 * blocks_x)
 
-    def part_of():
-        return pl.BlockSpec((layers, rows, features), lambda i: (first // layers, 0, 0), memory_space=pltpu.VMEM)
+    def part_of(width):
+        return pl.BlockSpec((layers, rows, width), lambda i: (first // layers, 0, 0), memory_space=pltpu.VMEM)
 
     return pl.pallas_call(
         functools.partial(backward_kernel, first=first),
         grid=(1,),
-        in_specs=[SM, VM, VM, part_of(), part_of()] + [HB] * len(stores),
+        in_specs=[SM, VM, VM, part_of(features), part_of(features), part_of(LANES)] + [HB] * len(stores),
         out_specs=[VM] * 3,
         out_shape=[
             shape((layers, rows, features), BF),
@@ -250,7 +238,7 @@
             pltpu.SemaphoreType.DMA((SLOTS,)),
         ],
         name="backward_stage",
-    )(core, grad, gains, xs, pres, *stores)
+    )(core, grad, gains, xs, slopes, scales, *stores)
 
 
 def product_stage(n_rows, das, tails, chunk):
@@ -323,24 +311,24 @@
     iz, ix = lax.axis_index(("zh", "zl")), lax.axis_index("x")
     nz = nzh * nzl
     rows, features = own_rows.shape
-    cut = rows * 3 // 8
+    cut = rows // 4
+    piece_rows = (rows - cut) // 2
+    wide = []
+    for k in range(2):
+        first = cut + k * piece_rows
+        gathered = lax.all_gather(own_rows[first : first + piece_rows], ("zh", "zl", "x"), axis=0)
+        wide.append(gathered.reshape(nz, nx, piece_rows, features))
     a = own_rows[:cut]
     a_left, a_right = turn(a, "x", 1), turn(a, "x", -1)
-    a_half = cut // 3
-    a_far = jnp.concatenate([turn(a_left[:a_half], "x", 1), turn(a_right[a_half:], "x", -1)])
+    a_far = jnp.concatenate([turn(a_left[: cut // 2], "x", 1), turn(a_right[cut // 2 :], "x", -1)])
     line = jnp.zeros((nx, cut, features), BF)
     for steps, piece in ((0, a), (1, a_left), (-1, a_right), (2, a_far)):
         line = lax.dynamic_update_slice(line, piece[None], ((ix - steps) % nx, 0, 0))
-    column = jnp.zeros((nz, rows - cut, features), BF)
-    for steps, piece in ring_spread(own_rows[cut:], ("zh", "zl"), nz // 2 - 1):
-        column = lax.dynamic_update_slice(column, piece[None], ((iz - steps) % nz, 0, 0))
-    line, column, small = lax.optimization_barrier((line, column, small))
+    line, small = lax.optimization_barrier((line, small))
     top = jnp.zeros((nz, nx, cut, features), BF)
     for steps, piece in ring_spread(line, ("zh", "zl"), nz // 2):
         top = lax.dynamic_update_slice(top, piece[None], ((iz - steps) % nz, 0, 0, 0))
-    left, right = turn(column, "x", 1), turn(column, "x", -1)
-    far = jnp.concatenate([turn(left[: nz // 2], "x", 1), turn(right[nz // 2 :], "x", -1)])
-    own = [top, column, left, right, far]
+    own = [top] + wide
     return own + [turn(piece, "c", 1) for piece in own], small
 
 
@@ -383,10 +371,11 @@
         jnp.zeros((layers, tokens, features), BF),
         jnp.zeros((nx, layers, tokens, features // nx), BF),
         jnp.zeros((layers, tokens, features), F32),
+        jnp.zeros((layers, tokens, LANES), F32),
         x,
     )
     for stage in range(ny):
-        x_in = x if stage == 0 else shift(saved[3], "y", 1)
+        x_in = x if stage == 0 else shift(saved[-1], "y", 1)
         saved = lax.cond(
             iy == stage,
             lambda x_in, saved: tuple(forward_stage(core, x_in, gains, stores, nx)),
@@ -394,7 +383,7 @@
             x_in,
             saved,
         )
-    xs, ns, pres, x_top = saved
+    xs, ns, slopes, scales, x_top = saved
 
     q, f, final_part, grad = lax.cond(
         iy == ny - 1,
@@ -413,7 +402,7 @@
     def backward(stage, grad_in, kept, first, count):
         return lax.cond(
             iy == stage,
-            lambda grad_in, kept: tuple(backward_stage(core, grad_in, gains, xs, pres, stores, first, count)),
+            lambda grad_in, kept: tuple(backward_stage(core, grad_in, gains, xs, slopes, scales, stores, first, count)),
             lambda grad_in, kept: kept,
             grad_in,
             kept,

time: 551 us -> 583 us (1.058)
  the two profiles are of different devices: /device:TPU:102 before, /device:TPU:8 now
where the time goes in v1:
time: 583 us; the launch traced here: 572 us
  waiting for transfers between devices  342 us (59%)
  starting transfers between devices  119 us (20%)
  Pallas kernels  39.4 us (7%)
  local copies, waits for them, and re-layouts  38.8 us (7%)
  between operations  15.4 us (3%)
  other arithmetic  15.1 us (3%)
    ppermute x56, waiting for transfers between devices, turn(): lax.ppermute(value, axis, [(i, (i + steps) % count) for i in range(count)])  156 us
    ppermute x6, waiting for transfers between devices, shift(): lax.ppermute(value, axis, [(i, i + steps) for i in range(count) if 0 <= i...  95.1 us
    ppermute x56, starting transfers between devices, turn(): lax.ppermute(value, axis, [(i, (i + steps) % count) for i in range(count)])  92.3 us
    all_gather x2, waiting for transfers between devices, gather_weights(): lax.all_gather(own_rows[first:first + piece_rows], ('zh', 'zl', 'x'), axi...  90 us
    ppermute x6, starting transfers between devices, shift(): lax.ppermute(value, axis, [(i, i + steps) for i in range(count) if 0 <= i...  26.7 us
    pallas_call x1, Pallas kernels, backward_stage(): pl.pallas_call(functools.partial(backward_kernel, first=first), grid=(1,)...  16.7 us
    pallas_call x1, Pallas kernels, forward_stage(): pl.pallas_call(forward_kernel, in_specs=[SM, VM, VM] + [HB] * len(stores)...  13.3 us
  transfers between devices with their start and end apart: 64, of which 30 were waited for; matrix products, arithmetic and copies ran while one was open for 6% of the time, Pallas kernels for 4%

profile of v1, /device:TPU:8, one launch (start us, length us, event | category | flops | bytes accessed | tf_op | source)
XLA Modules:
  0.0 571.9 jit_solution(5743652631830136929)
XLA Ops:
  15.8 7.3 %collective-permute-start.5 = (f32[2,2048]{1,0:T(2,128)S(1)}, f32[2,2048]{1,0:T(2,128)S(1)}, u32[]{:S(2)}, u32[]{:S(2)}) collective-permute-start(f32[2,2048]{1,0:T(2,128)S(1)} %maximum_select_fusion.2), channel_id=1, source_target_pairs={{0,32},{32,0},{1,33},{33,1},{2,34},{34,2},{3,35},{35,3},{4,36},{36... | collective-permute-start | bytes 49160 | tf_op jit(solution)/shard_map/ppermute | solution.py:279
  34.5 9.8 %collective-permute-done.8 = bf16[4,16,2048]{2,1,0:T(8,128)(2,1)S(1)} collective-permute-done((bf16[4,16,2048]{2,1,0:T(8,128)(2,1)S(1)}, bf16[4,16,2048]{2,1,0:T(8,128)(2,1)S(1)}, u32[]{:S(2)}, u32[]{:S(2)}) %collective-permute-start.8) | collective-permute-done | bytes 262176 | tf_op jit(solution)/shard_map/ppermute | solution.py:279
  44.8 24.0 %collective-permute-done.9 = bf16[8,16,2048]{2,1,0:T(8,128)(2,1)S(1)} collective-permute-done((bf16[8,16,2048]{2,1,0:T(8,128)(2,1)S(1)}, bf16[8,16,2048]{2,1,0:T(8,128)(2,1)S(1)}, u32[]{:S(2)}, u32[]{:S(2)}) %collective-permute-start.9) | collective-permute-done | bytes 524320 | tf_op jit(solution)/shard_map/ppermute | solution.py:279
  72.3 11.8 %collective-permute-done.10 = bf16[4,32,2048]{2,1,0:T(8,128)(2,1)S(1)} collective-permute-done((bf16[4,32,2048]{2,1,0:T(8,128)(2,1)S(1)}, bf16[4,32,2048]{2,1,0:T(8,128)(2,1)S(1)}, u32[]{:S(2)}, u32[]{:S(2)}) %collective-permute-start.10) | collective-permute-done | bytes 524320 | tf_op jit(solution)/shard_map/ppermute | solution.py:279
  90.6 20.1 %collective-permute-done.11 = bf16[4,32,2048]{2,1,0:T(8,128)(2,1)S(1)} collective-permute-done((bf16[4,32,2048]{2,1,0:T(8,128)(2,1)S(1)}, bf16[4,32,2048]{2,1,0:T(8,128)(2,1)S(1)}, u32[]{:S(2)}, u32[]{:S(2)}) %collective-permute-start.11) | collective-permute-done | bytes 524320 | tf_op jit(solution)/shard_map/ppermute | solution.py:279
  118.4 18.5 %collective-permute-done.12 = bf16[4,32,2048]{2,1,0:T(8,128)(2,1)} collective-permute-done((bf16[4,32,2048]{2,1,0:T(8,128)(2,1)S(1)}, bf16[4,32,2048]{2,1,0:T(8,128)(2,1)}, u32[]{:S(2)}, u32[]{:S(2)}) %collective-permute-start.12) | collective-permute-done | bytes 524320 | tf_op jit(solution)/shard_map/ppermute | solution.py:279
  137.7 90.0 %all-gather.5.cloned.1.call-done = bf16[32,48,2048]{2,1,0:T(8,128)(2,1)} async-done(((bf16[1,48,2048]{2,1,0:T(8,128)(2,1)}), bf16[32,48,2048]{2,1,0:T(8,128)(2,1)}) %all-gather.5.cloned.1.call-update) | async-done | bytes 6291472 | tf_op jit(solution)/shard_map/all_gather | solution.py:319
  236.4 7.7 %collective-permute-done.17 = bf16[8,4,32,2048]{3,2,1,0:T(8,128)(2,1)} collective-permute-done((bf16[8,4,32,2048]{3,2,1,0:T(8,128)(2,1)}, bf16[8,4,32,2048]{3,2,1,0:T(8,128)(2,1)}, u32[]{:S(2)}, u32[]{:S(2)}) %collective-permute-start.17) | collective-permute-done | bytes 4194336 | tf_op jit(solution)/shard_map/ppermute | solution.py:279
  249.1 18.9 %collective-permute-done.20 = bf16[64,2048]{1,0:T(8,128)(2,1)} collective-permute-done((bf16[64,2048]{1,0:T(8,128)(2,1)}, bf16[64,2048]{1,0:T(8,128)(2,1)}, u32[]{:S(2)}, u32[]{:S(2)}) %collective-permute-start.20) | collective-permute-done | bytes 262176 | tf_op jit(solution)/shard_map/ppermute | solution.py:284
  268.0 13.3 %conditional.11 = ((bf16[4,64,2048]{2,1,0:T(8,128)(2,1)S(1)}, bf16[4,4,64,512]{3,2,1,0:T(8,128)(2,1)}, f32[4,64,2048]{2,1,0:T(8,128)S(1)}, f32[4,64,128]{2,1,0:T(8,128)S(1)}, bf16[64,2048]{1,0:T(8,128)(2,1)})) conditional(s32[]{:T(128)} %convert_element_type.204, (bf16[4,64,2048]{2,1,0:T(8,128)(2,1)S(1)}, bf16[4,4,64,512]{3,2,1,0:T(8,128)(2,1)}, ...), branch_computations={%region_2.3_spmd, %region_3.4_spmd} | conditional | bytes 8 | solution.py:379
  268.0 13.3 %forward_stage.5 = (bf16[4,64,2048]{2,1,0:T(8,128)(2,1)S(1)}, bf16[4,4,64,512]{3,2,1,0:T(8,128)(2,1)}, f32[4,64,2048]{2,1,0:T(8,128)S(1)}, f32[4,64,128]{2,1,0:T(8,128)S(1)}, bf16[64,2048]{1,0:T(8,128)(2,1)}) custom-call(s32[2]{0:T(128)S(1)} %get-tuple-element.378.pos, bf16[64,2048]{1,0:T(8,128)(2,1)} %get-tuple-element.379.x_ref, ...), custom_call_target="tpu_custom_call" | custom-call | tf_op jit(solution)/shard_map/cond/branch_1_fun/forward_stage/pallas_call | solution.py:198
  283.3 8.2 %collective-permute-done.21 = bf16[64,2048]{1,0:T(8,128)(2,1)} collective-permute-done((bf16[64,2048]{1,0:T(8,128)(2,1)}, bf16[64,2048]{1,0:T(8,128)(2,1)}, u32[]{:S(2)}, u32[]{:S(2)}) %collective-permute-start.21) | collective-permute-done | bytes 262176 | tf_op jit(solution)/shard_map/ppermute | solution.py:284
  291.5 15.5 %collective-permute-start.22 = (bf16[64,2048]{1,0:T(8,128)(2,1)}, bf16[64,2048]{1,0:T(8,128)(2,1)}, u32[]{:S(2)}, u32[]{:S(2)}) collective-permute-start(bf16[64,2048]{1,0:T(8,128)(2,1)} %get-tuple-element.534), channel_id=1, source_target_pairs={{0,64},{64,128},{128,192},{1,65},{65,129},{129,193},{2,66},{66,130... | collective-permute-start | bytes 786440 | tf_op jit(solution)/shard_map/ppermute | solution.py:284
  321.8 9.7 %collective-permute-done.23 = bf16[64,2048]{1,0:T(8,128)(2,1)} collective-permute-done((bf16[64,2048]{1,0:T(8,128)(2,1)}, bf16[64,2048]{1,0:T(8,128)(2,1)}, u32[]{:S(2)}, u32[]{:S(2)}) %collective-permute-start.23) | collective-permute-done | bytes 262176 | tf_op jit(solution)/shard_map/ppermute | solution.py:284
  339.2 47.9 %collective-permute-done.24 = bf16[64,2048]{1,0:T(8,128)(2,1)} collective-permute-done((bf16[64,2048]{1,0:T(8,128)(2,1)}, bf16[64,2048]{1,0:T(8,128)(2,1)}, u32[]{:S(2)}, u32[]{:S(2)}) %collective-permute-start.24) | collective-permute-done | bytes 262176 | tf_op jit(solution)/shard_map/ppermute | solution.py:284
  387.2 16.7 %conditional.17 = ((bf16[64,2048]{1,0:T(8,128)(2,1)}, bf16[4,64,2048]{2,1,0:T(8,128)(2,1)}, f32[4,2048]{1,0:T(4,128)S(1)})) conditional(s32[]{:T(128)} %convert_element_type.204, (bf16[64,2048]{1,0:T(8,128)(2,1)}, bf16[4,64,2048]{2,1,0:T(8,128)(2,1)}, f32[4,2048]{1,0:T(4,128)S(1)}) %tuple.133, (s32[2]{0:T(128)S(1)}, bf16[64,2048]{1,0:T(8,128)(2,1)}, ...), branch_computations={%region_14.15_spmd, %region_15.16_spmd} | conditional | bytes 32 | solution.py:403
  387.2 16.7 %backward_stage.11 = (bf16[4,64,2048]{2,1,0:T(8,128)(2,1)}, f32[4,2048]{1,0:T(4,128)S(1)}, bf16[64,2048]{1,0:T(8,128)(2,1)}) custom-call(s32[2]{0:T(128)S(1)} %get-tuple-element.434.pos, bf16[64,2048]{1,0:T(8,128)(2,1)} %get-tuple-element.435.grad_ref, f32[4,2048]{1,0:T(4,128)S(1)} %get-tuple-element.436.gain_ref, ...), custom_call_target="tpu_custom_call" | custom-call | tf_op jit(solution)/shard_map/cond/branch_1_fun/backward_stage/pallas_call | solution.py:225
  408.5 5.2 collective-permute-done.25
  426.9 9.3 %collective-permute-done.36 = bf16[2,64,2048]{2,1,0:T(8,128)(2,1)S(1)} collective-permute-done((bf16[2,64,2048]{2,1,0:T(8,128)(2,1)}, bf16[2,64,2048]{2,1,0:T(8,128)(2,1)S(1)}, u32[]{:S(2)}, u32[]{:S(2)}) %collective-permute-start.36) | collective-permute-done | bytes 524320 | tf_op jit(solution)/shard_map/ppermute | solution.py:279
  440.6 6.9 %collective-permute-done.31 = bf16[2,64,2048]{2,1,0:T(8,128)(2,1)S(1)} collective-permute-done((bf16[2,64,2048]{2,1,0:T(8,128)(2,1)}, bf16[2,64,2048]{2,1,0:T(8,128)(2,1)S(1)}, u32[]{:S(2)}, u32[]{:S(2)}) %collective-permute-start.31) | collective-permute-done | bytes 524320 | tf_op jit(solution)/shard_map/ppermute | solution.py:279
  458.3 8.3 %collective-permute-done.33 = bf16[1,64,2048]{2,1,0:T(8,128)(2,1)S(1)} collective-permute-done((bf16[1,64,2048]{2,1,0:T(8,128)(2,1)S(1)}, bf16[1,64,2048]{2,1,0:T(8,128)(2,1)S(1)}, u32[]{:S(2)}, u32[]{:S(2)}) %collective-permute-start.33) | collective-permute-done | bytes 262176 | tf_op jit(solution)/shard_map/ppermute | solution.py:279
  493.6 5.7 collective-permute-done.45
  500.3 5.2 collective-permute-done.52
  538.5 21.7 %collective-permute-start.61 = (f32[2,2048]{1,0:T(2,128)S(1)}, f32[2,2048]{1,0:T(2,128)S(1)}, u32[]{:S(2)}, u32[]{:S(2)}) collective-permute-start(f32[2,2048]{1,0:T(2,128)S(1)} %get-tuple-element.621), channel_id=1, source_target_pairs={{0,192},{64,0},{128,64},{192,128},{1,193},{65,1},{129,65},{193,129... | collective-permute-start | bytes 49160 | tf_op jit(solution)/shard_map/ppermute | solution.py:279
  (268 shorter events, 184.2 us)
Async XLA Ops:
  7.2 130.5 %all-gather.3.cloned.1.call-start = ((), (), s32[]{:S(2)}) async-start(), calls=%async_computation | async-start | bytes 6488064 | tf_op jit(solution)/shard_map/all_gather | solution.py:319
  9.0 218.6 %all-gather.5.cloned.1.call-start = ((), (), s32[]{:S(2)}) async-start(), calls=%async_computation.1 | async-start | bytes 6488064 | tf_op jit(solution)/shard_map/all_gather | solution.py:319
  44.4 24.5 %collective-permute-start.9 = (bf16[8,16,2048]{2,1,0:T(8,128)(2,1)S(1)}, bf16[8,16,2048]{2,1,0:T(8,128)(2,1)S(1)}, u32[]{:S(2)}, u32[]{:S(2)}) collective-permute-start(bf16[8,16,2048]{2,1,0:T(8,128)(2,1)S(1)} %pad_maximum_fusion.2), channel_id=1, source_target_pairs={{0,8},{4,12},{8,0},{12,4},{1,9},{5,13},{9,1},{13,5},{2,10},{6,14},... | collective-permute-start | bytes 1572872 | tf_op jit(solution)/shard_map/ppermute | solution.py:279
  69.0 17.9 %collective-permute-start.14 = (bf16[4,32,2048]{2,1,0:T(8,128)(2,1)S(1)}, bf16[4,32,2048]{2,1,0:T(8,128)(2,1)S(1)}, u32[]{:S(2)}, u32[]{:S(2)}) collective-permute-start(bf16[4,32,2048]{2,1,0:T(8,128)(2,1)S(1)} %fusion.25), channel_id=1, source_target_pairs={{0,44},{4,0},{8,4},{12,8},{32,12},{36,32},{40,36},{44,40},{1,45},{... | collective-permute-start | bytes 1572872 | tf_op jit(solution)/shard_map/ppermute | solution.py:279
  84.0 26.7 %collective-permute-start.11 = (bf16[4,32,2048]{2,1,0:T(8,128)(2,1)S(1)}, bf16[4,32,2048]{2,1,0:T(8,128)(2,1)S(1)}, u32[]{:S(2)}, u32[]{:S(2)}) collective-permute-start(bf16[4,32,2048]{2,1,0:T(8,128)(2,1)S(1)} %collective-permute-done.10), channel_id=1, source_target_pairs={{0,4},{4,8},{8,12},{12,32},{32,36},{36,40},{40,44},{44,0},{1,5},{5... | collective-permute-start | bytes 1572872 | tf_op jit(solution)/shard_map/ppermute | solution.py:279
  86.9 28.0 %collective-permute-start.15 = (bf16[4,32,2048]{2,1,0:T(8,128)(2,1)S(1)}, bf16[4,32,2048]{2,1,0:T(8,128)(2,1)}, u32[]{:S(2)}, u32[]{:S(2)}) collective-permute-start(bf16[4,32,2048]{2,1,0:T(8,128)(2,1)S(1)} %collective-permute-done.14), channel_id=1, source_target_pairs={{0,44},{4,0},{8,4},{12,8},{32,12},{36,32},{40,36},{44,40},{1,45},{... | collective-permute-start | bytes 1572872 | tf_op jit(solution)/shard_map/ppermute | solution.py:279
  110.7 26.1 %collective-permute-start.12 = (bf16[4,32,2048]{2,1,0:T(8,128)(2,1)S(1)}, bf16[4,32,2048]{2,1,0:T(8,128)(2,1)}, u32[]{:S(2)}, u32[]{:S(2)}) collective-permute-start(bf16[4,32,2048]{2,1,0:T(8,128)(2,1)S(1)} %collective-permute-done.11), channel_id=1, source_target_pairs={{0,4},{4,8},{8,12},{12,32},{32,36},{36,40},{40,44},{44,0},{1,5},{5... | collective-permute-start | bytes 1572872 | tf_op jit(solution)/shard_map/ppermute | solution.py:279
  114.9 118.3 %collective-permute-start.16 = (bf16[4,32,2048]{2,1,0:T(8,128)(2,1)}, bf16[4,32,2048]{2,1,0:T(8,128)(2,1)S(1)}, u32[]{:S(2)}, u32[]{:S(2)}) collective-permute-start(bf16[4,32,2048]{2,1,0:T(8,128)(2,1)} %collective-permute-done.15), channel_id=1, source_target_pairs={{0,44},{4,0},{8,4},{12,8},{32,12},{36,32},{40,36},{44,40},{1,45},{... | collective-permute-start | bytes 1572872 | tf_op jit(solution)/shard_map/ppermute | solution.py:279
  136.8 92.7 %collective-permute-start.13 = (bf16[4,32,2048]{2,1,0:T(8,128)(2,1)}, bf16[4,32,2048]{2,1,0:T(8,128)(2,1)S(1)}, u32[]{:S(2)}, u32[]{:S(2)}) collective-permute-start(bf16[4,32,2048]{2,1,0:T(8,128)(2,1)} %collective-permute-done.12), channel_id=1, source_target_pairs={{0,4},{4,8},{8,12},{12,32},{32,36},{36,40},{40,44},{44,0},{1,5},{5... | collective-permute-start | bytes 1572872 | tf_op jit(solution)/shard_map/ppermute | solution.py:279
  137.7 106.5 %collective-permute-start.18 = (bf16[8,4,48,2048]{3,2,1,0:T(8,128)(2,1)}, bf16[8,4,48,2048]{3,2,1,0:T(8,128)(2,1)}, u32[]{:S(2)}, u32[]{:S(2)}) collective-permute-start(bf16[8,4,48,2048]{3,2,1,0:T(8,128)(2,1)} %bitcast.160), channel_id=1, source_target_pairs={{0,16},{16,0},{1,17},{17,1},{2,18},{18,2},{3,19},{19,3},{4,20},{20... | collective-permute-start | bytes 18874376 | tf_op jit(solution)/shard_map/ppermute | solution.py:279
  245.7 22.4 %collective-permute-start.20 = (bf16[64,2048]{1,0:T(8,128)(2,1)}, bf16[64,2048]{1,0:T(8,128)(2,1)}, u32[]{:S(2)}, u32[]{:S(2)}) collective-permute-start(bf16[64,2048]{1,0:T(8,128)(2,1)} %get-tuple-element.532), channel_id=1, source_target_pairs={{0,64},{64,128},{128,192},{1,65},{65,129},{129,193},{2,66},{66,130... | collective-permute-start | bytes 786440 | tf_op jit(solution)/shard_map/ppermute | solution.py:284
  291.5 20.7 %collective-permute-start.22 = (bf16[64,2048]{1,0:T(8,128)(2,1)}, bf16[64,2048]{1,0:T(8,128)(2,1)}, u32[]{:S(2)}, u32[]{:S(2)}) collective-permute-start(bf16[64,2048]{1,0:T(8,128)(2,1)} %get-tuple-element.534), channel_id=1, source_target_pairs={{0,64},{64,128},{128,192},{1,65},{65,129},{129,193},{2,66},{66,130... | collective-permute-start | bytes 786440 | tf_op jit(solution)/shard_map/ppermute | solution.py:284
  331.5 55.6 %collective-permute-start.24 = (bf16[64,2048]{1,0:T(8,128)(2,1)}, bf16[64,2048]{1,0:T(8,128)(2,1)}, u32[]{:S(2)}, u32[]{:S(2)}) collective-permute-start(bf16[64,2048]{1,0:T(8,128)(2,1)} %get-tuple-element.548), channel_id=1, source_target_pairs={{64,0},{128,64},{192,128},{65,1},{129,65},{193,129},{66,2},{130,66... | collective-permute-start | bytes 786440 | tf_op jit(solution)/shard_map/ppermute | solution.py:284
  335.8 70.3 %collective-permute-start.27 = (bf16[2,2,64,512]{3,2,1,0:T(8,128)(2,1)}, bf16[2,2,64,512]{3,2,1,0:T(8,128)(2,1)}, u32[]{:S(2)}, u32[]{:S(2)}) collective-permute-start(bf16[2,2,64,512]{3,2,1,0:T(8,128)(2,1)} %get-tuple-element.598), channel_id=1, source_target_pairs={{0,1},{1,2},{2,3},{3,0},{4,5},{5,6},{6,7},{7,4},{8,9},{9,10},{10,1... | collective-permute-start | bytes 786440 | tf_op jit(solution)/shard_map/ppermute | solution.py:279
  336.0 70.1 %collective-permute-start.28 = (bf16[2,2,64,512]{3,2,1,0:T(8,128)(2,1)}, bf16[2,2,64,512]{3,2,1,0:T(8,128)(2,1)}, u32[]{:S(2)}, u32[]{:S(2)}) collective-permute-start(bf16[2,2,64,512]{3,2,1,0:T(8,128)(2,1)} %get-tuple-element.599), channel_id=1, source_target_pairs={{0,3},{1,0},{2,1},{3,2},{4,7},{5,4},{6,5},{7,6},{8,11},{9,8},{10,9... | collective-permute-start | bytes 786440 | tf_op jit(solution)/shard_map/ppermute | solution.py:279
  339.0 67.1 %collective-permute-start.29 = (bf16[2,2,64,512]{3,2,1,0:T(8,128)(2,1)}, bf16[2,2,64,512]{3,2,1,0:T(8,128)(2,1)}, u32[]{:S(2)}, u32[]{:S(2)}) collective-permute-start(bf16[2,2,64,512]{3,2,1,0:T(8,128)(2,1)} %get-tuple-element.600), channel_id=1, source_target_pairs={{0,2},{1,3},{2,0},{3,1},{4,6},{5,7},{6,4},{7,5},{8,10},{9,11},{10,... | collective-permute-start | bytes 786440 | tf_op jit(solution)/shard_map/ppermute | solution.py:279
  339.2 66.7 %collective-permute-start.30 = (bf16[64,256]{0,1:T(8,128)(2,1)S(1)}, bf16[64,256]{0,1:T(8,128)(2,1)S(1)}, u32[]{:S(2)}, u32[]{:S(2)}) collective-permute-start(bf16[64,256]{0,1:T(8,128)(2,1)S(1)} %fusion.28), channel_id=1, source_target_pairs={{0,16},{16,0},{1,17},{17,1},{2,18},{18,2},{3,19},{19,3},{4,20},{20... | collective-permute-start | bytes 98312 | tf_op jit(solution)/shard_map/ppermute | solution.py:279
  423.3 24.2 %collective-permute-start.31 = (bf16[2,64,2048]{2,1,0:T(8,128)(2,1)}, bf16[2,64,2048]{2,1,0:T(8,128)(2,1)S(1)}, u32[]{:S(2)}, u32[]{:S(2)}) collective-permute-start(bf16[2,64,2048]{2,1,0:T(8,128)(2,1)} %get-tuple-element.560), channel_id=1, source_target_pairs={{0,1},{1,2},{2,3},{3,0},{4,5},{5,6},{6,7},{7,4},{8,9},{9,10},{10,1... | collective-permute-start | bytes 1572872 | tf_op jit(solution)/shard_map/ppermute | solution.py:279
  423.3 24.2 %collective-permute-start.32 = (bf16[2,64,2048]{2,1,0:T(8,128)(2,1)}, bf16[2,64,2048]{2,1,0:T(8,128)(2,1)S(1)}, u32[]{:S(2)}, u32[]{:S(2)}) collective-permute-start(bf16[2,64,2048]{2,1,0:T(8,128)(2,1)} %get-tuple-element.560), channel_id=1, source_target_pairs={{0,3},{1,0},{2,1},{3,2},{4,7},{5,4},{6,5},{7,6},{8,11},{9,8},{10,9... | collective-permute-start | bytes 1572872 | tf_op jit(solution)/shard_map/ppermute | solution.py:279
  440.6 29.8 %collective-permute-start.42 = (bf16[48,2048]{1,0:T(8,128)(2,1)}, bf16[48,2048]{1,0:T(8,128)(2,1)}, u32[]{:S(2)}, u32[]{:S(2)}) collective-permute-start(bf16[48,2048]{1,0:T(8,128)(2,1)} %get-tuple-element.611), channel_id=1, source_target_pairs={{0,1},{1,2},{2,3},{3,0},{4,5},{5,6},{6,7},{7,4},{8,9},{9,10},{10,1... | collective-permute-start | bytes 589832 | tf_op jit(solution)/shard_map/ppermute | solution.py:279
  447.5 22.9 %collective-permute-start.43 = (bf16[48,2048]{1,0:T(8,128)(2,1)}, bf16[48,2048]{1,0:T(8,128)(2,1)}, u32[]{:S(2)}, u32[]{:S(2)}) collective-permute-start(bf16[48,2048]{1,0:T(8,128)(2,1)} %get-tuple-element.612), channel_id=1, source_target_pairs={{0,3},{1,0},{2,1},{3,2},{4,7},{5,4},{6,5},{7,6},{8,11},{9,8},{10,9... | collective-permute-start | bytes 589832 | tf_op jit(solution)/shard_map/ppermute | solution.py:279
  447.5 22.9 %collective-permute-start.44 = (bf16[48,2048]{1,0:T(8,128)(2,1)S(1)}, bf16[48,2048]{1,0:T(8,128)(2,1)}, u32[]{:S(2)}, u32[]{:S(2)}) collective-permute-start(bf16[48,2048]{1,0:T(8,128)(2,1)S(1)} %get-tuple-element.613), channel_id=1, source_target_pairs={{0,2},{1,3},{2,0},{3,1},{4,6},{5,7},{6,4},{7,5},{8,10},{9,11},{10,... | collective-permute-start | bytes 589832 | tf_op jit(solution)/shard_map/ppermute | solution.py:279
  538.4 23.8 %collective-permute-start.60 = (f32[2,2048]{1,0:T(2,128)S(1)}, f32[2,2048]{1,0:T(2,128)S(1)}, u32[]{:S(2)}, u32[]{:S(2)}) collective-permute-start(f32[2,2048]{1,0:T(2,128)S(1)} %get-tuple-element.620), channel_id=1, source_target_pairs={{0,128},{64,192},{128,0},{192,64},{1,129},{65,193},{129,1},{193,65... | collective-permute-start | bytes 49160 | tf_op jit(solution)/shard_map/ppermute | solution.py:279
  538.5 24.8 %collective-permute-start.61 = (f32[2,2048]{1,0:T(2,128)S(1)}, f32[2,2048]{1,0:T(2,128)S(1)}, u32[]{:S(2)}, u32[]{:S(2)}) collective-permute-start(f32[2,2048]{1,0:T(2,128)S(1)} %get-tuple-element.621), channel_id=1, source_target_pairs={{0,192},{64,0},{128,64},{192,128},{1,193},{65,1},{129,65},{193,129... | collective-permute-start | bytes 49160 | tf_op jit(solution)/shard_map/ppermute | solution.py:279
  (56 other events, 613.1 us)
Sparse Core Ops, SparseCore 0:
  10.6 126.8 all-gather.2
  140.6 87.0 all-gather.4

commit v2 on v1

--- a/solution.py
+++ b/solution.py
@@ -39,19 +39,24 @@
     count = len(pieces) // 2
 
     def run(refs):
+        top, *by_x = refs
+        nz, nx, cut, features = top.shape
+        zs, size = nz // 2, features // CHUNKS
         for part in range(CHUNKS):
             slot = bank * CHUNKS + part
-            top = 0
-            for ref in refs:
-                nz, _, rows, features = ref.shape
-                zs, size = nz // 2, features // CHUNKS
+            cols = pl.ds(part * size, size)
+            if by_rows:
+                source, target = top.at[half * zs + part], wbuf.at[slot, :, pl.ds(0, cut), :]
+            else:
+                source, target = top.at[pl.ds(half * zs, zs), :, :, cols], wbuf.at[slot, :, :, pl.ds(0, cut), :]
+            pltpu.make_async_copy(source, target, sems.at[slot]).start()
+            for ref, offset in zip(by_x, (0, nx - 1, 1, 2)):
+                x = lax.rem(pos[1] + offset, nx)
+                rows = pl.ds(cut, ref.shape[1])
                 if by_rows:
-                    source = ref.at[half * zs + part]
-                    target = wbuf.at[slot, :, pl.ds(top, rows), :]
+                    source, target = ref.at[half * zs + part], wbuf.at[slot, x, rows, :]
                 else:
-                    source = ref.at[pl.ds(half * zs, zs), :, :, pl.ds(part * size, size)]
-                    target = wbuf.at[slot, :, :, pl.ds(top, rows), :]
-                top += rows
+                    source, target = ref.at[pl.ds(half * zs, zs), :, cols], wbuf.at[slot, :, x, rows, :]
                 pltpu.make_async_copy(source, target, sems.at[slot]).start()
 
     @pl.when(pos[0] == layer % 2)
@@ -292,44 +297,46 @@
     return jnp.where(place == 0, jnp.stack([own, partner]), jnp.stack([partner, own]))
 
 
-def ring_spread(value, axes, ups):
+def ring_spread(value, axes, ups, beside=None):
     count = lax.axis_size(axes)
     out = [(0, value)]
     moving = value
     for step in range(1, ups + 1):
+        if step == ups and beside is not None:
+            moving, beside = lax.optimization_barrier((moving, beside))
         moving = turn(moving, axes, 1)
         out.append((step, moving))
     moving = value
     for step in range(1, count - ups):
         moving = turn(moving, axes, -1)
         out.append((-step, moving))
-    return out
-
-
-def gather_weights(own_rows, small):
+    return out, beside
+
+
+def gather_weights(own_rows, small, small_inputs):
     nzh, nzl, nx = (lax.axis_size(a) for a in ("zh", "zl", "x"))
     iz, ix = lax.axis_index(("zh", "zl")), lax.axis_index("x")
     nz = nzh * nzl
     rows, features = own_rows.shape
-    cut = rows // 4
-    piece_rows = (rows - cut) // 2
-    wide = []
-    for k in range(2):
-        first = cut + k * piece_rows
-        gathered = lax.all_gather(own_rows[first : first + piece_rows], ("zh", "zl", "x"), axis=0)
-        wide.append(gathered.reshape(nz, nx, piece_rows, features))
+    cut = rows * 3 // 8
     a = own_rows[:cut]
     a_left, a_right = turn(a, "x", 1), turn(a, "x", -1)
-    a_far = jnp.concatenate([turn(a_left[: cut // 2], "x", 1), turn(a_right[cut // 2 :], "x", -1)])
+    a_far = jnp.concatenate([turn(a_left[: cut // 3], "x", 1), turn(a_right[cut // 3 :], "x", -1)])
     line = jnp.zeros((nx, cut, features), BF)
     for steps, piece in ((0, a), (1, a_left), (-1, a_right), (2, a_far)):
         line = lax.dynamic_update_slice(line, piece[None], ((ix - steps) % nx, 0, 0))
-    line, small = lax.optimization_barrier((line, small))
+    column = jnp.zeros((nz, rows - cut, features), BF)
+    for steps, piece in ring_spread(own_rows[cut:], ("zh", "zl"), nz // 2 - 1)[0]:
+        column = lax.dynamic_update_slice(column, piece[None], ((iz - steps) % nz, 0, 0))
+    line, column, small_inputs = lax.optimization_barrier((line, column, small_inputs))
     top = jnp.zeros((nz, nx, cut, features), BF)
-    for steps, piece in ring_spread(line, ("zh", "zl"), nz // 2):
+    spread, smalls = ring_spread(line, ("zh", "zl"), nz // 2, small(*small_inputs))
+    for steps, piece in spread:
         top = lax.dynamic_update_slice(top, piece[None], ((iz - steps) % nz, 0, 0, 0))
-    own = [top] + wide
-    return own + [turn(piece, "c", 1) for piece in own], small
+    left, right = turn(column, "x", 1), turn(column, "x", -1)
+    far = jnp.concatenate([turn(left[: nz // 2], "x", 1), turn(right[nz // 2 :], "x", -1)])
+    own = [top, column, left, right, far]
+    return own + [turn(piece, "c", 1) for piece in own], smalls
 
 
 def body(token_ids, target_ids, embedding, section_weight, section_gain, final_gain):
@@ -343,29 +350,30 @@
     tokens = token_ids.size // layers
     core = jnp.stack([ic, ix])
 
-    gain_pair = in_order(section_gain[0], turn(section_gain[0], "c", 1), ic)
-    gains = in_order(gain_pair, turn(gain_pair, "zh", 1), izh).reshape(layers, features)
-
-    ring = embedding[None]
-    for axis, count in (("x", nx), ("zl", nzl)):
-        reach = 1
-        while reach < count:
-            ring = jnp.concatenate([ring, turn(ring, axis, reach)])
-            reach *= 2
-    stores, (gains, ring) = gather_weights(section_weight[0], (gains, ring))
-    from_zl = (izl - jnp.arange(nzl)) % nzl
-    from_x = (ix - jnp.arange(nx)) % nx
-    owner = from_zl[:, None] * nx + from_x[None, :]
-    row_ids = (owner[:, :, None] * part_rows + jnp.arange(part_rows)).reshape(-1)
     vocab_iota = jnp.arange(vocab_rows, dtype=jnp.int32)
-    select = (vocab_iota[:, None] == row_ids[None, :]).astype(BF)
-    table = jnp.dot(select, ring.reshape(vocab_rows, features), preferred_element_type=F32).astype(BF)
-
     share = izh * nc + ic
     token_own = pick(token_ids.reshape(layers, tokens), share, 0)
     target_own = pick(target_ids.reshape(layers, tokens), share, 0)
     onehot_in = (token_own[:, None] == vocab_iota[None, :]).astype(BF)
-    x = jnp.dot(onehot_in, table, preferred_element_type=F32).astype(BF)
+
+    def small(embedding, gain_row):
+        gain_pair = in_order(gain_row, turn(gain_row, "c", 1), ic)
+        gains = in_order(gain_pair, turn(gain_pair, "zh", 1), izh).reshape(layers, features)
+        ring = embedding[None]
+        for axis, count in (("x", nx), ("zl", nzl)):
+            reach = 1
+            while reach < count:
+                ring = jnp.concatenate([ring, turn(ring, axis, reach)])
+                reach *= 2
+        from_zl = (izl - jnp.arange(nzl)) % nzl
+        from_x = (ix - jnp.arange(nx)) % nx
+        owner = from_zl[:, None] * nx + from_x[None, :]
+        row_ids = (owner[:, :, None] * part_rows + jnp.arange(part_rows)).reshape(-1)
+        select = (vocab_iota[:, None] == row_ids[None, :]).astype(BF)
+        table = jnp.dot(select, ring.reshape(vocab_rows, features), preferred_element_type=F32).astype(BF)
+        return gains, table, jnp.dot(onehot_in, table, preferred_element_type=F32).astype(BF)
+
+    stores, (gains, table, x) = gather_weights(section_weight[0], small, (embedding, section_gain[0]))
 
     saved = (
         jnp.zeros((layers, tokens, features), BF),

time: 583 us -> 575 us (0.986)
  waiting for transfers between devices: 342 us -> 275 us
  starting transfers between devices: 119 us -> 170 us
  local copies, waits for them, and re-layouts: 38.8 us -> 54.3 us
  between operations: 15.4 us -> 1.93 us
    all_gather x2 -> x0, waiting for transfers between devices: 90 us -> none  [gather_weights(): lax.all_gather(own_rows[first:first + piece_rows], ('zh', 'zl', 'x'), axi...]
    ppermute x56 -> x69, starting transfers between devices: 92.3 us -> 143 us  [turn(): lax.ppermute(value, axis, [(i, (i + steps) % count) for i in range(count)])]
    ppermute x56 -> x69, waiting for transfers between devices: 156 us -> 178 us  [turn(): lax.ppermute(value, axis, [(i, (i + steps) % count) for i in range(count)])]
  transfers between devices with their start and end apart: 64 -> 75, of which waited for: 30 -> 33; matrix products, arithmetic and copies ran while one was open for 6% -> 10% of each run, Pallas kernels for 4% -> 4%
where the time goes in v2:
time: 575 us; the launch traced here: 564 us
  waiting for transfers between devices  275 us (48%)
  starting transfers between devices  170 us (30%)
  local copies, waits for them, and re-layouts  54.3 us (9%)
  Pallas kernels  41 us (7%)
  other arithmetic  19.4 us (3%)
    ppermute x69, waiting for transfers between devices, turn(): lax.ppermute(value, axis, [(i, (i + steps) % count) for i in range(count)])  178 us
    ppermute x69, starting transfers between devices, turn(): lax.ppermute(value, axis, [(i, (i + steps) % count) for i in range(count)])  143 us
    ppermute x6, waiting for transfers between devices, shift(): lax.ppermute(value, axis, [(i, i + steps) for i in range(count) if 0 <= i...  96.4 us
    ppermute x6, starting transfers between devices, shift(): lax.ppermute(value, axis, [(i, i + steps) for i in range(count) if 0 <= i...  27.6 us
    pallas_call x1, Pallas kernels, backward_stage(): pl.pallas_call(functools.partial(backward_kernel, first=first), grid=(1,)...  18.1 us
    pallas_call x1, Pallas kernels, forward_stage(): pl.pallas_call(forward_kernel, in_specs=[SM, VM, VM] + [HB] * len(stores)...  13.7 us
  transfers between devices with their start and end apart: 75, of which 33 were waited for; matrix products, arithmetic and copies ran while one was open for 10% of the time, Pallas kernels for 4%

profile of v2, /device:TPU:8, one launch (start us, length us, event | category | flops | bytes accessed | tf_op | source)
XLA Modules:
  0.0 564.0 jit_solution(10767289499477153843)
XLA Ops:
  63.2 43.9 %collective-permute-done.16 = bf16[1,16,2048]{2,1,0:T(8,128)(2,1)S(1)} collective-permute-done((bf16[1,16,2048]{2,1,0:T(8,128)(2,1)S(1)}, bf16[1,16,2048]{2,1,0:T(8,128)(2,1)S(1)}, u32[]{:S(2)}, u32[]{:S(2)}) %collective-permute-start.16) | collective-permute-done | bytes 65568 | tf_op jit(solution)/shard_map/ppermute | solution.py:284
  115.7 5.6 collective-permute-done.17
  125.2 7.3 %collective-permute-done.18 = bf16[4,16,2048]{2,1,0:T(8,128)(2,1)S(1)} collective-permute-done((bf16[4,16,2048]{2,1,0:T(8,128)(2,1)S(1)}, bf16[4,16,2048]{2,1,0:T(8,128)(2,1)S(1)}, u32[]{:S(2)}, u32[]{:S(2)}) %collective-permute-start.18) | collective-permute-done | bytes 262176 | tf_op jit(solution)/shard_map/ppermute | solution.py:284
  138.0 7.0 %collective-permute-done.12 = bf16[4,48,2048]{2,1,0:T(8,128)(2,1)S(1)} collective-permute-done((bf16[4,48,2048]{2,1,0:T(8,128)(2,1)}, bf16[4,48,2048]{2,1,0:T(8,128)(2,1)S(1)}, u32[]{:S(2)}, u32[]{:S(2)}) %collective-permute-start.12) | collective-permute-done | bytes 786464 | tf_op jit(solution)/shard_map/ppermute | solution.py:284
  145.1 13.7 %collective-permute-start.13 = (bf16[4,48,2048]{2,1,0:T(8,128)(2,1)S(1)}, bf16[4,48,2048]{2,1,0:T(8,128)(2,1)S(1)}, u32[]{:S(2)}, u32[]{:S(2)}) collective-permute-start(bf16[4,48,2048]{2,1,0:T(8,128)(2,1)S(1)} %collective-permute-done.12), channel_id=1, source_target_pairs={{0,4},{4,8},{8,12},{12,32},{32,36},{36,40},{40,44},{44,0},{1,5},{5... | collective-permute-start | bytes 2359304 | tf_op jit(solution)/shard_map/ppermute | solution.py:284
  163.8 8.3 %collective-permute-start.23 = (bf16[4,48,2048]{2,1,0:T(8,128)(2,1)S(1)}, bf16[4,48,2048]{2,1,0:T(8,128)(2,1)S(1)}, u32[]{:S(2)}, u32[]{:S(2)}) collective-permute-start(bf16[4,48,2048]{2,1,0:T(8,128)(2,1)S(1)} %collective-permute-done.22), channel_id=1, source_target_pairs={{0,44},{4,0},{8,4},{12,8},{32,12},{36,32},{40,36},{44,40},{1,45},{... | collective-permute-start | bytes 2359304 | tf_op jit(solution)/shard_map/ppermute | solution.py:284
  172.0 12.1 %collective-permute-start.20 = (bf16[4,48,2048]{2,1,0:T(8,128)(2,1)S(1)}, bf16[4,48,2048]{2,1,0:T(8,128)(2,1)S(1)}, u32[]{:S(2)}, u32[]{:S(2)}) collective-permute-start(bf16[4,48,2048]{2,1,0:T(8,128)(2,1)S(1)} %collective-permute-done.13), channel_id=1, source_target_pairs={{0,4},{4,8},{8,12},{12,32},{32,36},{36,40},{40,44},{44,0},{1,5},{5... | collective-permute-start | bytes 2359304 | tf_op jit(solution)/shard_map/ppermute | solution.py:284
  186.1 7.5 %collective-permute-done.20 = bf16[4,48,2048]{2,1,0:T(8,128)(2,1)S(1)} collective-permute-done((bf16[4,48,2048]{2,1,0:T(8,128)(2,1)S(1)}, bf16[4,48,2048]{2,1,0:T(8,128)(2,1)S(1)}, u32[]{:S(2)}, u32[]{:S(2)}) %collective-permute-start.20) | collective-permute-done | bytes 786464 | tf_op jit(solution)/shard_map/ppermute | solution.py:284
  205.7 27.0 %collective-permute-done.26 = bf16[4,80,2048]{2,1,0:T(8,128)(2,1)S(1)} collective-permute-done((bf16[4,80,2048]{2,1,0:T(8,128)(2,1)S(1)}, bf16[4,80,2048]{2,1,0:T(8,128)(2,1)S(1)}, u32[]{:S(2)}, u32[]{:S(2)}) %collective-permute-start.26) | collective-permute-done | bytes 1310752 | tf_op jit(solution)/shard_map/ppermute | solution.py:284
  248.9 15.2 %collective-permute-done.33 = bf16[64,2048]{1,0:T(8,128)(2,1)S(1)} collective-permute-done((bf16[64,2048]{1,0:T(8,128)(2,1)S(1)}, bf16[64,2048]{1,0:T(8,128)(2,1)S(1)}, u32[]{:S(2)}, u32[]{:S(2)}) %collective-permute-start.33) | collective-permute-done | bytes 262176 | tf_op jit(solution)/shard_map/ppermute | solution.py:289
  264.1 13.7 %conditional.11 = ((bf16[4,64,2048]{2,1,0:T(8,128)(2,1)}, bf16[4,4,64,512]{3,2,1,0:T(8,128)(2,1)}, f32[4,64,2048]{2,1,0:T(8,128)}, f32[4,64,128]{2,1,0:T(8,128)S(1)}, bf16[64,2048]{1,0:T(8,128)(2,1)S(1)})) conditional(s32[]{:T(128)} %convert_element_type.201, (bf16[4,64,2048]{2,1,0:T(8,128)(2,1)}, bf16[4,4,64,512]{3,2,1,0:T(8,128)(2,1)}, ...), branch_computations={%region_2.3_spmd, %region_3.4_spmd} | conditional | bytes 8 | solution.py:387
  264.1 13.7 %forward_stage.5 = (bf16[4,64,2048]{2,1,0:T(8,128)(2,1)}, bf16[4,4,64,512]{3,2,1,0:T(8,128)(2,1)}, f32[4,64,2048]{2,1,0:T(8,128)}, f32[4,64,128]{2,1,0:T(8,128)S(1)}, bf16[64,2048]{1,0:T(8,128)(2,1)S(1)}) custom-call(s32[2]{0:T(128)S(1)} %get-tuple-element.454.pos, bf16[64,2048]{1,0:T(8,128)(2,1)S(1)} %get-tuple-element.455.x_ref, ...), custom_call_target="tpu_custom_call" | custom-call | tf_op jit(solution)/shard_map/cond/branch_1_fun/forward_stage/pallas_call | solution.py:203
  279.8 8.4 %collective-permute-done.34 = bf16[64,2048]{1,0:T(8,128)(2,1)S(1)} collective-permute-done((bf16[64,2048]{1,0:T(8,128)(2,1)S(1)}, bf16[64,2048]{1,0:T(8,128)(2,1)S(1)}, u32[]{:S(2)}, u32[]{:S(2)}) %collective-permute-start.34) | collective-permute-done | bytes 262176 | tf_op jit(solution)/shard_map/ppermute | solution.py:289
  288.2 16.0 %collective-permute-start.35 = (bf16[64,2048]{1,0:T(8,128)(2,1)S(1)}, bf16[64,2048]{1,0:T(8,128)(2,1)S(1)}, u32[]{:S(2)}, u32[]{:S(2)}) collective-permute-start(bf16[64,2048]{1,0:T(8,128)(2,1)S(1)} %get-tuple-element.651), channel_id=1, source_target_pairs={{0,64},{64,128},{128,192},{1,65},{65,129},{129,193},{2,66},{66,130... | collective-permute-start | bytes 786440 | tf_op jit(solution)/shard_map/ppermute | solution.py:289
  304.2 5.7 %collective-permute-done.35 = bf16[64,2048]{1,0:T(8,128)(2,1)S(1)} collective-permute-done((bf16[64,2048]{1,0:T(8,128)(2,1)S(1)}, bf16[64,2048]{1,0:T(8,128)(2,1)S(1)}, u32[]{:S(2)}, u32[]{:S(2)}) %collective-permute-start.35) | collective-permute-done | bytes 262176 | tf_op jit(solution)/shard_map/ppermute | solution.py:289
  317.5 9.7 %collective-permute-done.36 = bf16[64,2048]{1,0:T(8,128)(2,1)} collective-permute-done((bf16[64,2048]{1,0:T(8,128)(2,1)}, bf16[64,2048]{1,0:T(8,128)(2,1)}, u32[]{:S(2)}, u32[]{:S(2)}) %collective-permute-start.36) | collective-permute-done | bytes 262176 | tf_op jit(solution)/shard_map/ppermute | solution.py:289
  334.8 52.7 %collective-permute-done.37 = bf16[64,2048]{1,0:T(8,128)(2,1)} collective-permute-done((bf16[64,2048]{1,0:T(8,128)(2,1)}, bf16[64,2048]{1,0:T(8,128)(2,1)}, u32[]{:S(2)}, u32[]{:S(2)}) %collective-permute-start.37) | collective-permute-done | bytes 262176 | tf_op jit(solution)/shard_map/ppermute | solution.py:289
  387.4 18.1 %conditional.17 = ((bf16[64,2048]{1,0:T(8,128)(2,1)}, bf16[4,64,2048]{2,1,0:T(8,128)(2,1)}, f32[4,2048]{1,0:T(4,128)S(1)})) conditional(s32[]{:T(128)} %convert_element_type.201, (bf16[64,2048]{1,0:T(8,128)(2,1)}, bf16[4,64,2048]{2,1,0:T(8,128)(2,1)}, f32[4,2048]{1,0:T(4,128)S(1)}) %tuple.135, (s32[2]{0:T(128)S(1)}, bf16[64,2048]{1,0:T(8,128)(2,1)}, ...), branch_computations={%region_14.15_spmd, %region_15.16_spmd} | conditional | bytes 32 | solution.py:411
  387.4 18.1 %backward_stage.11 = (bf16[4,64,2048]{2,1,0:T(8,128)(2,1)}, f32[4,2048]{1,0:T(4,128)S(1)}, bf16[64,2048]{1,0:T(8,128)(2,1)}) custom-call(s32[2]{0:T(128)S(1)} %get-tuple-element.530.pos, bf16[64,2048]{1,0:T(8,128)(2,1)} %get-tuple-element.531.grad_ref, f32[4,2048]{1,0:T(4,128)S(1)} %get-tuple-element.532.gain_ref, ...), custom_call_target="tpu_custom_call" | custom-call | tf_op jit(solution)/shard_map/cond/branch_1_fun/backward_stage/pallas_call | solution.py:230
  428.3 9.3 %collective-permute-done.49 = bf16[2,64,2048]{2,1,0:T(8,128)(2,1)S(1)} collective-permute-done((bf16[2,64,2048]{2,1,0:T(8,128)(2,1)}, bf16[2,64,2048]{2,1,0:T(8,128)(2,1)S(1)}, u32[]{:S(2)}, u32[]{:S(2)}) %collective-permute-start.49) | collective-permute-done | bytes 524320 | tf_op jit(solution)/shard_map/ppermute | solution.py:284
  441.9 6.9 %collective-permute-done.44 = bf16[2,64,2048]{2,1,0:T(8,128)(2,1)S(1)} collective-permute-done((bf16[2,64,2048]{2,1,0:T(8,128)(2,1)}, bf16[2,64,2048]{2,1,0:T(8,128)(2,1)S(1)}, u32[]{:S(2)}, u32[]{:S(2)}) %collective-permute-start.44) | collective-permute-done | bytes 524320 | tf_op jit(solution)/shard_map/ppermute | solution.py:284
  459.5 8.4 %collective-permute-done.46 = bf16[1,64,2048]{2,1,0:T(8,128)(2,1)S(1)} collective-permute-done((bf16[1,64,2048]{2,1,0:T(8,128)(2,1)S(1)}, bf16[1,64,2048]{2,1,0:T(8,128)(2,1)S(1)}, u32[]{:S(2)}, u32[]{:S(2)}) %collective-permute-start.46) | collective-permute-done | bytes 262176 | tf_op jit(solution)/shard_map/ppermute | solution.py:284
  502.7 5.0 collective-permute-done.65
  540.6 18.8 %collective-permute-start.74 = (f32[2,2048]{1,0:T(2,128)S(1)}, f32[2,2048]{1,0:T(2,128)S(1)}, u32[]{:S(2)}, u32[]{:S(2)}) collective-permute-start(f32[2,2048]{1,0:T(2,128)S(1)} %get-tuple-element.739), channel_id=1, source_target_pairs={{0,192},{64,0},{128,64},{192,128},{1,193},{65,1},{129,65},{193,129... | collective-permute-start | bytes 49160 | tf_op jit(solution)/shard_map/ppermute | solution.py:284
  (303 shorter events, 251.9 us)
Async XLA Ops:
  48.6 72.9 %collective-permute-start.11 = (bf16[4,48,2048]{2,1,0:T(8,128)(2,1)}, bf16[4,48,2048]{2,1,0:T(8,128)(2,1)}, u32[]{:S(2)}, u32[]{:S(2)}) collective-permute-start(bf16[4,48,2048]{2,1,0:T(8,128)(2,1)} %fusion.25), channel_id=1, source_target_pairs={{0,4},{4,8},{8,12},{12,32},{32,36},{36,40},{40,44},{44,0},{1,5},{5... | collective-permute-start | bytes 2359304 | tf_op jit(solution)/shard_map/ppermute | solution.py:284
  48.7 89.4 %collective-permute-start.21 = (bf16[4,48,2048]{2,1,0:T(8,128)(2,1)}, bf16[4,48,2048]{2,1,0:T(8,128)(2,1)}, u32[]{:S(2)}, u32[]{:S(2)}) collective-permute-start(bf16[4,48,2048]{2,1,0:T(8,128)(2,1)} %fusion.25), channel_id=1, source_target_pairs={{0,44},{4,0},{8,4},{12,8},{32,12},{36,32},{40,36},{44,40},{1,45},{... | collective-permute-start | bytes 2359304 | tf_op jit(solution)/shard_map/ppermute | solution.py:284
  52.4 146.3 %collective-permute-start.24 = (bf16[8,80,2048]{2,1,0:T(8,128)(2,1)S(1)}, bf16[8,80,2048]{2,1,0:T(8,128)(2,1)}, u32[]{:S(2)}, u32[]{:S(2)}) collective-permute-start(bf16[8,80,2048]{2,1,0:T(8,128)(2,1)S(1)} %bitcast_dynamic-update-slice_fusion.8), channel_id=1, source_target_pairs={{0,1},{1,2},{2,3},{3,0},{4,5},{5,6},{6,7},{7,4},{8,9},{9,10},{10,1... | collective-permute-start | bytes 7864328 | tf_op jit(solution)/shard_map/ppermute | solution.py:284
  53.2 147.0 %collective-permute-start.25 = (bf16[8,80,2048]{2,1,0:T(8,128)(2,1)S(1)}, bf16[8,80,2048]{2,1,0:T(8,128)(2,1)}, u32[]{:S(2)}, u32[]{:S(2)}) collective-permute-start(bf16[8,80,2048]{2,1,0:T(8,128)(2,1)S(1)} %bitcast_dynamic-update-slice_fusion.8), channel_id=1, source_target_pairs={{0,3},{1,0},{2,1},{3,2},{4,7},{5,4},{6,5},{7,6},{8,11},{9,8},{10,9... | collective-permute-start | bytes 7864328 | tf_op jit(solution)/shard_map/ppermute | solution.py:284
  63.2 44.0 %collective-permute-start.16 = (bf16[1,16,2048]{2,1,0:T(8,128)(2,1)S(1)}, bf16[1,16,2048]{2,1,0:T(8,128)(2,1)S(1)}, u32[]{:S(2)}, u32[]{:S(2)}) collective-permute-start(bf16[1,16,2048]{2,1,0:T(8,128)(2,1)S(1)} %bitcast.183), channel_id=1, source_target_pairs={{0,1},{1,2},{2,3},{3,0},{4,5},{5,6},{6,7},{7,4},{8,9},{9,10},{10,1... | collective-permute-start | bytes 196616 | tf_op jit(solution)/shard_map/ppermute | solution.py:284
  121.4 23.6 %collective-permute-start.12 = (bf16[4,48,2048]{2,1,0:T(8,128)(2,1)}, bf16[4,48,2048]{2,1,0:T(8,128)(2,1)S(1)}, u32[]{:S(2)}, u32[]{:S(2)}) collective-permute-start(bf16[4,48,2048]{2,1,0:T(8,128)(2,1)} %collective-permute-done.11), channel_id=1, source_target_pairs={{0,4},{4,8},{8,12},{12,32},{32,36},{36,40},{40,44},{44,0},{1,5},{5... | collective-permute-start | bytes 2359304 | tf_op jit(solution)/shard_map/ppermute | solution.py:284
  132.5 28.4 %collective-permute-start.19 = (bf16[8,16,2048]{2,1,0:T(8,128)(2,1)S(1)}, bf16[8,16,2048]{2,1,0:T(8,128)(2,1)S(1)}, u32[]{:S(2)}, u32[]{:S(2)}) collective-permute-start(bf16[8,16,2048]{2,1,0:T(8,128)(2,1)S(1)} %pad_maximum_fusion.2), channel_id=1, source_target_pairs={{0,8},{4,12},{8,0},{12,4},{1,9},{5,13},{9,1},{13,5},{2,10},{6,14},... | collective-permute-start | bytes 1572872 | tf_op jit(solution)/shard_map/ppermute | solution.py:284
  138.0 25.7 %collective-permute-start.22 = (bf16[4,48,2048]{2,1,0:T(8,128)(2,1)}, bf16[4,48,2048]{2,1,0:T(8,128)(2,1)S(1)}, u32[]{:S(2)}, u32[]{:S(2)}) collective-permute-start(bf16[4,48,2048]{2,1,0:T(8,128)(2,1)} %collective-permute-done.21), channel_id=1, source_target_pairs={{0,44},{4,0},{8,4},{12,8},{32,12},{36,32},{40,36},{44,40},{1,45},{... | collective-permute-start | bytes 2359304 | tf_op jit(solution)/shard_map/ppermute | solution.py:284
  145.1 27.0 %collective-permute-start.13 = (bf16[4,48,2048]{2,1,0:T(8,128)(2,1)S(1)}, bf16[4,48,2048]{2,1,0:T(8,128)(2,1)S(1)}, u32[]{:S(2)}, u32[]{:S(2)}) collective-permute-start(bf16[4,48,2048]{2,1,0:T(8,128)(2,1)S(1)} %collective-permute-done.12), channel_id=1, source_target_pairs={{0,4},{4,8},{8,12},{12,32},{32,36},{36,40},{40,44},{44,0},{1,5},{5... | collective-permute-start | bytes 2359304 | tf_op jit(solution)/shard_map/ppermute | solution.py:284
  163.8 34.0 %collective-permute-start.23 = (bf16[4,48,2048]{2,1,0:T(8,128)(2,1)S(1)}, bf16[4,48,2048]{2,1,0:T(8,128)(2,1)S(1)}, u32[]{:S(2)}, u32[]{:S(2)}) collective-permute-start(bf16[4,48,2048]{2,1,0:T(8,128)(2,1)S(1)} %collective-permute-done.22), channel_id=1, source_target_pairs={{0,44},{4,0},{8,4},{12,8},{32,12},{36,32},{40,36},{44,40},{1,45},{... | collective-permute-start | bytes 2359304 | tf_op jit(solution)/shard_map/ppermute | solution.py:284
  198.7 42.9 %collective-permute-start.28 = (bf16[8,4,48,2048]{3,2,1,0:T(8,128)(2,1)}, bf16[8,4,48,2048]{3,2,1,0:T(8,128)(2,1)}, u32[]{:S(2)}, u32[]{:S(2)}) collective-permute-start(bf16[8,4,48,2048]{3,2,1,0:T(8,128)(2,1)} %bitcast_dynamic-update-slice_fusion), channel_id=1, source_target_pairs={{0,16},{16,0},{1,17},{17,1},{2,18},{18,2},{3,19},{19,3},{4,20},{20... | collective-permute-start | bytes 18874376 | tf_op jit(solution)/shard_map/ppermute | solution.py:284
  200.2 32.5 %collective-permute-start.26 = (bf16[4,80,2048]{2,1,0:T(8,128)(2,1)S(1)}, bf16[4,80,2048]{2,1,0:T(8,128)(2,1)S(1)}, u32[]{:S(2)}, u32[]{:S(2)}) collective-permute-start(bf16[4,80,2048]{2,1,0:T(8,128)(2,1)S(1)} %slice.133), channel_id=1, source_target_pairs={{0,1},{1,2},{2,3},{3,0},{4,5},{5,6},{6,7},{7,4},{8,9},{9,10},{10,1... | collective-permute-start | bytes 3932168 | tf_op jit(solution)/shard_map/ppermute | solution.py:284
  201.7 32.1 %collective-permute-start.27 = (bf16[4,80,2048]{2,1,0:T(8,128)(2,1)S(1)}, bf16[4,80,2048]{2,1,0:T(8,128)(2,1)S(1)}, u32[]{:S(2)}, u32[]{:S(2)}) collective-permute-start(bf16[4,80,2048]{2,1,0:T(8,128)(2,1)S(1)} %slice.134), channel_id=1, source_target_pairs={{0,3},{1,0},{2,1},{3,2},{4,7},{5,4},{6,5},{7,6},{8,11},{9,8},{10,9... | collective-permute-start | bytes 3932168 | tf_op jit(solution)/shard_map/ppermute | solution.py:284
  205.0 30.6 %collective-permute-start.29 = (bf16[8,80,2048]{2,1,0:T(8,128)(2,1)S(1)}, bf16[8,80,2048]{2,1,0:T(8,128)(2,1)}, u32[]{:S(2)}, u32[]{:S(2)}) collective-permute-start(bf16[8,80,2048]{2,1,0:T(8,128)(2,1)S(1)} %bitcast_dynamic-update-slice_fusion.8), channel_id=1, source_target_pairs={{0,16},{16,0},{1,17},{17,1},{2,18},{18,2},{3,19},{19,3},{4,20},{20... | collective-permute-start | bytes 7864328 | tf_op jit(solution)/shard_map/ppermute | solution.py:284
  205.2 30.5 %collective-permute-start.30 = (bf16[8,80,2048]{2,1,0:T(8,128)(2,1)}, bf16[8,80,2048]{2,1,0:T(8,128)(2,1)}, u32[]{:S(2)}, u32[]{:S(2)}) collective-permute-start(bf16[8,80,2048]{2,1,0:T(8,128)(2,1)} %collective-permute-done.24), channel_id=1, source_target_pairs={{0,16},{16,0},{1,17},{17,1},{2,18},{18,2},{3,19},{19,3},{4,20},{20... | collective-permute-start | bytes 7864328 | tf_op jit(solution)/shard_map/ppermute | solution.py:284
  327.3 60.2 %collective-permute-start.37 = (bf16[64,2048]{1,0:T(8,128)(2,1)}, bf16[64,2048]{1,0:T(8,128)(2,1)}, u32[]{:S(2)}, u32[]{:S(2)}) collective-permute-start(bf16[64,2048]{1,0:T(8,128)(2,1)} %get-tuple-element.666), channel_id=1, source_target_pairs={{64,0},{128,64},{192,128},{65,1},{129,65},{193,129},{66,2},{130,66... | collective-permute-start | bytes 786440 | tf_op jit(solution)/shard_map/ppermute | solution.py:289
  331.3 76.9 %collective-permute-start.40 = (bf16[2,2,64,512]{3,2,1,0:T(8,128)(2,1)}, bf16[2,2,64,512]{3,2,1,0:T(8,128)(2,1)}, u32[]{:S(2)}, u32[]{:S(2)}) collective-permute-start(bf16[2,2,64,512]{3,2,1,0:T(8,128)(2,1)} %get-tuple-element.716), channel_id=1, source_target_pairs={{0,1},{1,2},{2,3},{3,0},{4,5},{5,6},{6,7},{7,4},{8,9},{9,10},{10,1... | collective-permute-start | bytes 786440 | tf_op jit(solution)/shard_map/ppermute | solution.py:284
  331.3 76.9 %collective-permute-start.41 = (bf16[2,2,64,512]{3,2,1,0:T(8,128)(2,1)}, bf16[2,2,64,512]{3,2,1,0:T(8,128)(2,1)}, u32[]{:S(2)}, u32[]{:S(2)}) collective-permute-start(bf16[2,2,64,512]{3,2,1,0:T(8,128)(2,1)} %get-tuple-element.717), channel_id=1, source_target_pairs={{0,3},{1,0},{2,1},{3,2},{4,7},{5,4},{6,5},{7,6},{8,11},{9,8},{10,9... | collective-permute-start | bytes 786440 | tf_op jit(solution)/shard_map/ppermute | solution.py:284
  334.6 73.6 %collective-permute-start.42 = (bf16[2,2,64,512]{3,2,1,0:T(8,128)(2,1)}, bf16[2,2,64,512]{3,2,1,0:T(8,128)(2,1)}, u32[]{:S(2)}, u32[]{:S(2)}) collective-permute-start(bf16[2,2,64,512]{3,2,1,0:T(8,128)(2,1)} %get-tuple-element.718), channel_id=1, source_target_pairs={{0,2},{1,3},{2,0},{3,1},{4,6},{5,7},{6,4},{7,5},{8,10},{9,11},{10,... | collective-permute-start | bytes 786440 | tf_op jit(solution)/shard_map/ppermute | solution.py:284
  334.8 73.2 %collective-permute-start.43 = (bf16[64,256]{0,1:T(8,128)(2,1)S(1)}, bf16[64,256]{0,1:T(8,128)(2,1)S(1)}, u32[]{:S(2)}, u32[]{:S(2)}) collective-permute-start(bf16[64,256]{0,1:T(8,128)(2,1)S(1)} %fusion.28), channel_id=1, source_target_pairs={{0,16},{16,0},{1,17},{17,1},{2,18},{18,2},{3,19},{19,3},{4,20},{20... | collective-permute-start | bytes 98312 | tf_op jit(solution)/shard_map/ppermute | solution.py:284
  424.6 24.2 %collective-permute-start.44 = (bf16[2,64,2048]{2,1,0:T(8,128)(2,1)}, bf16[2,64,2048]{2,1,0:T(8,128)(2,1)S(1)}, u32[]{:S(2)}, u32[]{:S(2)}) collective-permute-start(bf16[2,64,2048]{2,1,0:T(8,128)(2,1)} %get-tuple-element.678), channel_id=1, source_target_pairs={{0,1},{1,2},{2,3},{3,0},{4,5},{5,6},{6,7},{7,4},{8,9},{9,10},{10,1... | collective-permute-start | bytes 1572872 | tf_op jit(solution)/shard_map/ppermute | solution.py:284
  424.6 25.2 %collective-permute-start.45 = (bf16[2,64,2048]{2,1,0:T(8,128)(2,1)}, bf16[2,64,2048]{2,1,0:T(8,128)(2,1)S(1)}, u32[]{:S(2)}, u32[]{:S(2)}) collective-permute-start(bf16[2,64,2048]{2,1,0:T(8,128)(2,1)} %get-tuple-element.678), channel_id=1, source_target_pairs={{0,3},{1,0},{2,1},{3,2},{4,7},{5,4},{6,5},{7,6},{8,11},{9,8},{10,9... | collective-permute-start | bytes 1572872 | tf_op jit(solution)/shard_map/ppermute | solution.py:284
  441.9 29.9 %collective-permute-start.55 = (bf16[48,2048]{1,0:T(8,128)(2,1)}, bf16[48,2048]{1,0:T(8,128)(2,1)}, u32[]{:S(2)}, u32[]{:S(2)}) collective-permute-start(bf16[48,2048]{1,0:T(8,128)(2,1)} %get-tuple-element.729), channel_id=1, source_target_pairs={{0,1},{1,2},{2,3},{3,0},{4,5},{5,6},{6,7},{7,4},{8,9},{9,10},{10,1... | collective-permute-start | bytes 589832 | tf_op jit(solution)/shard_map/ppermute | solution.py:284
  448.8 23.0 %collective-permute-start.56 = (bf16[48,2048]{1,0:T(8,128)(2,1)}, bf16[48,2048]{1,0:T(8,128)(2,1)}, u32[]{:S(2)}, u32[]{:S(2)}) collective-permute-start(bf16[48,2048]{1,0:T(8,128)(2,1)} %get-tuple-element.730), channel_id=1, source_target_pairs={{0,3},{1,0},{2,1},{3,2},{4,7},{5,4},{6,5},{7,6},{8,11},{9,8},{10,9... | collective-permute-start | bytes 589832 | tf_op jit(solution)/shard_map/ppermute | solution.py:284
  (68 other events, 796.6 us)

commit v3 on v2

--- a/solution.py
+++ b/solution.py
@@ -328,7 +328,7 @@
     column = jnp.zeros((nz, rows - cut, features), BF)
     for steps, piece in ring_spread(own_rows[cut:], ("zh", "zl"), nz // 2 - 1)[0]:
         column = lax.dynamic_update_slice(column, piece[None], ((iz - steps) % nz, 0, 0))
-    line, column, small_inputs = lax.optimization_barrier((line, column, small_inputs))
+    line, column = lax.optimization_barrier((line, column))
     top = jnp.zeros((nz, nx, cut, features), BF)
     spread, smalls = ring_spread(line, ("zh", "zl"), nz // 2, small(*small_inputs))
     for steps, piece in spread:
@@ -359,10 +359,11 @@
     def small(embedding, gain_row):
         gain_pair = in_order(gain_row, turn(gain_row, "c", 1), ic)
         gains = in_order(gain_pair, turn(gain_pair, "zh", 1), izh).reshape(layers, features)
-        ring = embedding[None]
+        ring, step = embedding[None], 0
         for axis, count in (("x", nx), ("zl", nzl)):
             reach = 1
             while reach < count:
+                step += 1
                 ring = jnp.concatenate([ring, turn(ring, axis, reach)])
                 reach *= 2
         from_zl = (izl - jnp.arange(nzl)) % nzl

time: 575 us -> 532 us (0.925)
  the two profiles are of different devices: /device:TPU:8 before, /device:TPU:6 now
where the time goes in v3:
time: 532 us; the launch traced here: 523 us
  waiting for transfers between devices  263 us (49%)
  starting transfers between devices  141 us (27%)
  local copies, waits for them, and re-layouts  51.3 us (10%)
  Pallas kernels  42.9 us (8%)
  other arithmetic  19.1 us (4%)
    ppermute x69, waiting for transfers between devices, turn(): lax.ppermute(value, axis, [(i, (i + steps) % count) for i in range(count)])  152 us
    ppermute x69, starting transfers between devices, turn(): lax.ppermute(value, axis, [(i, (i + steps) % count) for i in range(count)])  113 us
    ppermute x6, waiting for transfers between devices, shift(): lax.ppermute(value, axis, [(i, i + steps) for i in range(count) if 0 <= i...  112 us
    ppermute x6, starting transfers between devices, shift(): lax.ppermute(value, axis, [(i, i + steps) for i in range(count) if 0 <= i...  28.2 us
    pallas_call x2, Pallas kernels, backward_stage(): pl.pallas_call(functools.partial(backward_kernel, first=first), grid=(1,)...  19.9 us
    pallas_call x1, Pallas kernels, forward_stage(): pl.pallas_call(forward_kernel, in_specs=[SM, VM, VM] + [HB] * len(stores)...  13.7 us
  transfers between devices with their start and end apart: 75, of which 33 were waited for; matrix products, arithmetic and copies ran while one was open for 11% of the time, Pallas kernels for 1%

profile of v3, /device:TPU:6, one launch (start us, length us, event | category | flops | bytes accessed | tf_op | source)
XLA Modules:
  0.0 522.5 jit_solution(16948331397964918888)
XLA Ops:
  20.6 5.4 %collective-permute-done.17 = bf16[2,16,2048]{2,1,0:T(8,128)(2,1)S(1)} collective-permute-done((bf16[2,16,2048]{2,1,0:T(8,128)(2,1)S(1)}, bf16[2,16,2048]{2,1,0:T(8,128)(2,1)S(1)}, u32[]{:S(2)}, u32[]{:S(2)}) %collective-permute-start.17) | collective-permute-done | bytes 131104 | tf_op jit(solution)/shard_map/ppermute | solution.py:284
  47.9 8.2 %collective-permute-done.9 = bf16[80,2048]{1,0:T(8,128)(2,1)S(1)} collective-permute-done((bf16[80,2048]{1,0:T(8,128)(2,1)S(1)}, bf16[80,2048]{1,0:T(8,128)(2,1)S(1)}, u32[]{:S(2)}, u32[]{:S(2)}) %collective-permute-start.9) | collective-permute-done | bytes 327712 | tf_op jit(solution)/shard_map/ppermute | solution.py:284
  58.4 6.1 %collective-permute-done.10 = bf16[80,2048]{1,0:T(8,128)(2,1)S(1)} collective-permute-done((bf16[80,2048]{1,0:T(8,128)(2,1)S(1)}, bf16[80,2048]{1,0:T(8,128)(2,1)S(1)}, u32[]{:S(2)}, u32[]{:S(2)}) %collective-permute-start.10) | collective-permute-done | bytes 327712 | tf_op jit(solution)/shard_map/ppermute | solution.py:284
  69.9 13.1 %collective-permute-done.11 = bf16[4,48,2048]{2,1,0:T(8,128)(2,1)} collective-permute-done((bf16[4,48,2048]{2,1,0:T(8,128)(2,1)}, bf16[4,48,2048]{2,1,0:T(8,128)(2,1)}, u32[]{:S(2)}, u32[]{:S(2)}) %collective-permute-start.11) | collective-permute-done | bytes 786464 | tf_op jit(solution)/shard_map/ppermute | solution.py:284
  83.0 11.9 %collective-permute-start.12 = (bf16[4,48,2048]{2,1,0:T(8,128)(2,1)}, bf16[4,48,2048]{2,1,0:T(8,128)(2,1)S(1)}, u32[]{:S(2)}, u32[]{:S(2)}) collective-permute-start(bf16[4,48,2048]{2,1,0:T(8,128)(2,1)} %collective-permute-done.11), channel_id=1, source_target_pairs={{0,4},{4,8},{8,12},{12,32},{32,36},{36,40},{40,44},{44,0},{1,5},{5... | collective-permute-start | bytes 2359304 | tf_op jit(solution)/shard_map/ppermute | solution.py:284
  101.2 13.8 %collective-permute-start.22 = (bf16[4,48,2048]{2,1,0:T(8,128)(2,1)S(1)}, bf16[4,48,2048]{2,1,0:T(8,128)(2,1)S(1)}, u32[]{:S(2)}, u32[]{:S(2)}) collective-permute-start(bf16[4,48,2048]{2,1,0:T(8,128)(2,1)S(1)} %collective-permute-done.21), channel_id=1, source_target_pairs={{0,44},{4,0},{8,4},{12,8},{32,12},{36,32},{40,36},{44,40},{1,45},{... | collective-permute-start | bytes 2359304 | tf_op jit(solution)/shard_map/ppermute | solution.py:284
  115.0 5.8 %collective-permute-start.13 = (bf16[4,48,2048]{2,1,0:T(8,128)(2,1)S(1)}, bf16[4,48,2048]{2,1,0:T(8,128)(2,1)S(1)}, u32[]{:S(2)}, u32[]{:S(2)}) collective-permute-start(bf16[4,48,2048]{2,1,0:T(8,128)(2,1)S(1)} %collective-permute-done.12), channel_id=1, source_target_pairs={{0,4},{4,8},{8,12},{12,32},{32,36},{36,40},{40,44},{44,0},{1,5},{5... | collective-permute-start | bytes 2359304 | tf_op jit(solution)/shard_map/ppermute | solution.py:284
  128.6 5.5 %collective-permute-done.13 = bf16[4,48,2048]{2,1,0:T(8,128)(2,1)S(1)} collective-permute-done((bf16[4,48,2048]{2,1,0:T(8,128)(2,1)S(1)}, bf16[4,48,2048]{2,1,0:T(8,128)(2,1)S(1)}, u32[]{:S(2)}, u32[]{:S(2)}) %collective-permute-start.13) | collective-permute-done | bytes 786464 | tf_op jit(solution)/shard_map/ppermute | solution.py:284
  140.2 9.8 %collective-permute-done.20 = bf16[4,48,2048]{2,1,0:T(8,128)(2,1)S(1)} collective-permute-done((bf16[4,48,2048]{2,1,0:T(8,128)(2,1)S(1)}, bf16[4,48,2048]{2,1,0:T(8,128)(2,1)S(1)}, u32[]{:S(2)}, u32[]{:S(2)}) %collective-permute-start.20) | collective-permute-done | bytes 786464 | tf_op jit(solution)/shard_map/ppermute | solution.py:284
  159.7 26.9 %collective-permute-done.26 = bf16[4,80,2048]{2,1,0:T(8,128)(2,1)S(1)} collective-permute-done((bf16[4,80,2048]{2,1,0:T(8,128)(2,1)S(1)}, bf16[4,80,2048]{2,1,0:T(8,128)(2,1)S(1)}, u32[]{:S(2)}, u32[]{:S(2)}) %collective-permute-start.26) | collective-permute-done | bytes 1310752 | tf_op jit(solution)/shard_map/ppermute | solution.py:284
  197.5 13.7 %conditional.10 = ((bf16[4,64,2048]{2,1,0:T(8,128)(2,1)}, bf16[4,4,64,512]{3,2,1,0:T(8,128)(2,1)}, f32[4,64,2048]{2,1,0:T(8,128)}, f32[4,64,128]{2,1,0:T(8,128)S(1)}, bf16[64,2048]{1,0:T(8,128)(2,1)S(1)})) conditional(s32[]{:T(128)} %convert_element_type.204, bf16[64,2048]{1,0:T(8,128)(2,1)S(1)} %convolution_convert_fusion.2, (s32[2]{0:T(128)S(1)}, ...), branch_computations={%region_0.1_spmd, %region_1.2_spmd} | conditional | bytes 4849724 | solution.py:388
  197.5 13.7 %forward_stage.4 = (bf16[4,64,2048]{2,1,0:T(8,128)(2,1)}, bf16[4,4,64,512]{3,2,1,0:T(8,128)(2,1)}, f32[4,64,2048]{2,1,0:T(8,128)}, f32[4,64,128]{2,1,0:T(8,128)S(1)}, bf16[64,2048]{1,0:T(8,128)(2,1)S(1)}) custom-call(s32[2]{0:T(128)S(1)} %get-tuple-element.441.pos, bf16[64,2048]{1,0:T(8,128)(2,1)S(1)} %get-tuple-element.442.x_ref, ...), custom_call_target="tpu_custom_call" | custom-call | tf_op jit(solution)/shard_map/cond/branch_1_fun/forward_stage/pallas_call | solution.py:203
  212.6 6.5 %collective-permute-done.33 = bf16[64,2048]{1,0:T(8,128)(2,1)S(1)} collective-permute-done((bf16[64,2048]{1,0:T(8,128)(2,1)S(1)}, bf16[64,2048]{1,0:T(8,128)(2,1)S(1)}, u32[]{:S(2)}, u32[]{:S(2)}) %collective-permute-start.33) | collective-permute-done | bytes 262176 | tf_op jit(solution)/shard_map/ppermute | solution.py:289
  219.1 18.2 %collective-permute-start.34 = (bf16[64,2048]{1,0:T(8,128)(2,1)S(1)}, bf16[64,2048]{1,0:T(8,128)(2,1)S(1)}, u32[]{:S(2)}, u32[]{:S(2)}) collective-permute-start(bf16[64,2048]{1,0:T(8,128)(2,1)S(1)} %get-tuple-element.646), channel_id=1, source_target_pairs={{0,64},{64,128},{128,192},{1,65},{65,129},{129,193},{2,66},{66,130... | collective-permute-start | bytes 786440 | tf_op jit(solution)/shard_map/ppermute | solution.py:289
  237.2 6.0 %collective-permute-done.34 = bf16[64,2048]{1,0:T(8,128)(2,1)S(1)} collective-permute-done((bf16[64,2048]{1,0:T(8,128)(2,1)S(1)}, bf16[64,2048]{1,0:T(8,128)(2,1)S(1)}, u32[]{:S(2)}, u32[]{:S(2)}) %collective-permute-start.34) | collective-permute-done | bytes 262176 | tf_op jit(solution)/shard_map/ppermute | solution.py:289
  259.7 22.6 %collective-permute-done.36 = bf16[64,2048]{1,0:T(8,128)(2,1)} collective-permute-done((bf16[64,2048]{1,0:T(8,128)(2,1)}, bf16[64,2048]{1,0:T(8,128)(2,1)}, u32[]{:S(2)}, u32[]{:S(2)}) %collective-permute-start.36) | collective-permute-done | bytes 262176 | tf_op jit(solution)/shard_map/ppermute | solution.py:289
  295.4 6.6 %collective-permute-done.41 = bf16[2,2,64,512]{3,2,1,0:T(8,128)(2,1)} collective-permute-done((bf16[2,2,64,512]{3,2,1,0:T(8,128)(2,1)}, bf16[2,2,64,512]{3,2,1,0:T(8,128)(2,1)}, u32[]{:S(2)}, u32[]{:S(2)}) %collective-permute-start.41) | collective-permute-done | bytes 262176 | tf_op jit(solution)/shard_map/ppermute | solution.py:284
  304.3 66.6 %collective-permute-done.38 = bf16[64,2048]{1,0:T(8,128)(2,1)S(1)} collective-permute-done((bf16[64,2048]{1,0:T(8,128)(2,1)}, bf16[64,2048]{1,0:T(8,128)(2,1)S(1)}, u32[]{:S(2)}, u32[]{:S(2)}) %collective-permute-start.38) | collective-permute-done | bytes 262176 | tf_op jit(solution)/shard_map/ppermute | solution.py:289
  370.9 12.1 %conditional.18 = (bf16[2,64,2048]{2,1,0:T(8,128)(2,1)}, bf16[64,2048]{1,0:T(8,128)(2,1)S(1)}, bf16[1,2,64,2048]{3,2,1,0:T(8,128)(2,1)S(1)}, f32[1,2,2048]{2,1,0:T(2,128)S(1)}) conditional(s32[]{:T(128)} %convert_element_type.204, (bf16[4,64,2048]{2,1,0:T(8,128)(2,1)S(1)}, f32[4,2048]{1,0:T(4,128)S(1)}, ...), branch_computations={%region_16.17_spmd, %region_17.18_spmd} | conditional | bytes 2129952 | solution.py:412
  371.6 10.3 %backward_stage.12 = (bf16[2,64,2048]{2,1,0:T(8,128)(2,1)}, f32[2,2048]{1,0:T(2,128)S(1)}, bf16[64,2048]{1,0:T(8,128)(2,1)S(1)}) custom-call(s32[2]{0:T(128)S(1)} %get-tuple-element.552.pos, bf16[64,2048]{1,0:T(8,128)(2,1)} %copy.148.grad_ref, f32[4,2048]{1,0:T(4,128)S(1)} %get-tuple-element.554.gain_ref, bf16[4,64,2048]{2,1,0:T(8,128)(2,1)} %get-tuple-element.555.xs_ref, ...), custom_call_target="tpu_custom_call" | custom-call | tf_op jit(solution)/shard_map/cond/branch_1_fun/backward_stage/pallas_call | solution.py:230
  383.8 11.4 %conditional.19 = (bf16[2,64,2048]{2,1,0:T(8,128)(2,1)}, bf16[64,2048]{1,0:T(8,128)(2,1)S(1)}, bf16[1,2,64,2048]{3,2,1,0:T(8,128)(2,1)S(1)}, f32[1,2,2048]{2,1,0:T(2,128)S(1)}) conditional(s32[]{:T(128)} %convert_element_type.204, (bf16[4,64,2048]{2,1,0:T(8,128)(2,1)}, f32[4,2048]{1,0:T(4,128)S(1)}, bf16[64,2048]{1,0:T(8,128)(2,1)S(1)}) %tuple.140, ...), branch_computations={%region_18.19_spmd, %region_19.20_spmd} | conditional | bytes 2129952 | solution.py:412
  384.5 9.6 %backward_stage.13 = (bf16[2,64,2048]{2,1,0:T(8,128)(2,1)}, f32[2,2048]{1,0:T(2,128)S(1)}, bf16[64,2048]{1,0:T(8,128)(2,1)S(1)}) custom-call(s32[2]{0:T(128)S(1)} %get-tuple-element.574.pos, bf16[64,2048]{1,0:T(8,128)(2,1)} %copy.149.grad_ref, f32[4,2048]{1,0:T(4,128)S(1)} %get-tuple-element.576.gain_ref, bf16[4,64,2048]{2,1,0:T(8,128)(2,1)} %get-tuple-element.577.xs_ref, ...), custom_call_target="tpu_custom_call" | custom-call | tf_op jit(solution)/shard_map/cond/branch_1_fun/backward_stage/pallas_call | solution.py:230
  400.5 10.1 %collective-permute-done.49 = bf16[2,64,2048]{2,1,0:T(8,128)(2,1)S(1)} collective-permute-done((bf16[2,64,2048]{2,1,0:T(8,128)(2,1)}, bf16[2,64,2048]{2,1,0:T(8,128)(2,1)S(1)}, u32[]{:S(2)}, u32[]{:S(2)}) %collective-permute-start.49) | collective-permute-done | bytes 524320 | tf_op jit(solution)/shard_map/ppermute | solution.py:284
  431.7 9.2 %collective-permute-done.46 = bf16[1,64,2048]{2,1,0:T(8,128)(2,1)S(1)} collective-permute-done((bf16[1,64,2048]{2,1,0:T(8,128)(2,1)S(1)}, bf16[1,64,2048]{2,1,0:T(8,128)(2,1)S(1)}, u32[]{:S(2)}, u32[]{:S(2)}) %collective-permute-start.46) | collective-permute-done | bytes 262176 | tf_op jit(solution)/shard_map/ppermute | solution.py:284
  (297 shorter events, 237.3 us)
Async XLA Ops:
  2.6 33.1 %collective-permute-start.4 = (bf16[80,2048]{1,0:T(8,128)(2,1)}, bf16[80,2048]{1,0:T(8,128)(2,1)}, u32[]{:S(2)}, u32[]{:S(2)}) collective-permute-start(bf16[80,2048]{1,0:T(8,128)(2,1)} %get-tuple-element.721), channel_id=1, source_target_pairs={{0,4},{4,8},{8,12},{12,32},{32,36},{36,40},{40,44},{44,0},{1,5},{5... | collective-permute-start | bytes 983048 | tf_op jit(solution)/shard_map/ppermute | solution.py:284
  4.5 31.2 %collective-permute-start.7 = (bf16[80,2048]{1,0:T(8,128)(2,1)}, bf16[80,2048]{1,0:T(8,128)(2,1)}, u32[]{:S(2)}, u32[]{:S(2)}) collective-permute-start(bf16[80,2048]{1,0:T(8,128)(2,1)} %get-tuple-element.721), channel_id=1, source_target_pairs={{0,44},{4,0},{8,4},{12,8},{32,12},{36,32},{40,36},{44,40},{1,45},{... | collective-permute-start | bytes 983048 | tf_op jit(solution)/shard_map/ppermute | solution.py:284
  26.0 38.6 %collective-permute-start.15 = (f32[2,2048]{1,0:T(2,128)S(1)}, f32[2,2048]{1,0:T(2,128)S(1)}, u32[]{:S(2)}, u32[]{:S(2)}) collective-permute-start(f32[2,2048]{1,0:T(2,128)S(1)} %maximum_select_fusion.2), channel_id=1, source_target_pairs={{0,32},{32,0},{1,33},{33,1},{2,34},{34,2},{3,35},{35,3},{4,36},{36... | collective-permute-start | bytes 49160 | tf_op jit(solution)/shard_map/ppermute | solution.py:284
  39.9 24.8 %collective-permute-start.18 = (bf16[4,16,2048]{2,1,0:T(8,128)(2,1)}, bf16[4,16,2048]{2,1,0:T(8,128)(2,1)S(1)}, u32[]{:S(2)}, u32[]{:S(2)}) collective-permute-start(bf16[4,16,2048]{2,1,0:T(8,128)(2,1)} %pad_maximum_fusion.8), channel_id=1, source_target_pairs={{0,4},{4,8},{8,12},{12,0},{1,5},{5,9},{9,13},{13,1},{2,6},{6,10},{... | collective-permute-start | bytes 786440 | tf_op jit(solution)/shard_map/ppermute | solution.py:284
  64.8 30.9 %collective-permute-start.19 = (bf16[8,16,2048]{2,1,0:T(8,128)(2,1)S(1)}, bf16[8,16,2048]{2,1,0:T(8,128)(2,1)S(1)}, u32[]{:S(2)}, u32[]{:S(2)}) collective-permute-start(bf16[8,16,2048]{2,1,0:T(8,128)(2,1)S(1)} %pad_maximum_fusion.2), channel_id=1, source_target_pairs={{0,8},{4,12},{8,0},{12,4},{1,9},{5,13},{9,1},{13,5},{2,10},{6,14},... | collective-permute-start | bytes 1572872 | tf_op jit(solution)/shard_map/ppermute | solution.py:284
  67.8 33.4 %collective-permute-start.21 = (bf16[4,48,2048]{2,1,0:T(8,128)(2,1)}, bf16[4,48,2048]{2,1,0:T(8,128)(2,1)S(1)}, u32[]{:S(2)}, u32[]{:S(2)}) collective-permute-start(bf16[4,48,2048]{2,1,0:T(8,128)(2,1)} %fusion.25), channel_id=1, source_target_pairs={{0,44},{4,0},{8,4},{12,8},{32,12},{36,32},{40,36},{44,40},{1,45},{... | collective-permute-start | bytes 2359304 | tf_op jit(solution)/shard_map/ppermute | solution.py:284
  83.0 31.9 %collective-permute-start.12 = (bf16[4,48,2048]{2,1,0:T(8,128)(2,1)}, bf16[4,48,2048]{2,1,0:T(8,128)(2,1)S(1)}, u32[]{:S(2)}, u32[]{:S(2)}) collective-permute-start(bf16[4,48,2048]{2,1,0:T(8,128)(2,1)} %collective-permute-done.11), channel_id=1, source_target_pairs={{0,4},{4,8},{8,12},{12,32},{32,36},{36,40},{40,44},{44,0},{1,5},{5... | collective-permute-start | bytes 2359304 | tf_op jit(solution)/shard_map/ppermute | solution.py:284
  99.2 54.7 %collective-permute-start.24 = (bf16[8,80,2048]{2,1,0:T(8,128)(2,1)S(1)}, bf16[8,80,2048]{2,1,0:T(8,128)(2,1)}, u32[]{:S(2)}, u32[]{:S(2)}) collective-permute-start(bf16[8,80,2048]{2,1,0:T(8,128)(2,1)S(1)} %bitcast_dynamic-update-slice_fusion.8), channel_id=1, source_target_pairs={{0,1},{1,2},{2,3},{3,0},{4,5},{5,6},{6,7},{7,4},{8,9},{9,10},{10,1... | collective-permute-start | bytes 7864328 | tf_op jit(solution)/shard_map/ppermute | solution.py:284
  100.8 56.6 %collective-permute-start.25 = (bf16[8,80,2048]{2,1,0:T(8,128)(2,1)S(1)}, bf16[8,80,2048]{2,1,0:T(8,128)(2,1)}, u32[]{:S(2)}, u32[]{:S(2)}) collective-permute-start(bf16[8,80,2048]{2,1,0:T(8,128)(2,1)S(1)} %bitcast_dynamic-update-slice_fusion.8), channel_id=1, source_target_pairs={{0,3},{1,0},{2,1},{3,2},{4,7},{5,4},{6,5},{7,6},{8,11},{9,8},{10,9... | collective-permute-start | bytes 7864328 | tf_op jit(solution)/shard_map/ppermute | solution.py:284
  101.2 27.4 %collective-permute-start.22 = (bf16[4,48,2048]{2,1,0:T(8,128)(2,1)S(1)}, bf16[4,48,2048]{2,1,0:T(8,128)(2,1)S(1)}, u32[]{:S(2)}, u32[]{:S(2)}) collective-permute-start(bf16[4,48,2048]{2,1,0:T(8,128)(2,1)S(1)} %collective-permute-done.21), channel_id=1, source_target_pairs={{0,44},{4,0},{8,4},{12,8},{32,12},{36,32},{40,36},{44,40},{1,45},{... | collective-permute-start | bytes 2359304 | tf_op jit(solution)/shard_map/ppermute | solution.py:284
  128.6 24.3 %collective-permute-start.23 = (bf16[4,48,2048]{2,1,0:T(8,128)(2,1)S(1)}, bf16[4,48,2048]{2,1,0:T(8,128)(2,1)S(1)}, u32[]{:S(2)}, u32[]{:S(2)}) collective-permute-start(bf16[4,48,2048]{2,1,0:T(8,128)(2,1)S(1)} %collective-permute-done.22), channel_id=1, source_target_pairs={{0,44},{4,0},{8,4},{12,8},{32,12},{36,32},{40,36},{44,40},{1,45},{... | collective-permute-start | bytes 2359304 | tf_op jit(solution)/shard_map/ppermute | solution.py:284
  153.9 43.7 %collective-permute-start.28 = (bf16[8,4,48,2048]{3,2,1,0:T(8,128)(2,1)}, bf16[8,4,48,2048]{3,2,1,0:T(8,128)(2,1)}, u32[]{:S(2)}, u32[]{:S(2)}) collective-permute-start(bf16[8,4,48,2048]{3,2,1,0:T(8,128)(2,1)} %bitcast_dynamic-update-slice_fusion), channel_id=1, source_target_pairs={{0,16},{16,0},{1,17},{17,1},{2,18},{18,2},{3,19},{19,3},{4,20},{20... | collective-permute-start | bytes 18874376 | tf_op jit(solution)/shard_map/ppermute | solution.py:284
  155.3 31.3 %collective-permute-start.26 = (bf16[4,80,2048]{2,1,0:T(8,128)(2,1)S(1)}, bf16[4,80,2048]{2,1,0:T(8,128)(2,1)S(1)}, u32[]{:S(2)}, u32[]{:S(2)}) collective-permute-start(bf16[4,80,2048]{2,1,0:T(8,128)(2,1)S(1)} %slice.133), channel_id=1, source_target_pairs={{0,1},{1,2},{2,3},{3,0},{4,5},{5,6},{6,7},{7,4},{8,9},{9,10},{10,1... | collective-permute-start | bytes 3932168 | tf_op jit(solution)/shard_map/ppermute | solution.py:284
  158.9 32.2 %collective-permute-start.27 = (bf16[4,80,2048]{2,1,0:T(8,128)(2,1)S(1)}, bf16[4,80,2048]{2,1,0:T(8,128)(2,1)S(1)}, u32[]{:S(2)}, u32[]{:S(2)}) collective-permute-start(bf16[4,80,2048]{2,1,0:T(8,128)(2,1)S(1)} %slice.134), channel_id=1, source_target_pairs={{0,3},{1,0},{2,1},{3,2},{4,7},{5,4},{6,5},{7,6},{8,11},{9,8},{10,9... | collective-permute-start | bytes 3932168 | tf_op jit(solution)/shard_map/ppermute | solution.py:284
  159.0 33.4 %collective-permute-start.29 = (bf16[8,80,2048]{2,1,0:T(8,128)(2,1)S(1)}, bf16[8,80,2048]{2,1,0:T(8,128)(2,1)}, u32[]{:S(2)}, u32[]{:S(2)}) collective-permute-start(bf16[8,80,2048]{2,1,0:T(8,128)(2,1)S(1)} %bitcast_dynamic-update-slice_fusion.8), channel_id=1, source_target_pairs={{0,16},{16,0},{1,17},{17,1},{2,18},{18,2},{3,19},{19,3},{4,20},{20... | collective-permute-start | bytes 7864328 | tf_op jit(solution)/shard_map/ppermute | solution.py:284
  159.3 33.1 %collective-permute-start.30 = (bf16[8,80,2048]{2,1,0:T(8,128)(2,1)}, bf16[8,80,2048]{2,1,0:T(8,128)(2,1)}, u32[]{:S(2)}, u32[]{:S(2)}) collective-permute-start(bf16[8,80,2048]{2,1,0:T(8,128)(2,1)} %collective-permute-done.24), channel_id=1, source_target_pairs={{0,16},{16,0},{1,17},{17,1},{2,18},{18,2},{3,19},{19,3},{4,20},{20... | collective-permute-start | bytes 7864328 | tf_op jit(solution)/shard_map/ppermute | solution.py:284
  219.1 24.1 %collective-permute-start.34 = (bf16[64,2048]{1,0:T(8,128)(2,1)S(1)}, bf16[64,2048]{1,0:T(8,128)(2,1)S(1)}, u32[]{:S(2)}, u32[]{:S(2)}) collective-permute-start(bf16[64,2048]{1,0:T(8,128)(2,1)S(1)} %get-tuple-element.646), channel_id=1, source_target_pairs={{0,64},{64,128},{128,192},{1,65},{65,129},{129,193},{2,66},{66,130... | collective-permute-start | bytes 786440 | tf_op jit(solution)/shard_map/ppermute | solution.py:289
  258.4 25.2 %collective-permute-start.39 = (bf16[4,2,64,512]{3,2,1,0:T(8,128)(2,1)}, bf16[4,2,64,512]{3,2,1,0:T(8,128)(2,1)}, u32[]{:S(2)}, u32[]{:S(2)}) collective-permute-start(bf16[4,2,64,512]{3,2,1,0:T(8,128)(2,1)} %get-tuple-element.715), channel_id=1, source_target_pairs={{0,16},{16,0},{1,17},{17,1},{2,18},{18,2},{3,19},{19,3},{4,20},{20... | collective-permute-start | bytes 1572872 | tf_op jit(solution)/shard_map/ppermute | solution.py:284
  258.4 23.9 %collective-permute-start.36 = (bf16[64,2048]{1,0:T(8,128)(2,1)}, bf16[64,2048]{1,0:T(8,128)(2,1)}, u32[]{:S(2)}, u32[]{:S(2)}) collective-permute-start(bf16[64,2048]{1,0:T(8,128)(2,1)} %get-tuple-element.661), channel_id=1, source_target_pairs={{64,0},{128,64},{192,128},{65,1},{129,65},{193,129},{66,2},{130,66... | collective-permute-start | bytes 786440 | tf_op jit(solution)/shard_map/ppermute | solution.py:289
  293.4 77.6 %collective-permute-start.38 = (bf16[64,2048]{1,0:T(8,128)(2,1)}, bf16[64,2048]{1,0:T(8,128)(2,1)S(1)}, u32[]{:S(2)}, u32[]{:S(2)}) collective-permute-start(bf16[64,2048]{1,0:T(8,128)(2,1)} %get-tuple-element.665), channel_id=1, source_target_pairs={{64,0},{128,64},{192,128},{65,1},{129,65},{193,129},{66,2},{130,66... | collective-permute-start | bytes 786440 | tf_op jit(solution)/shard_map/ppermute | solution.py:289
  397.6 24.2 %collective-permute-start.44 = (bf16[2,64,2048]{2,1,0:T(8,128)(2,1)}, bf16[2,64,2048]{2,1,0:T(8,128)(2,1)S(1)}, u32[]{:S(2)}, u32[]{:S(2)}) collective-permute-start(bf16[2,64,2048]{2,1,0:T(8,128)(2,1)} %get-tuple-element.674), channel_id=1, source_target_pairs={{0,1},{1,2},{2,3},{3,0},{4,5},{5,6},{6,7},{7,4},{8,9},{9,10},{10,1... | collective-permute-start | bytes 1572872 | tf_op jit(solution)/shard_map/ppermute | solution.py:284
  400.0 24.2 %collective-permute-start.45 = (bf16[2,64,2048]{2,1,0:T(8,128)(2,1)}, bf16[2,64,2048]{2,1,0:T(8,128)(2,1)S(1)}, u32[]{:S(2)}, u32[]{:S(2)}) collective-permute-start(bf16[2,64,2048]{2,1,0:T(8,128)(2,1)} %get-tuple-element.674), channel_id=1, source_target_pairs={{0,3},{1,0},{2,1},{3,2},{4,7},{5,4},{6,5},{7,6},{8,11},{9,8},{10,9... | collective-permute-start | bytes 1572872 | tf_op jit(solution)/shard_map/ppermute | solution.py:284
  414.1 32.3 %collective-permute-start.55 = (bf16[48,2048]{1,0:T(8,128)(2,1)}, bf16[48,2048]{1,0:T(8,128)(2,1)}, u32[]{:S(2)}, u32[]{:S(2)}) collective-permute-start(bf16[48,2048]{1,0:T(8,128)(2,1)} %get-tuple-element.725), channel_id=1, source_target_pairs={{0,1},{1,2},{2,3},{3,0},{4,5},{5,6},{6,7},{7,4},{8,9},{9,10},{10,1... | collective-permute-start | bytes 589832 | tf_op jit(solution)/shard_map/ppermute | solution.py:284
  421.8 24.7 %collective-permute-start.56 = (bf16[48,2048]{1,0:T(8,128)(2,1)}, bf16[48,2048]{1,0:T(8,128)(2,1)}, u32[]{:S(2)}, u32[]{:S(2)}) collective-permute-start(bf16[48,2048]{1,0:T(8,128)(2,1)} %get-tuple-element.726), channel_id=1, source_target_pairs={{0,3},{1,0},{2,1},{3,2},{4,7},{5,4},{6,5},{7,6},{8,11},{9,8},{10,9... | collective-permute-start | bytes 589832 | tf_op jit(solution)/shard_map/ppermute | solution.py:284
  (68 other events, 784.7 us)

commit v4 on v3

--- a/solution.py
+++ b/solution.py
@@ -34,7 +34,7 @@
     return values * scale_inv, scale_inv
 
 
-def start_layer(pos, pieces, layer, bank, wbuf, sems, by_rows):
+def start_chunks(pos, pieces, layer, parts, bank, wbuf, sems, by_rows):
     half = layer // 2
     count = len(pieces) // 2
 
@@ -42,7 +42,7 @@
         top, *by_x = refs
         nz, nx, cut, features = top.shape
         zs, size = nz // 2, features // CHUNKS
-        for part in range(CHUNKS):
+        for part in parts:
             slot = bank * CHUNKS + part
             cols = pl.ds(part * size, size)
             if by_rows:
@@ -72,61 +72,95 @@
     pltpu.make_async_copy(buf, buf, sem).wait()
 
 
+EARLY, LATE = range(CHUNKS // 2), range(CHUNKS // 2, CHUNKS)
+
+
 def forward_kernel(pos, x_ref, gain_ref, *refs):
-    count = len(refs) - 7
+    count = len(refs) - 12
     pieces = refs[:count]
-    xs_ref, ns_ref, slope_ref, scale_ref, out_ref, wbuf, sems = refs[count:]
+    xs_out, ns_out, slope_out, scale_out, out_ref, wbuf, sems = refs[count : count + 7]
+    saves = refs[count + 7 : count + 11]
+    save_sems = refs[count + 11]
+    xs_ref, ns_ref, slope_ref, scale_ref = saves
     layers = gain_ref.shape[0]
     nx, block, size = wbuf.shape[2:]
-    start_layer(pos, pieces, 0, 0, wbuf, sems, False)
+    start_chunks(pos, pieces, 0, EARLY, 0, wbuf, sems, False)
     out_ref[...] = x_ref[...]
+
+    def saved(layer, bank):
+        targets = (xs_out.at[layer], ns_out.at[:, layer], slope_out.at[layer], scale_out.at[layer])
+        return [
+            pltpu.make_async_copy(ref.at[bank], target, save_sems.at[bank, k])
+            for k, (ref, target) in enumerate(zip(saves, targets))
+        ]
 
     def layer_step(layer, carry):
         bank = lax.rem(layer, 2)
 
-        @pl.when(layer + 1 < layers)
+        @pl.when(layer >= 2)
         def _():
-            start_layer(pos, pieces, layer + 1, 1 - bank, wbuf, sems, False)
+            for copy in saved(layer - 2, bank):
+                copy.wait()
 
         residual = out_ref[...]
-        xs_ref[layer] = residual
+        xs_ref[bank] = residual
         unit, scale_inv = unit_of(residual)
-        scale_ref[layer] = jnp.broadcast_to(scale_inv, scale_ref.shape[1:])
+        scale_ref[bank] = jnp.broadcast_to(scale_inv, scale_ref.shape[1:])
         rounded = (unit * gain_ref[pl.ds(layer, 1), :]).astype(BF)
         for b in range(rounded.shape[1] // block):
-            ns_ref[b % nx, layer, :, b // nx * block : (b // nx + 1) * block] = rounded[:, b * block : (b + 1) * block]
+            ns_ref[bank, b % nx, :, b // nx * block : (b // nx + 1) * block] = rounded[:, b * block : (b + 1) * block]
         for part in range(CHUNKS):
             cols = slice(part * size, (part + 1) * size)
             slot = bank * CHUNKS + part
             wait_chunk(wbuf.at[slot], sems.at[slot])
+            if part == 0:
+                start_chunks(pos, pieces, layer, LATE, bank, wbuf, sems, False)
+            if part == CHUNKS // 2:
+
+                @pl.when(layer + 1 < layers)
+                def _():
+                    start_chunks(pos, pieces, layer + 1, EARLY, 1 - bank, wbuf, sems, False)
+
             pre_act = jnp.dot(rounded, wbuf[slot].reshape(-1, size), preferred_element_type=F32)
             value, slope = gelu_and_slope(pre_act)
-            slope_ref[layer, :, cols] = slope
+            slope_ref[bank, :, cols] = slope
             out_ref[:, cols] = (residual[:, cols].astype(F32) + value).astype(BF)
+        for copy in saved(layer, bank):
+            copy.start()
         return carry
 
     lax.fori_loop(0, layers, layer_step, 0)
-
-
-def backward_kernel(pos, grad_ref, gain_ref, xs_ref, slope_ref, scale_ref, *refs, first):
-    count = len(refs) - 6
+    for layer in (layers - 2, layers - 1):
+        for copy in saved(layer, layer % 2):
+            copy.wait()
+
+
+def backward_kernel(pos, grad_ref, gain_ref, xs_in, slope_in, scale_in, *refs, first):
+    count = len(refs) - 10
     pieces = refs[:count]
-    da_ref, gp_ref, out_ref, wbuf, dn_ref, sems = refs[count:]
+    da_ref, gp_ref, out_ref, wbuf, dn_ref, sems, xs_ref, slope_ref, scale_ref, load_sems = refs[count:]
     layers = xs_ref.shape[0]
     features = wbuf.shape[3]
     size = features // CHUNKS
-    start_layer(pos, pieces, first + layers - 1, 0, wbuf, sems, True)
+
+    def loads(local):
+        return [
+            pltpu.make_async_copy(source.at[first + local], ref.at[local], load_sems.at[k, local])
+            for k, (source, ref) in enumerate(((slope_in, slope_ref), (scale_in, scale_ref), (xs_in, xs_ref)))
+        ]
+
+    start_chunks(pos, pieces, first + layers - 1, EARLY, 0, wbuf, sems, True)
+    for local in range(layers - 1, -1, -1):
+        for copy in loads(local):
+            copy.start()
     out_ref[...] = grad_ref[...]
 
     def layer_step(step, carry):
         local = layers - 1 - step
         layer = first + local
         bank = lax.rem(step, 2)
-
-        @pl.when(step + 1 < layers)
-        def _():
-            start_layer(pos, pieces, layer - 1, 1 - bank, wbuf, sems, True)
-
+        for copy in loads(local):
+            copy.wait()
         grad_pre = (out_ref[...].astype(F32) * slope_ref[local]).astype(BF)
         da_ref[local] = grad_pre
         scale_inv = scale_ref[local][:, :1]
@@ -135,6 +169,14 @@
             cols = slice(part * size, (part + 1) * size)
             slot = bank * CHUNKS + part
             wait_chunk(wbuf.at[slot], sems.at[slot])
+            if part == 0:
+                start_chunks(pos, pieces, layer, LATE, bank, wbuf, sems, True)
+            if part == CHUNKS // 2:
+
+                @pl.when(step + 1 < layers)
+                def _():
+                    start_chunks(pos, pieces, layer - 1, EARLY, 1 - bank, wbuf, sems, True)
+
             grad_norm = lax.dot_general(
                 grad_pre, wbuf[slot].reshape(size, features), CONTRACT_LAST, preferred_element_type=F32
             )
@@ -203,7 +245,7 @@
     return pl.pallas_call(
         forward_kernel,
         in_specs=[SM, VM, VM] + [HB] * len(stores),
-        out_specs=[VM] * 5,
+        out_specs=[HB] * 4 + [VM],
         out_shape=[
             shape((layers, rows, features), BF),
             shape((nx, layers, rows, features // nx), BF),
@@ -214,6 +256,11 @@
         scratch_shapes=[
             pltpu.VMEM((SLOTS, nz // 2, blocks_x, rows_in, features // CHUNKS), BF),
             pltpu.SemaphoreType.DMA((SLOTS,)),
+            pltpu.VMEM((2, rows, features), BF),
+            pltpu.VMEM((2, nx, rows, features // nx), BF),
+            pltpu.VMEM((2, rows, features), F32),
+            pltpu.VMEM((2, rows, LANES), F32),
+            pltpu.SemaphoreType.DMA((2, 4)),
         ],
         name="forward_stage",
     )(core, x, gains, *stores)
@@ -224,13 +271,9 @@
     nz, blocks_x, _, _ = stores[0].shape
     rows_in = features // (nz // 2 * blocks_x)
 
-    def part_of(width):
-        return pl.BlockSpec((layers, rows, width), lambda i: (first // layers, 0, 0), memory_space=pltpu.VMEM)
-
     return pl.pallas_call(
         functools.partial(backward_kernel, first=first),
-        grid=(1,),
-        in_specs=[SM, VM, VM, part_of(features), part_of(features), part_of(LANES)] + [HB] * len(stores),
+        in_specs=[SM, VM, VM, HB, HB, HB] + [HB] * len(stores),
         out_specs=[VM] * 3,
         out_shape=[
             shape((layers, rows, features), BF),
@@ -241,6 +284,10 @@
             pltpu.VMEM((SLOTS, blocks_x, rows_in, features), BF),
             pltpu.VMEM((rows, features), F32),
             pltpu.SemaphoreType.DMA((SLOTS,)),
+            pltpu.VMEM((layers, rows, features), BF),
+            pltpu.VMEM((layers, rows, features), F32),
+            pltpu.VMEM((layers, rows, LANES), F32),
+            pltpu.SemaphoreType.DMA((3, layers)),
         ],
         name="backward_stage",
     )(core, grad, gains, xs, slopes, scales, *stores)
@@ -330,10 +377,10 @@
         column = lax.dynamic_update_slice(column, piece[None], ((iz - steps) % nz, 0, 0))
     line, column = lax.optimization_barrier((line, column))
     top = jnp.zeros((nz, nx, cut, features), BF)
-    spread, smalls = ring_spread(line, ("zh", "zl"), nz // 2, small(*small_inputs))
+    left, right = turn(column, "x", 1), turn(column, "x", -1)
+    spread, (left, right, smalls) = ring_spread(line, ("zh", "zl"), nz // 2, (left, right, small(*small_inputs)))
     for steps, piece in spread:
         top = lax.dynamic_update_slice(top, piece[None], ((iz - steps) % nz, 0, 0, 0))
-    left, right = turn(column, "x", 1), turn(column, "x", -1)
     far = jnp.concatenate([turn(left[: nz // 2], "x", 1), turn(right[nz // 2 :], "x", -1)])
     own = [top, column, left, right, far]
     return own + [turn(piece, "c", 1) for piece in own], smalls

time: 532 us -> 539 us (1.013)
  starting transfers between devices: 141 us -> 155 us
  waiting for transfers between devices: 263 us -> 253 us
    ppermute x69, waiting for transfers between devices: 152 us -> 140 us  [turn(): lax.ppermute(value, axis, [(i, (i + steps) % count) for i in range(count)])]
    ppermute x69, starting transfers between devices: 113 us -> 125 us  [turn(): lax.ppermute(value, axis, [(i, (i + steps) % count) for i in range(count)])]
  transfers between devices with their start and end apart: 75 -> 75, of which waited for: 33 -> 34; matrix products, arithmetic and copies ran while one was open for 11% -> 10% of each run, Pallas kernels for 1% -> 1%
where the time goes in v4:
time: 539 us; the launch traced here: 530 us
  waiting for transfers between devices  253 us (47%)
  starting transfers between devices  155 us (29%)
  local copies, waits for them, and re-layouts  51.6 us (10%)
  Pallas kernels  46.3 us (9%)
  other arithmetic  19.1 us (4%)
    ppermute x69, waiting for transfers between devices, turn(): lax.ppermute(value, axis, [(i, (i + steps) % count) for i in range(count)])  140 us
    ppermute x69, starting transfers between devices, turn(): lax.ppermute(value, axis, [(i, (i + steps) % count) for i in range(count)])  125 us
    ppermute x6, waiting for transfers between devices, shift(): lax.ppermute(value, axis, [(i, i + steps) for i in range(count) if 0 <= i...  113 us
    ppermute x6, starting transfers between devices, shift(): lax.ppermute(value, axis, [(i, i + steps) for i in range(count) if 0 <= i...  29.8 us
    pallas_call x2, Pallas kernels, backward_stage(): pl.pallas_call(functools.partial(backward_kernel, first=first), in_specs=...  21.4 us
    pallas_call x1, Pallas kernels, forward_stage(): pl.pallas_call(forward_kernel, in_specs=[SM, VM, VM] + [HB] * len(stores)...  15.7 us
  transfers between devices with their start and end apart: 75, of which 34 were waited for; matrix products, arithmetic and copies ran while one was open for 10% of the time, Pallas kernels for 1%

profile of v4, /device:TPU:6, one launch (start us, length us, event | category | flops | bytes accessed | tf_op | source)
XLA Modules:
  0.0 529.7 jit_solution(11455925248369559199)
XLA Ops:
  20.6 5.4 %collective-permute-done.19 = bf16[2,16,2048]{2,1,0:T(8,128)(2,1)S(1)} collective-permute-done((bf16[2,16,2048]{2,1,0:T(8,128)(2,1)S(1)}, bf16[2,16,2048]{2,1,0:T(8,128)(2,1)S(1)}, u32[]{:S(2)}, u32[]{:S(2)}) %collective-permute-start.19) | collective-permute-done | bytes 131104 | tf_op jit(solution)/shard_map/ppermute | solution.py:331
  47.9 8.2 %collective-permute-done.9 = bf16[80,2048]{1,0:T(8,128)(2,1)S(1)} collective-permute-done((bf16[80,2048]{1,0:T(8,128)(2,1)S(1)}, bf16[80,2048]{1,0:T(8,128)(2,1)S(1)}, u32[]{:S(2)}, u32[]{:S(2)}) %collective-permute-start.9) | collective-permute-done | bytes 327712 | tf_op jit(solution)/shard_map/ppermute | solution.py:331
  58.2 6.1 %collective-permute-done.10 = bf16[80,2048]{1,0:T(8,128)(2,1)S(1)} collective-permute-done((bf16[80,2048]{1,0:T(8,128)(2,1)S(1)}, bf16[80,2048]{1,0:T(8,128)(2,1)S(1)}, u32[]{:S(2)}, u32[]{:S(2)}) %collective-permute-start.10) | collective-permute-done | bytes 327712 | tf_op jit(solution)/shard_map/ppermute | solution.py:331
  71.9 11.0 %collective-permute-done.11 = bf16[4,48,2048]{2,1,0:T(8,128)(2,1)} collective-permute-done((bf16[4,48,2048]{2,1,0:T(8,128)(2,1)}, bf16[4,48,2048]{2,1,0:T(8,128)(2,1)}, u32[]{:S(2)}, u32[]{:S(2)}) %collective-permute-start.11) | collective-permute-done | bytes 786464 | tf_op jit(solution)/shard_map/ppermute | solution.py:331
  82.8 11.9 %collective-permute-start.12 = (bf16[4,48,2048]{2,1,0:T(8,128)(2,1)}, bf16[4,48,2048]{2,1,0:T(8,128)(2,1)S(1)}, u32[]{:S(2)}, u32[]{:S(2)}) collective-permute-start(bf16[4,48,2048]{2,1,0:T(8,128)(2,1)} %collective-permute-done.11), channel_id=1, source_target_pairs={{0,4},{4,8},{8,12},{12,32},{32,36},{36,40},{40,44},{44,0},{1,5},{5... | collective-permute-start | bytes 2359304 | tf_op jit(solution)/shard_map/ppermute | solution.py:331
  99.3 13.9 %collective-permute-start.24 = (bf16[4,48,2048]{2,1,0:T(8,128)(2,1)S(1)}, bf16[4,48,2048]{2,1,0:T(8,128)(2,1)S(1)}, u32[]{:S(2)}, u32[]{:S(2)}) collective-permute-start(bf16[4,48,2048]{2,1,0:T(8,128)(2,1)S(1)} %collective-permute-done.23), channel_id=1, source_target_pairs={{0,44},{4,0},{8,4},{12,8},{32,12},{36,32},{40,36},{44,40},{1,45},{... | collective-permute-start | bytes 2359304 | tf_op jit(solution)/shard_map/ppermute | solution.py:331
  113.2 7.4 %collective-permute-start.13 = (bf16[4,48,2048]{2,1,0:T(8,128)(2,1)S(1)}, bf16[4,48,2048]{2,1,0:T(8,128)(2,1)S(1)}, u32[]{:S(2)}, u32[]{:S(2)}) collective-permute-start(bf16[4,48,2048]{2,1,0:T(8,128)(2,1)S(1)} %collective-permute-done.12), channel_id=1, source_target_pairs={{0,4},{4,8},{8,12},{12,32},{32,36},{36,40},{40,44},{44,0},{1,5},{5... | collective-permute-start | bytes 2359304 | tf_op jit(solution)/shard_map/ppermute | solution.py:331
  128.3 5.5 %collective-permute-done.13 = bf16[4,48,2048]{2,1,0:T(8,128)(2,1)S(1)} collective-permute-done((bf16[4,48,2048]{2,1,0:T(8,128)(2,1)S(1)}, bf16[4,48,2048]{2,1,0:T(8,128)(2,1)S(1)}, u32[]{:S(2)}, u32[]{:S(2)}) %collective-permute-start.13) | collective-permute-done | bytes 786464 | tf_op jit(solution)/shard_map/ppermute | solution.py:331
  140.1 9.7 %collective-permute-done.22 = bf16[4,48,2048]{2,1,0:T(8,128)(2,1)S(1)} collective-permute-done((bf16[4,48,2048]{2,1,0:T(8,128)(2,1)S(1)}, bf16[4,48,2048]{2,1,0:T(8,128)(2,1)S(1)}, u32[]{:S(2)}, u32[]{:S(2)}) %collective-permute-start.22) | collective-permute-done | bytes 786464 | tf_op jit(solution)/shard_map/ppermute | solution.py:331
  159.1 10.2 %collective-permute-start.30 = (bf16[8,80,2048]{2,1,0:T(8,128)(2,1)}, bf16[8,80,2048]{2,1,0:T(8,128)(2,1)}, u32[]{:S(2)}, u32[]{:S(2)}) collective-permute-start(bf16[8,80,2048]{2,1,0:T(8,128)(2,1)} %collective-permute-done.14), channel_id=1, source_target_pairs={{0,16},{16,0},{1,17},{17,1},{2,18},{18,2},{3,19},{19,3},{4,20},{20... | collective-permute-start | bytes 7864328 | tf_op jit(solution)/shard_map/ppermute | solution.py:331
  169.3 17.1 %collective-permute-done.26 = bf16[4,80,2048]{2,1,0:T(8,128)(2,1)S(1)} collective-permute-done((bf16[4,80,2048]{2,1,0:T(8,128)(2,1)S(1)}, bf16[4,80,2048]{2,1,0:T(8,128)(2,1)S(1)}, u32[]{:S(2)}, u32[]{:S(2)}) %collective-permute-start.26) | collective-permute-done | bytes 1310752 | tf_op jit(solution)/shard_map/ppermute | solution.py:331
  197.3 15.7 %conditional.10 = ((bf16[4,64,2048]{2,1,0:T(8,128)(2,1)}, bf16[4,4,64,512]{3,2,1,0:T(8,128)(2,1)}, f32[4,64,2048]{2,1,0:T(8,128)}, f32[4,64,128]{2,1,0:T(8,128)S(1)}, bf16[64,2048]{1,0:T(8,128)(2,1)S(1)})) conditional(s32[]{:T(128)} %convert_element_type.204, bf16[64,2048]{1,0:T(8,128)(2,1)S(1)} %convolution_convert_fusion.2, (s32[2]{0:T(128)S(1)}, ...), branch_computations={%region_0.1_spmd, %region_1.2_spmd} | conditional | bytes 4849724 | solution.py:435
  197.3 15.7 %forward_stage.4 = (bf16[4,64,2048]{2,1,0:T(8,128)(2,1)}, bf16[4,4,64,512]{3,2,1,0:T(8,128)(2,1)}, f32[4,64,2048]{2,1,0:T(8,128)}, f32[4,64,128]{2,1,0:T(8,128)S(1)}, bf16[64,2048]{1,0:T(8,128)(2,1)S(1)}) custom-call(s32[2]{0:T(128)S(1)} %get-tuple-element.441.pos, bf16[64,2048]{1,0:T(8,128)(2,1)S(1)} %get-tuple-element.442.x_ref, ...), custom_call_target="tpu_custom_call" | custom-call | tf_op jit(solution)/shard_map/cond/branch_1_fun/forward_stage/pallas_call | solution.py:245
  214.4 5.9 %collective-permute-done.33 = bf16[64,2048]{1,0:T(8,128)(2,1)S(1)} collective-permute-done((bf16[64,2048]{1,0:T(8,128)(2,1)S(1)}, bf16[64,2048]{1,0:T(8,128)(2,1)S(1)}, u32[]{:S(2)}, u32[]{:S(2)}) %collective-permute-start.33) | collective-permute-done | bytes 262176 | tf_op jit(solution)/shard_map/ppermute | solution.py:336
  220.3 20.1 %collective-permute-start.34 = (bf16[64,2048]{1,0:T(8,128)(2,1)S(1)}, bf16[64,2048]{1,0:T(8,128)(2,1)S(1)}, u32[]{:S(2)}, u32[]{:S(2)}) collective-permute-start(bf16[64,2048]{1,0:T(8,128)(2,1)S(1)} %get-tuple-element.650), channel_id=1, source_target_pairs={{0,64},{64,128},{128,192},{1,65},{65,129},{129,193},{2,66},{66,130... | collective-permute-start | bytes 786440 | tf_op jit(solution)/shard_map/ppermute | solution.py:336
  261.0 24.0 %collective-permute-done.36 = bf16[64,2048]{1,0:T(8,128)(2,1)} collective-permute-done((bf16[64,2048]{1,0:T(8,128)(2,1)}, bf16[64,2048]{1,0:T(8,128)(2,1)}, u32[]{:S(2)}, u32[]{:S(2)}) %collective-permute-start.36) | collective-permute-done | bytes 262176 | tf_op jit(solution)/shard_map/ppermute | solution.py:336
  298.0 6.8 %collective-permute-done.41 = bf16[2,2,64,512]{3,2,1,0:T(8,128)(2,1)} collective-permute-done((bf16[2,2,64,512]{3,2,1,0:T(8,128)(2,1)}, bf16[2,2,64,512]{3,2,1,0:T(8,128)(2,1)}, u32[]{:S(2)}, u32[]{:S(2)}) %collective-permute-start.41) | collective-permute-done | bytes 262176 | tf_op jit(solution)/shard_map/ppermute | solution.py:331
  307.1 69.5 %collective-permute-done.38 = bf16[64,2048]{1,0:T(8,128)(2,1)S(1)} collective-permute-done((bf16[64,2048]{1,0:T(8,128)(2,1)}, bf16[64,2048]{1,0:T(8,128)(2,1)S(1)}, u32[]{:S(2)}, u32[]{:S(2)}) %collective-permute-start.38) | collective-permute-done | bytes 262176 | tf_op jit(solution)/shard_map/ppermute | solution.py:336
  376.6 12.5 %conditional.18 = (bf16[2,64,2048]{2,1,0:T(8,128)(2,1)}, bf16[64,2048]{1,0:T(8,128)(2,1)S(1)}, bf16[1,2,64,2048]{3,2,1,0:T(8,128)(2,1)S(1)}, f32[1,2,2048]{2,1,0:T(2,128)S(1)}) conditional(s32[]{:T(128)} %convert_element_type.204, (bf16[4,64,2048]{2,1,0:T(8,128)(2,1)S(1)}, f32[4,2048]{1,0:T(4,128)S(1)}, ...), branch_computations={%region_16.17_spmd, %region_17.18_spmd} | conditional | bytes 2129952 | solution.py:459
  377.3 10.7 %backward_stage.12 = (bf16[2,64,2048]{2,1,0:T(8,128)(2,1)}, f32[2,2048]{1,0:T(2,128)S(1)}, bf16[64,2048]{1,0:T(8,128)(2,1)S(1)}) custom-call(s32[2]{0:T(128)S(1)} %get-tuple-element.552.pos, bf16[64,2048]{1,0:T(8,128)(2,1)} %copy.148.grad_ref, f32[4,2048]{1,0:T(4,128)S(1)} %get-tuple-element.554.gain_ref, bf16[4,64,2048]{2,1,0:T(8,128)(2,1)} %get-tuple-element.555.xs_in, ...), custom_call_target="tpu_custom_call" | custom-call | tf_op jit(solution)/shard_map/cond/branch_1_fun/backward_stage/pallas_call | solution.py:274
  389.9 12.6 %conditional.19 = (bf16[2,64,2048]{2,1,0:T(8,128)(2,1)}, bf16[64,2048]{1,0:T(8,128)(2,1)S(1)}, bf16[1,2,64,2048]{3,2,1,0:T(8,128)(2,1)S(1)}, f32[1,2,2048]{2,1,0:T(2,128)S(1)}) conditional(s32[]{:T(128)} %convert_element_type.204, (bf16[4,64,2048]{2,1,0:T(8,128)(2,1)}, f32[4,2048]{1,0:T(4,128)S(1)}, bf16[64,2048]{1,0:T(8,128)(2,1)S(1)}) %tuple.140, ...), branch_computations={%region_18.19_spmd, %region_19.20_spmd} | conditional | bytes 2129952 | solution.py:459
  390.5 10.7 %backward_stage.13 = (bf16[2,64,2048]{2,1,0:T(8,128)(2,1)}, f32[2,2048]{1,0:T(2,128)S(1)}, bf16[64,2048]{1,0:T(8,128)(2,1)S(1)}) custom-call(s32[2]{0:T(128)S(1)} %get-tuple-element.574.pos, bf16[64,2048]{1,0:T(8,128)(2,1)} %copy.149.grad_ref, f32[4,2048]{1,0:T(4,128)S(1)} %get-tuple-element.576.gain_ref, bf16[4,64,2048]{2,1,0:T(8,128)(2,1)} %get-tuple-element.577.xs_in, ...), custom_call_target="tpu_custom_call" | custom-call | tf_op jit(solution)/shard_map/cond/branch_1_fun/backward_stage/pallas_call | solution.py:274
  407.8 10.1 %collective-permute-done.49 = bf16[2,64,2048]{2,1,0:T(8,128)(2,1)S(1)} collective-permute-done((bf16[2,64,2048]{2,1,0:T(8,128)(2,1)}, bf16[2,64,2048]{2,1,0:T(8,128)(2,1)S(1)}, u32[]{:S(2)}, u32[]{:S(2)}) %collective-permute-start.49) | collective-permute-done | bytes 524320 | tf_op jit(solution)/shard_map/ppermute | solution.py:331
  439.1 9.2 %collective-permute-done.46 = bf16[1,64,2048]{2,1,0:T(8,128)(2,1)S(1)} collective-permute-done((bf16[1,64,2048]{2,1,0:T(8,128)(2,1)S(1)}, bf16[1,64,2048]{2,1,0:T(8,128)(2,1)S(1)}, u32[]{:S(2)}, u32[]{:S(2)}) %collective-permute-start.46) | collective-permute-done | bytes 262176 | tf_op jit(solution)/shard_map/ppermute | solution.py:331
  (297 shorter events, 240.8 us)
Async XLA Ops:
  2.6 33.1 %collective-permute-start.4 = (bf16[80,2048]{1,0:T(8,128)(2,1)}, bf16[80,2048]{1,0:T(8,128)(2,1)}, u32[]{:S(2)}, u32[]{:S(2)}) collective-permute-start(bf16[80,2048]{1,0:T(8,128)(2,1)} %get-tuple-element.725), channel_id=1, source_target_pairs={{0,4},{4,8},{8,12},{12,32},{32,36},{36,40},{40,44},{44,0},{1,5},{5... | collective-permute-start | bytes 983048 | tf_op jit(solution)/shard_map/ppermute | solution.py:331
  4.5 31.2 %collective-permute-start.7 = (bf16[80,2048]{1,0:T(8,128)(2,1)}, bf16[80,2048]{1,0:T(8,128)(2,1)}, u32[]{:S(2)}, u32[]{:S(2)}) collective-permute-start(bf16[80,2048]{1,0:T(8,128)(2,1)} %get-tuple-element.725), channel_id=1, source_target_pairs={{0,44},{4,0},{8,4},{12,8},{32,12},{36,32},{40,36},{44,40},{1,45},{... | collective-permute-start | bytes 983048 | tf_op jit(solution)/shard_map/ppermute | solution.py:331
  26.0 38.4 %collective-permute-start.17 = (f32[2,2048]{1,0:T(2,128)S(1)}, f32[2,2048]{1,0:T(2,128)S(1)}, u32[]{:S(2)}, u32[]{:S(2)}) collective-permute-start(f32[2,2048]{1,0:T(2,128)S(1)} %maximum_select_fusion.2), channel_id=1, source_target_pairs={{0,32},{32,0},{1,33},{33,1},{2,34},{34,2},{3,35},{35,3},{4,36},{36... | collective-permute-start | bytes 49160 | tf_op jit(solution)/shard_map/ppermute | solution.py:331
  39.9 26.7 %collective-permute-start.20 = (bf16[4,16,2048]{2,1,0:T(8,128)(2,1)}, bf16[4,16,2048]{2,1,0:T(8,128)(2,1)S(1)}, u32[]{:S(2)}, u32[]{:S(2)}) collective-permute-start(bf16[4,16,2048]{2,1,0:T(8,128)(2,1)} %pad_maximum_fusion.8), channel_id=1, source_target_pairs={{0,4},{4,8},{8,12},{12,0},{1,5},{5,9},{9,13},{13,1},{2,6},{6,10},{... | collective-permute-start | bytes 786440 | tf_op jit(solution)/shard_map/ppermute | solution.py:331
  64.5 69.3 %collective-permute-start.14 = (bf16[8,80,2048]{2,1,0:T(8,128)(2,1)S(1)}, bf16[8,80,2048]{2,1,0:T(8,128)(2,1)}, u32[]{:S(2)}, u32[]{:S(2)}) collective-permute-start(bf16[8,80,2048]{2,1,0:T(8,128)(2,1)S(1)} %bitcast_dynamic-update-slice_fusion.8), channel_id=1, source_target_pairs={{0,1},{1,2},{2,3},{3,0},{4,5},{5,6},{6,7},{7,4},{8,9},{9,10},{10,1... | collective-permute-start | bytes 7864328 | tf_op jit(solution)/shard_map/ppermute | solution.py:331
  66.2 67.6 %collective-permute-start.15 = (bf16[8,80,2048]{2,1,0:T(8,128)(2,1)S(1)}, bf16[8,80,2048]{2,1,0:T(8,128)(2,1)}, u32[]{:S(2)}, u32[]{:S(2)}) collective-permute-start(bf16[8,80,2048]{2,1,0:T(8,128)(2,1)S(1)} %bitcast_dynamic-update-slice_fusion.8), channel_id=1, source_target_pairs={{0,3},{1,0},{2,1},{3,2},{4,7},{5,4},{6,5},{7,6},{8,11},{9,8},{10,9... | collective-permute-start | bytes 7864328 | tf_op jit(solution)/shard_map/ppermute | solution.py:331
  66.7 28.8 %collective-permute-start.21 = (bf16[8,16,2048]{2,1,0:T(8,128)(2,1)S(1)}, bf16[8,16,2048]{2,1,0:T(8,128)(2,1)S(1)}, u32[]{:S(2)}, u32[]{:S(2)}) collective-permute-start(bf16[8,16,2048]{2,1,0:T(8,128)(2,1)S(1)} %pad_maximum_fusion.2), channel_id=1, source_target_pairs={{0,8},{4,12},{8,0},{12,4},{1,9},{5,13},{9,1},{13,5},{2,10},{6,14},... | collective-permute-start | bytes 1572872 | tf_op jit(solution)/shard_map/ppermute | solution.py:331
  69.7 29.7 %collective-permute-start.23 = (bf16[4,48,2048]{2,1,0:T(8,128)(2,1)}, bf16[4,48,2048]{2,1,0:T(8,128)(2,1)S(1)}, u32[]{:S(2)}, u32[]{:S(2)}) collective-permute-start(bf16[4,48,2048]{2,1,0:T(8,128)(2,1)} %fusion.25), channel_id=1, source_target_pairs={{0,44},{4,0},{8,4},{12,8},{32,12},{36,32},{40,36},{44,40},{1,45},{... | collective-permute-start | bytes 2359304 | tf_op jit(solution)/shard_map/ppermute | solution.py:331
  82.8 30.4 %collective-permute-start.12 = (bf16[4,48,2048]{2,1,0:T(8,128)(2,1)}, bf16[4,48,2048]{2,1,0:T(8,128)(2,1)S(1)}, u32[]{:S(2)}, u32[]{:S(2)}) collective-permute-start(bf16[4,48,2048]{2,1,0:T(8,128)(2,1)} %collective-permute-done.11), channel_id=1, source_target_pairs={{0,4},{4,8},{8,12},{12,32},{32,36},{36,40},{40,44},{44,0},{1,5},{5... | collective-permute-start | bytes 2359304 | tf_op jit(solution)/shard_map/ppermute | solution.py:331
  99.3 29.0 %collective-permute-start.24 = (bf16[4,48,2048]{2,1,0:T(8,128)(2,1)S(1)}, bf16[4,48,2048]{2,1,0:T(8,128)(2,1)S(1)}, u32[]{:S(2)}, u32[]{:S(2)}) collective-permute-start(bf16[4,48,2048]{2,1,0:T(8,128)(2,1)S(1)} %collective-permute-done.23), channel_id=1, source_target_pairs={{0,44},{4,0},{8,4},{12,8},{32,12},{36,32},{40,36},{44,40},{1,45},{... | collective-permute-start | bytes 2359304 | tf_op jit(solution)/shard_map/ppermute | solution.py:331
  128.3 24.3 %collective-permute-start.25 = (bf16[4,48,2048]{2,1,0:T(8,128)(2,1)S(1)}, bf16[4,48,2048]{2,1,0:T(8,128)(2,1)S(1)}, u32[]{:S(2)}, u32[]{:S(2)}) collective-permute-start(bf16[4,48,2048]{2,1,0:T(8,128)(2,1)S(1)} %collective-permute-done.24), channel_id=1, source_target_pairs={{0,44},{4,0},{8,4},{12,8},{32,12},{36,32},{40,36},{44,40},{1,45},{... | collective-permute-start | bytes 2359304 | tf_op jit(solution)/shard_map/ppermute | solution.py:331
  153.7 43.7 %collective-permute-start.28 = (bf16[8,4,48,2048]{3,2,1,0:T(8,128)(2,1)}, bf16[8,4,48,2048]{3,2,1,0:T(8,128)(2,1)}, u32[]{:S(2)}, u32[]{:S(2)}) collective-permute-start(bf16[8,4,48,2048]{3,2,1,0:T(8,128)(2,1)} %bitcast_dynamic-update-slice_fusion), channel_id=1, source_target_pairs={{0,16},{16,0},{1,17},{17,1},{2,18},{18,2},{3,19},{19,3},{4,20},{20... | collective-permute-start | bytes 18874376 | tf_op jit(solution)/shard_map/ppermute | solution.py:331
  155.1 31.3 %collective-permute-start.26 = (bf16[4,80,2048]{2,1,0:T(8,128)(2,1)S(1)}, bf16[4,80,2048]{2,1,0:T(8,128)(2,1)S(1)}, u32[]{:S(2)}, u32[]{:S(2)}) collective-permute-start(bf16[4,80,2048]{2,1,0:T(8,128)(2,1)S(1)} %slice.114), channel_id=1, source_target_pairs={{0,1},{1,2},{2,3},{3,0},{4,5},{5,6},{6,7},{7,4},{8,9},{9,10},{10,1... | collective-permute-start | bytes 3932168 | tf_op jit(solution)/shard_map/ppermute | solution.py:331
  158.6 32.2 %collective-permute-start.27 = (bf16[4,80,2048]{2,1,0:T(8,128)(2,1)S(1)}, bf16[4,80,2048]{2,1,0:T(8,128)(2,1)S(1)}, u32[]{:S(2)}, u32[]{:S(2)}) collective-permute-start(bf16[4,80,2048]{2,1,0:T(8,128)(2,1)S(1)} %slice.115), channel_id=1, source_target_pairs={{0,3},{1,0},{2,1},{3,2},{4,7},{5,4},{6,5},{7,6},{8,11},{9,8},{10,9... | collective-permute-start | bytes 3932168 | tf_op jit(solution)/shard_map/ppermute | solution.py:331
  158.8 33.4 %collective-permute-start.29 = (bf16[8,80,2048]{2,1,0:T(8,128)(2,1)S(1)}, bf16[8,80,2048]{2,1,0:T(8,128)(2,1)}, u32[]{:S(2)}, u32[]{:S(2)}) collective-permute-start(bf16[8,80,2048]{2,1,0:T(8,128)(2,1)S(1)} %bitcast_dynamic-update-slice_fusion.8), channel_id=1, source_target_pairs={{0,16},{16,0},{1,17},{17,1},{2,18},{18,2},{3,19},{19,3},{4,20},{20... | collective-permute-start | bytes 7864328 | tf_op jit(solution)/shard_map/ppermute | solution.py:331
  159.1 33.1 %collective-permute-start.30 = (bf16[8,80,2048]{2,1,0:T(8,128)(2,1)}, bf16[8,80,2048]{2,1,0:T(8,128)(2,1)}, u32[]{:S(2)}, u32[]{:S(2)}) collective-permute-start(bf16[8,80,2048]{2,1,0:T(8,128)(2,1)} %collective-permute-done.14), channel_id=1, source_target_pairs={{0,16},{16,0},{1,17},{17,1},{2,18},{18,2},{3,19},{19,3},{4,20},{20... | collective-permute-start | bytes 7864328 | tf_op jit(solution)/shard_map/ppermute | solution.py:331
  220.3 25.1 %collective-permute-start.34 = (bf16[64,2048]{1,0:T(8,128)(2,1)S(1)}, bf16[64,2048]{1,0:T(8,128)(2,1)S(1)}, u32[]{:S(2)}, u32[]{:S(2)}) collective-permute-start(bf16[64,2048]{1,0:T(8,128)(2,1)S(1)} %get-tuple-element.650), channel_id=1, source_target_pairs={{0,64},{64,128},{128,192},{1,65},{65,129},{129,193},{2,66},{66,130... | collective-permute-start | bytes 786440 | tf_op jit(solution)/shard_map/ppermute | solution.py:336
  259.7 26.6 %collective-permute-start.39 = (bf16[4,2,64,512]{3,2,1,0:T(8,128)(2,1)}, bf16[4,2,64,512]{3,2,1,0:T(8,128)(2,1)}, u32[]{:S(2)}, u32[]{:S(2)}) collective-permute-start(bf16[4,2,64,512]{3,2,1,0:T(8,128)(2,1)} %get-tuple-element.719), channel_id=1, source_target_pairs={{0,16},{16,0},{1,17},{17,1},{2,18},{18,2},{3,19},{19,3},{4,20},{20... | collective-permute-start | bytes 1572872 | tf_op jit(solution)/shard_map/ppermute | solution.py:331
  259.7 25.3 %collective-permute-start.36 = (bf16[64,2048]{1,0:T(8,128)(2,1)}, bf16[64,2048]{1,0:T(8,128)(2,1)}, u32[]{:S(2)}, u32[]{:S(2)}) collective-permute-start(bf16[64,2048]{1,0:T(8,128)(2,1)} %get-tuple-element.665), channel_id=1, source_target_pairs={{64,0},{128,64},{192,128},{65,1},{129,65},{193,129},{66,2},{130,66... | collective-permute-start | bytes 786440 | tf_op jit(solution)/shard_map/ppermute | solution.py:336
  296.2 80.5 %collective-permute-start.38 = (bf16[64,2048]{1,0:T(8,128)(2,1)}, bf16[64,2048]{1,0:T(8,128)(2,1)S(1)}, u32[]{:S(2)}, u32[]{:S(2)}) collective-permute-start(bf16[64,2048]{1,0:T(8,128)(2,1)} %get-tuple-element.669), channel_id=1, source_target_pairs={{64,0},{128,64},{192,128},{65,1},{129,65},{193,129},{66,2},{130,66... | collective-permute-start | bytes 786440 | tf_op jit(solution)/shard_map/ppermute | solution.py:336
  404.9 24.2 %collective-permute-start.44 = (bf16[2,64,2048]{2,1,0:T(8,128)(2,1)}, bf16[2,64,2048]{2,1,0:T(8,128)(2,1)S(1)}, u32[]{:S(2)}, u32[]{:S(2)}) collective-permute-start(bf16[2,64,2048]{2,1,0:T(8,128)(2,1)} %get-tuple-element.678), channel_id=1, source_target_pairs={{0,1},{1,2},{2,3},{3,0},{4,5},{5,6},{6,7},{7,4},{8,9},{9,10},{10,1... | collective-permute-start | bytes 1572872 | tf_op jit(solution)/shard_map/ppermute | solution.py:331
  407.4 24.2 %collective-permute-start.45 = (bf16[2,64,2048]{2,1,0:T(8,128)(2,1)}, bf16[2,64,2048]{2,1,0:T(8,128)(2,1)S(1)}, u32[]{:S(2)}, u32[]{:S(2)}) collective-permute-start(bf16[2,64,2048]{2,1,0:T(8,128)(2,1)} %get-tuple-element.678), channel_id=1, source_target_pairs={{0,3},{1,0},{2,1},{3,2},{4,7},{5,4},{6,5},{7,6},{8,11},{9,8},{10,9... | collective-permute-start | bytes 1572872 | tf_op jit(solution)/shard_map/ppermute | solution.py:331
  421.5 32.6 %collective-permute-start.55 = (bf16[48,2048]{1,0:T(8,128)(2,1)}, bf16[48,2048]{1,0:T(8,128)(2,1)}, u32[]{:S(2)}, u32[]{:S(2)}) collective-permute-start(bf16[48,2048]{1,0:T(8,128)(2,1)} %get-tuple-element.729), channel_id=1, source_target_pairs={{0,1},{1,2},{2,3},{3,0},{4,5},{5,6},{6,7},{7,4},{8,9},{9,10},{10,1... | collective-permute-start | bytes 589832 | tf_op jit(solution)/shard_map/ppermute | solution.py:331
  429.1 24.9 %collective-permute-start.56 = (bf16[48,2048]{1,0:T(8,128)(2,1)}, bf16[48,2048]{1,0:T(8,128)(2,1)}, u32[]{:S(2)}, u32[]{:S(2)}) collective-permute-start(bf16[48,2048]{1,0:T(8,128)(2,1)} %get-tuple-element.730), channel_id=1, source_target_pairs={{0,3},{1,0},{2,1},{3,2},{4,7},{5,4},{6,5},{7,6},{8,11},{9,8},{10,9... | collective-permute-start | bytes 589832 | tf_op jit(solution)/shard_map/ppermute | solution.py:331
  (68 other events, 787.6 us)
